TPU v7x, 128 devices: a whole 4x4x4 slice. The times are simulated.
128 devices in a mesh: dp: 16 (over z, y), fsdp: 8 (over x, core).
Axes of the slice: x: 4, y: 4, z: 4, core: 2. Of those that a mesh axis runs over, the one named last changes fastest.
Arguments:
- x_in: bfloat16 [128, 256, 768], P(('dp', 'fsdp'))
- grad_y: bfloat16 [128, 256, 768], P(('dp', 'fsdp'))
- norm_scale: bfloat16 [2, 768], P(None, 'fsdp')
- w_in: bfloat16 [2, 768, 7040], P(None, 'fsdp')
- w_out: bfloat16 [2, 3840, 768], P(None, 'fsdp')
Outputs:
- output 1: bfloat16 [128, 256, 768], P(('dp', 'fsdp'))
- output 2: bfloat16 [128, 256, 768], P(('dp', 'fsdp'))
- output 3: float32 [2, 768], P(None, 'fsdp')
- output 4: float32 [2, 768, 7040], P(None, 'fsdp')
- output 5: float32 [2, 3840, 768], P(None, 'fsdp')
All inputs are finite; a program needn't handle non-finite values.
Results may differ from a plain program's by a relative error of at most 0.0145081.
Values are sent between devices in bfloat16 or wider.
A program may use at most 1 GiB of HBM per device.

v0:
```python
import functools
import jax
import jax.numpy as jnp
from jax import lax
from jax.experimental import pallas as pl
from jax.experimental.pallas import tpu as pltpu
from jax.sharding import PartitionSpec as P

MESH_ID = pl.DeviceIdType.MESH
BOTH = (1, -1)
AROUND = (1, -1, 2)
PARTS = (True, False)
ALL, ZERO = ..., 0.0
LANE, WIDE, STRIP, HEAD = 128, 256, 512, 64
ROW, BAND, SIDE, PAIR = 8, 32, 4, 2


class Links:
    def __init__(self, send_sems, recv_sems):
        self.send_sems, self.recv_sems = send_sems, recv_sems
        self.slots, self.batches, self.sent = {}, {}, {}

    def send(self, key, src, dst, device, landing=None, whole=None, batch=None, lane=None):
        slot = self.slots.setdefault(landing or key, len(self.slots))
        leaving = self.batches.setdefault(batch or key, len(self.batches))
        copy = pltpu.make_async_remote_copy(
            src_ref=src, dst_ref=dst, send_sem=self.send_sems.at[leaving], recv_sem=self._landing(slot, lane),
            device_id=device, device_id_type=MESH_ID)
        copy.start()
        self.sent[batch or key] = (whole or src, leaving)

    def _landing(self, slot, lane):
        return self.recv_sems.at[slot] if lane is None else self.recv_sems.at[slot, lane]

    def arrive(self, key, landed, lane=None):
        slot = self.slots.setdefault(key, len(self.slots))
        pltpu.make_async_copy(landed, landed, self._landing(slot, lane)).wait()

    def drain(self):
        for left, leaving in self.sent.values():
            pltpu.make_async_copy(left, left, self.send_sems.at[leaving]).wait()
        self.sent.clear()


def rem(a, n):
    return a % n if isinstance(a, int) else lax.rem(a, n)


def chip_position():
    f, d = lax.axis_index("fsdp"), lax.axis_index("dp")
    return f // PAIR, rem(d, SIDE), d // SIDE, rem(f, PAIR)


def device_at(x, y, z, core):
    return (z * SIDE + y, x * PAIR + core)


def step(coord, by):
    return rem(coord + SIDE + by, SIDE)


def announce(devices):
    barrier = pltpu.get_barrier_semaphore()
    for device in devices:
        pl.semaphore_signal(barrier, inc=1, device_id=device, device_id_type=MESH_ID)
    pl.semaphore_wait(barrier, len(devices))


def plan(tasks, latency=2.5):
    free, landed, order, now = {}, {}, [], ZERO
    left = list(tasks)
    while left:
        best = None
        for place, (name, rank, start, needs, after, _, _) in enumerate(left):
            if all(n[0] in landed for n in needs) and all(n in landed for n in after):
                ready = max([start, now] + [landed[task][i] for task, i in needs])
                best = min(best or (ready, rank, place), (ready, rank, place))
        now, _, place = best
        name, _, _, _, _, sends, cost = left.pop(place)
        order.append(name)
        now += cost
        landed[name] = []
        for link, time in sends:
            free[link] = max(now, free.get(link, ZERO)) + time
            landed[name].append(free[link] + latency)
    return order


def layers_order(rows_i, cols_i, rows_o, cols_o, seq, starts):
    rate = 23300.0
    tasks = []
    for m in range(SIDE):
        is_in = m % PAIR == 0
        edge = cols_i // LANE * SIDE // 9 // PAIR * WIDE
        size = {"y": rows_i // SIDE * edge, "x": rows_i * (cols_i - PAIR * edge)} if is_in else {"y": rows_o // SIDE * cols_o // PAIR}
        size["z"] = size["y"]
        for color in "yzx" if is_in else "yz":
            cost = size[color] / rate
            both = [(("x", by), cost) for by in BOTH]
            spread = [((color, by), cost) for by in BOTH] if color != "x" else []
            tasks.append((("reach", m, color), m, starts[m], [], [], both, 0.2))
            for i, by in enumerate(BOTH):
                tasks.append((("relay", m, color, by), m, ZERO, [(("reach", m, color), i)], [], [(("x", by), cost / PAIR)] + spread, 0.2))
            halves = [(("relay", m, color, by), 0) for by in BOTH]
            tasks.append((("far", m, color), m, ZERO, halves, [], spread, 0.2))
            if color == "x":
                continue
            for off, source, first in ((-1, ("relay", m, color, 1), 1), (1, ("relay", m, color, -1), 1), (PAIR, ("far", m, color), 0)):
                for i, by in enumerate(BOTH):
                    tasks.append((("pass", m, color, off, by), m, ZERO, [(source, first + i)], [], [((color, by), cost / PAIR)], 0.2))
                halves = [(("pass", m, color, off, by), 0) for by in BOTH]
                tasks.append((("close", m, color, off), m, ZERO, halves, [], [], 0.2))
        for off in (-1, 1, PAIR):
            last = [("close", m, color, off) for color in "yz"]
            if is_in:
                last.append(("far", m, "x") if off == PAIR else ("relay", m, "x", -off))
            tasks.append((("hand", m, off), m, ZERO, [], last, [("chip", (rows_i * cols_i if is_in else rows_o * cols_o) / 150000.0)], 0.2))
    before = []

    def work(name, cost, mats=()):
        needs = [(("hand", m, off), 0) for m in mats for off in (-1, 1, PAIR)]
        tasks.append((name, 99, ZERO, needs, list(before), [], cost))
        before[:] = [name]

    for l in range(PAIR):
        work(("norm", l), 0.8)
        work(("project", l), 4.0, [PAIR * l])
        work(("attend", l), 3.0)
        work(("mlp", l), 2.4)
        work(("put", l), 1.6, [PAIR * l + 1])
    for l in (1, 0):
        work(("back_out", l), 2.9)
        work(("back_mlp", l), 2.0)
        work(("back_heads", l), 1.0)
        work(("back_quad", l), 4.8)
        work(("back_keys", l), 0.2)
        for i in range(PAIR):
            work(("back_in", l, i), 1.3 + 0.7 * i)
        work(("back_norm", l), 1.0)
    def send(name, rank, start, after, sends):
        tasks.append((name, rank, start, [], [after] if after else [], sends, 0.4))

    def follow(name, rank, needs, sends):
        tasks.append((name, rank, ZERO, needs, [], sends, 0.2))

    def both(axis, size):
        return [((axis, by), size / rate) for by in BOTH]

    model = rows_i * ROW
    for l in (1, 0):
        for axis in "yz":
            name = ("send_h", l, axis)
            send(name, 20 - l, 58.0, ("norm", l), both(axis, seq * model))
            for i, by in enumerate(BOTH):
                for index in range(PAIR):
                    follow(("pass_h", l, axis, by, index), 10, [(name, i)], [((axis, by), seq * model / SIDE / rate)])
        name = ("send_m", l)
        send(name, 22 - l, ZERO, ("mlp", l), both("x", seq * rows_o) + both("x", PAIR * seq * rows_o))
        for i, by in enumerate(BOTH):
            for index in range(PAIR):
                follow(("pass_m", l, by, index), 11, [(name, i)], [(("x", by), seq * rows_o / PAIR / rate)])
        if l == 0:
            send(("own_y",), 15, ZERO, ("back_norm", 1), [])
            send(("send_scale", l), 15, ZERO, ("back_norm", l), [])
            continue
        name = ("send_y", l)
        send(name, 12, 42.0, None, both("x", seq * model))
        for i, by in enumerate(BOTH):
            follow(("pass_y", l, by), 12, [(name, i)], [(("x", by), seq * model / PAIR / rate)])
        follow(("far_y", l), 12, [(("pass_y", l, by), 0) for by in BOTH], [])
        for axis in "zy":
            name = ("send_z", l, axis)
            share = seq * (cols_i + LANE) / ROW
            send(name, 13, ZERO, ("back_mlp", l) if axis == "z" else ("back_keys", l), both(axis, share / PAIR) + both(axis, share))
            for i, by in enumerate(BOTH):
                follow(("pass_z", l, axis, by), 13, [(name, i)], [((axis, by), share / PAIR / rate)])
                follow(("twin_z", l, axis, by), 14, [(name, PAIR + i)], [])
            follow(("far_z", l, axis), 14, [(("pass_z", l, axis, by), 0) for by in BOTH], [])
        send(("send_scale", l), 15, ZERO, ("back_norm", l), [])
    send(("own_z",), 15, ZERO, ("back_keys", 0), [])
    return plan(tasks)


def gather_stages(links, position, shard_i, shard_o, wi, wo, lsem):
    x, y, z, core = position
    twin = device_at(x, y, z, 1 - core)
    rows_i, cols_i = shard_i.shape[1:]
    rows_o, cols_o = shard_o.shape[1:]
    quarter_i, quarter_o = rows_i // SIDE, rows_o // SIDE
    third_i = cols_i // LANE * SIDE // 9 // PAIR * WIDE
    half_o = cols_o // PAIR
    cut_o = quarter_o // 16 * ROW + ROW if quarter_o % 16 else quarter_o // PAIR
    place = {"x": x, "y": y, "z": z}

    spots = {(axis, o): step(place[axis], o) for axis in "xyz" for o in range(SIDE)}

    def spot(axis, o):
        return spots[axis, o % SIDE]

    table = {}
    for axis in "xyz":
        for o in range(1, SIDE):
            moved = {**place, axis: spot(axis, o)}
            table[axis, o] = device_at(moved["x"], moved["y"], moved["z"], core)

    def peer(axis, o):
        return table[axis, o % SIDE]

    mats = []
    for l in range(PAIR):
        mats.append((shard_i.at[l], wi.at[l], rows_i, True))
        mats.append((shard_o.at[l], wo.at[l], rows_o, False))

    def region(is_in, color, q):
        if is_in:
            if color == "x":
                lo, hi = PAIR * third_i, cols_i
                rows = (0, rows_i)
            else:
                lo, hi = (0, third_i) if color == "y" else (third_i, PAIR * third_i)
                rows = (q * quarter_i, quarter_i)
            mid = lo + ((hi - lo) // LANE + 1) // PAIR * LANE
            return (rows, (lo, hi - lo)), (rows, (lo, mid - lo)), (rows, (mid, hi - mid))
        cols = (0, half_o) if color == "y" else (half_o, half_o)
        start = q * quarter_o
        return ((start, quarter_o), cols), ((start, cut_o), cols), ((start + cut_o, quarter_o - cut_o), cols)

    def at(m, xb, area):
        (r, nr), (c, nc) = area
        _, out, size, _ = mats[m]
        return out.at[pl.ds(pl.multiple_of((PAIR * xb + core) * size + r, ROW), nr), pl.ds(c, nc)]

    def block(m, xb, index):
        _, out, size, _ = mats[m]
        return out.at[pl.ds(pl.multiple_of((PAIR * xb + index) * size, BAND), size)]

    def colors(m):
        return "yzx" if mats[m][3] else "yz"

    def reach(m, color):
        src, _, _, is_in = mats[m]
        area = region(is_in, color, place[color])[0]
        for by in BOTH:
            links.send((m, "x1", color, by), src.at[pl.ds(pl.multiple_of(area[0][0], ROW), area[0][1]), pl.ds(*area[1])], at(m, x, area), peer("x", by))

    def launch(m, color, off):
        is_in = mats[m][3]
        moved = at(m, spot("x", off), region(is_in, color, place[color])[0])
        for by in BOTH:
            links.send((m, "p1", color, off, by), moved, moved, peer(color, by))

    def relay(m, color, by):
        is_in = mats[m][3]
        xb = spot("x", -by)
        areas = region(is_in, color, place[color])
        links.arrive((m, "x1", color, by), at(m, xb, areas[0]))
        part = at(m, xb, areas[1] if by == 1 else areas[PAIR])
        links.send((m, "x2", color, by), part, part, peer("x", by))
        if color != "x":
            launch(m, color, -by)

    def far(m, color):
        is_in = mats[m][3]
        areas = region(is_in, color, place[color])
        for by in BOTH:
            links.arrive((m, "x2", color, by), at(m, spot("x", PAIR), areas[1] if by == 1 else areas[PAIR]))
        if color != "x":
            launch(m, color, PAIR)

    def pass_on(m, color, off, by):
        is_in = mats[m][3]
        xb = spot("x", off)
        areas = region(is_in, color, spot(color, -by))
        links.arrive((m, "p1", color, off, by), at(m, xb, areas[0]))
        part = at(m, xb, areas[1] if by == 1 else areas[PAIR])
        links.send((m, "p2", color, off, by), part, part, peer(color, by))

    def close(m, color, off):
        is_in = mats[m][3]
        areas = region(is_in, color, spot(color, PAIR))
        for by in BOTH:
            links.arrive((m, "p2", color, off, by), at(m, spot("x", off), areas[1] if by == 1 else areas[PAIR]))

    def hand(m, off):
        whole = block(m, spot("x", off), core)
        links.send((m, "d2d", off), whole, whole, twin)

    owns = []

    def begin():
        for m, (src, _, _, _) in enumerate(mats):
            copy = pltpu.make_async_copy(src, block(m, x, core), lsem.at[m])
            copy.start()
            owns.append(copy)
            links.send((m, "d2d", 0), src, block(m, x, core), twin)

    def ready(m):
        owns[m].wait()
        for off in (0, -1, 1, PAIR):
            links.arrive((m, "d2d", off), block(m, spot("x", off), 1 - core))

    return begin, ready, peer, {"reach": reach, "relay": relay, "far": far, "pass": pass_on, "close": close, "hand": hand}


BF, F32 = jnp.bfloat16, jnp.float32


def product(a, b, contract=((1,), (0,))):
    return lax.dot_general(a, b, (contract, ((), ())), preferred_element_type=F32)


def lanes(start, size):
    return pl.ds(start if isinstance(start, int) else pl.multiple_of(start, LANE), size)


def layers_kernel(order, sc_ref, wi_ref, wo_ref, x_ref, dy_ref, freq_ref,
                  y_ref, gx_ref, hy_a, hy_b, hz_a, hz_b, mx_a, mx_b, yx_b, zy_b, zz_b, z_a, dy_a, sc_out, relay_m, relay_z,
                  wi, wo, z, om, h, hid, qr, kts, vsl, ksl, turned_q, turned_o, scores, dscores, pcat, dscat, cos_ref, sin_ref, turn_ref,
                  dot_heads, qt, dht, dkv, omt, ht, dyt, sc, gains, gain_ref, load_sems, own_sems, send_sems, recv_sems,
                  share_send_sems, share_recv_sems):
    seq, dim = x_ref.shape
    ff = (wi.shape[PAIR] - dim - LANE) // PAIR
    position = chip_position()
    x, y, zc, core = position
    twin = device_at(x, y, zc, 1 - core)
    me = PAIR * x + core
    links, shared = Links(send_sems, recv_sems), Links(share_send_sems, share_recv_sems)
    stored = []
    spots, _ = around(position)
    h_out, m_out, y_out, z_out = {"y": (hy_a, hy_b), "z": (hz_a, hz_b)}, (mx_a, mx_b), {1: yx_b}, {(1, "y"): zy_b, (1, "z"): zz_b}
    middle = hid.at[1]
    begin, ready, peer, stages = gather_stages(links, position, wi_ref, wo_ref, wi, wo, load_sems)
    others = [(zc * SIDE + y, rem(me + k, ROW)) for k in range(1, ROW)]

    def spot(axis, o):
        return spots[axis, o % SIDE]

    def device(axis, o, index):
        moved = {"x": x, "y": y, "z": zc, axis: spot(axis, o)}
        return device_at(moved["x"], moved["y"], moved["z"], index)

    announce(others + [device(axis, o, index) for axis in "yz" for o in AROUND for index in range(PAIR)])
    begin()
    for k, far in enumerate(others):
        links.send(("sc", k), sc_ref, gains.at[me], far)

    def keep(src, dst):
        copy = pltpu.make_async_copy(src, dst, own_sems.at[len(stored)])
        copy.start()
        stored.append(copy)

    def tokens(axis, o, index):
        return pl.ds(pl.multiple_of((PAIR * spot(axis, o) + index) * seq, seq), seq)

    def columns(axis, o):
        size = z.shape[PAIR] // ROW
        return lanes(((0 if axis == "y" else SIDE) + spot(axis, o)) * size, size)

    def send_h(l, axis):
        out = h_out[axis][l].at[:, :, tokens(axis, 0, core)]
        for by in BOTH:
            for index in range(PAIR):
                shared.send(("h", l, axis, by), ht.at[l, :, index], out, device(axis, by, index), batch=("h", l, axis, by, index), lane=core)
        shared.send(("h", l, axis), ht.at[l, :, 1 - core], out, twin, lane=0)
        keep(ht.at[l, :, core], out)

    def pass_h(l, axis, by, index):
        out = h_out[axis][l]
        shared.arrive(("h", l, axis, by), out.at[:, :, tokens(axis, -by, index)], index)
        part = out.at[pl.ds(1 - by, PAIR), :, tokens(axis, -by, index)]
        shared.send(("h2", l, axis, by), part, part, device(axis, by, core), batch=("h2", l, axis, by, index), lane=index)

    def arrive_h(l):
        for axis in "yz":
            for by in BOTH:
                for index in range(PAIR):
                    shared.arrive(("h2", l, axis, by), h_out[axis][l].at[pl.ds(1 - by, PAIR), :, tokens(axis, PAIR, index)], index)
            shared.arrive(("h", l, axis), h_out[axis][l].at[:, :, tokens(axis, 0, 1 - core)], 0)

    def row_block(l, o, index, part=None):
        size = omt.shape[1] // ROW
        start = (PAIR * spot("x", o) + index) * size
        if part is not None:
            size = size // PAIR
            start = start + part * size
        return omt.at[l, pl.ds(pl.multiple_of(start, 16), size)]

    def row_half(k):
        size = m_out[0].shape[0] // PAIR
        return pl.ds(k * size, size)

    def send_m(l):
        out = m_out[l].at[:, tokens("x", 0, core)]
        for k, by in enumerate(BOTH):
            for index in range(PAIR):
                shared.send(("mr", l, by), row_block(l, PAIR, index, k), relay_m.at[l, k, core], device("x", by, index), batch=("mr", l, by, index), lane=core)
        for by in BOTH:
            for index in range(PAIR):
                shared.send(("m", l, by), row_block(l, by, index), out, device("x", by, index), batch=("m", l, by, index), lane=core)
        shared.send(("m", l), row_block(l, 0, 1 - core), out, twin, lane=0)
        keep(row_block(l, 0, core), out)

    def pass_m(l, by, index):
        k = (1 - by) // PAIR
        shared.arrive(("mr", l, by), relay_m.at[l, k, index], index)
        shared.send(("m2", l, by), relay_m.at[l, k, index], m_out[l].at[row_half(k), tokens("x", -by, index)], device("x", by, core),
                    batch=("m2", l, by, index), lane=index)

    def arrive_m(l):
        for k, by in enumerate(BOTH):
            for index in range(PAIR):
                shared.arrive(("m", l, by), m_out[l].at[:, tokens("x", -by, index)], index)
                shared.arrive(("m2", l, by), m_out[l].at[row_half(k), tokens("x", PAIR, index)], index)
        shared.arrive(("m", l), m_out[l].at[:, tokens("x", 0, 1 - core)], 0)

    def token_half(axis, o, k):
        return pl.ds(pl.multiple_of((PAIR * spot(axis, o) + core) * seq + k * (seq // PAIR), seq // PAIR), seq // PAIR)

    def send_y(l):
        src, out = dy_ref, y_out[l].at[tokens("x", 0, core)]
        for by in BOTH:
            shared.send(("y", l, by), src, out, device("x", by, core), lane=0)
        shared.send(("y", l), src, out, twin, lane=0)
        keep(src, out)

    def pass_y(l, by):
        landed, part = y_out[l].at[tokens("x", -by, core)], y_out[l].at[token_half("x", -by, (1 - by) // PAIR)]
        shared.arrive(("y", l, by), landed, 0)
        shared.send(("y2", l, by), part, part, device("x", by, core), lane=0)
        shared.send(("yp", l, by), landed, landed, twin, lane=0)

    def far_y(l):
        for k, by in enumerate(BOTH):
            shared.arrive(("y2", l, by), y_out[l].at[token_half("x", PAIR, k)], 0)
        landed = y_out[l].at[tokens("x", PAIR, core)]
        shared.send(("yp", l, PAIR), landed, landed, twin, lane=0)

    def arrive_y(l):
        for o in AROUND:
            shared.arrive(("yp", l, o), y_out[l].at[tokens("x", -o, 1 - core)], 0)
        shared.arrive(("y", l), y_out[l].at[tokens("x", 0, 1 - core)], 0)

    def send_z(l, axis):
        out = z_out[l, axis].at[tokens(axis, 0, core)]
        for k, by in enumerate(BOTH):
            shared.send(("zr", l, axis, by), z.at[l, pl.ds(k * (seq // PAIR), seq // PAIR), columns(axis, PAIR)], relay_z.at[l, "yz".index(axis), k],
                        device(axis, by, core), lane=0)
        for by in BOTH:
            shared.send(("z", l, axis, by), z.at[l, :, columns(axis, by)], out, device(axis, by, core), lane=0)
        shared.send(("z", l, axis), z.at[l, :, columns(axis, 0)], out, twin, lane=0)
        keep(z.at[l, :, columns(axis, 0)], out)

    def pass_z(l, axis, by):
        k = (1 - by) // PAIR
        half = relay_z.at[l, "yz".index(axis), k]
        shared.arrive(("zr", l, axis, by), half, 0)
        shared.send(("z2", l, axis, by), half, z_out[l, axis].at[token_half(axis, -by, k)], device(axis, by, core), lane=0)

    def twin_z(l, axis, by):
        landed = z_out[l, axis].at[tokens(axis, -by, core)]
        shared.arrive(("z", l, axis, by), landed, 0)
        shared.send(("zp", l, axis, by), landed, landed, twin, lane=0)

    def far_z(l, axis):
        for k, by in enumerate(BOTH):
            shared.arrive(("z2", l, axis, by), z_out[l, axis].at[token_half(axis, PAIR, k)], 0)
        landed = z_out[l, axis].at[tokens(axis, PAIR, core)]
        shared.send(("zp", l, axis, PAIR), landed, landed, twin, lane=0)

    def arrive_z(l, axis):
        for o in AROUND:
            shared.arrive(("zp", l, axis, o), z_out[l, axis].at[tokens(axis, -o, 1 - core)], 0)
        shared.arrive(("z", l, axis), z_out[l, axis].at[tokens(axis, 0, 1 - core)], 0)

    def send_scale(l):
        for k, far in enumerate(others):
            shared.send(("scale", l, k), sc.at[l], sc_out.at[l, me], far, lane=0)
        keep(sc.at[l], sc_out.at[l, me])

    def arrive_scale(l):
        for k in range(len(others)):
            shared.arrive(("scale", l, k), sc_out.at[l, rem(me + 7 - k, ROW)], 0)

    gains[me] = sc_ref[ALL]
    z[:, :, wi.shape[PAIR]:] = jnp.zeros((PAIR, seq, z.shape[PAIR] - wi.shape[PAIR]), BF)
    entry = (x_ref, hid.at[0])
    angle = lax.broadcasted_iota(jnp.int32, (seq, LANE), 0).astype(F32) * freq_ref[0:1]
    for half in range(PAIR):
        cos_ref[:, LANE * half:LANE * (half + 1)] = jnp.cos(angle)
        sin_ref[:, LANE * half:LANE * (half + 1)] = jnp.sin(angle)
    lane = lax.broadcasted_iota(jnp.int32, turn_ref.shape, 1)
    down = lax.broadcasted_iota(jnp.int32, turn_ref.shape, 0) - lane
    low = rem(lane, HEAD) < BAND
    turn_ref[ALL] = jnp.where(low & (down == BAND), -1.0, jnp.where(jnp.logical_not(low) & (down == -BAND), 1.0, ZERO)).astype(BF)
    kts[ALL] = jnp.zeros(kts.shape, BF)
    pcat[ALL] = jnp.zeros(pcat.shape, BF)
    dscat[ALL] = jnp.zeros(dscat.shape, BF)

    def normalise(l, src):
        @pl.loop(0, seq // BAND, unroll=SIDE)
        def _(r):
            rows = pl.ds(pl.multiple_of(r * BAND, BAND), BAND)
            v = src[rows].astype(F32)
            v = v - jnp.mean(v, axis=-1, keepdims=True)
            var = jnp.mean(v * v, axis=-1, keepdims=True)
            h[l, rows] = (v * lax.rsqrt(var + 1e-6) * gain_ref[l:l + 1]).astype(BF)

    def project(l):
        strip = wi.shape[PAIR] // 5

        @pl.loop(0, 5)
        def _(i):
            at = lanes(i * strip, strip)
            z[l, :, at] = product(h[l], wi[l, :, at]).astype(BF)

    def heads(l):
        cos, sin = cos_ref[ALL], sin_ref[ALL]
        for g in range(dim // WIDE):
            q = z[l, :, g * WIDE:(g + 1) * WIDE]
            qr[l, :, g * WIDE:(g + 1) * WIDE] = ((q.astype(F32) * cos + product(q, turn_ref[ALL]) * sin) * 0.125).astype(BF)
        kv = z[l, :, dim:dim + LANE]
        turned = kv.astype(F32) * cos[:, :LANE] + product(kv, turn_ref[:LANE, :LANE]) * sin[:, :LANE]
        first = lax.broadcasted_iota(jnp.int32, turned.shape, 1) < HEAD
        key_lo = jnp.where(first, turned, ZERO)
        val_hi = jnp.where(first, ZERO, kv.astype(F32))
        return key_lo, pltpu.roll(key_lo, HEAD, 1), pltpu.roll(val_hi, HEAD, 1), val_hi

    def slot_rows(ref, lo, hi):
        zero = jnp.zeros((seq, LANE), BF)
        lo, hi = lo.astype(BF), hi.astype(BF)
        for i, (left, right) in enumerate(((lo, zero), (hi, zero), (zero, lo), (zero, hi))):
            ref[i * seq:(i + 1) * seq, :LANE] = left
            ref[i * seq:(i + 1) * seq, LANE:] = right

    def slot_cols(ref, lo):
        flat = lo.T[:HEAD].astype(BF)
        for i in range(SIDE):
            ref[HEAD * i:HEAD * (i + 1), i * seq:(i + 1) * seq] = flat

    def chances(i, half):
        n, at = LANE * (half + 1), slice(LANE * half, LANE * (half + 1))
        rows = pl.ds(pl.multiple_of(i * seq, seq), n)
        s = scores[rows, at]
        query = lax.broadcasted_iota(jnp.int32, s.shape, 1) + LANE * half
        s = jnp.where(query >= lax.broadcasted_iota(jnp.int32, s.shape, 0), s, -1e30)
        e = jnp.exp(s - jnp.max(s, axis=0, keepdims=True))
        return rows, at, e * (1.0 / jnp.sum(e, axis=0, keepdims=True))

    def attend(l):
        key_lo, key_hi, val_lo, _ = heads(l)
        slot_rows(ksl, key_lo, key_hi)
        slot_cols(kts, val_lo)
        flip(lambda at: qr[l, :, lanes(at, WIDE)], qt, dim)

        @pl.loop(0, dim // WIDE)
        def _(g):
            rows = pl.ds(pl.multiple_of(g * WIDE, WIDE), WIDE)
            scores[ALL] = product(ksl[ALL], qt[rows])

            @pl.loop(0, SIDE)
            def _(i):
                for half in range(PAIR):
                    keys, at, p = chances(i, half)
                    pcat[keys, at] = p.astype(BF)
            flat = product(kts[ALL], pcat[ALL]).astype(BF)
            omt[l, rows] = flat
            om[:, lanes(g * WIDE, WIDE)] = flat.T

    def mlp(l):
        @pl.loop(0, seq // BAND)
        def _(r):
            rows = pl.ds(pl.multiple_of(r * BAND, BAND), BAND)

            @pl.loop(0, ff // STRIP)
            def _(i):
                gate = z[l, rows, lanes(dim + LANE + i * STRIP, STRIP)].astype(F32)
                up = z[l, rows, lanes(dim + LANE + ff + i * STRIP, STRIP)].astype(F32)
                om[rows, lanes(dim + i * STRIP, STRIP)] = (gate * jax.nn.sigmoid(gate) * up).astype(BF)

    def put_out(l, dst):
        for n in range(dim // WIDE):
            cols = slice(n * WIDE, (n + 1) * WIDE)
            total = product(om[ALL], wo[l, :, cols])
            dst[:, cols] = (entry[l][:, cols].astype(F32) + total).astype(BF)

    def flip(src, dst, width, first=0):
        @pl.loop(first // WIDE, width // WIDE)
        def _(i):
            dst[pl.ds(pl.multiple_of(i * WIDE, WIDE), WIDE)] = src(i * WIDE).T

    upstream = (middle, dy_ref)

    def back_out(l):
        dy = upstream[l]
        flip(lambda at: dy[:, lanes(at, WIDE)], dyt, dim)

        @pl.loop(0, wo.shape[1] // dim)
        def _(n):
            rows = pl.ds(pl.multiple_of(n * dim, dim), dim)
            part = product(wo[l, rows], dyt[ALL]).astype(BF)
            om[:, lanes(n * dim, dim)] = part.T

            @pl.when(n == 0)
            def _():
                dot_heads[ALL] = part

    def back_mlp(l):
        @pl.loop(0, seq // BAND)
        def _(r):
            rows = pl.ds(pl.multiple_of(r * BAND, BAND), BAND)

            @pl.loop(0, ff // STRIP)
            def _(i):
                gate_at, up_at = lanes(dim + LANE + i * STRIP, STRIP), lanes(dim + LANE + ff + i * STRIP, STRIP)
                gate, up = z[l, rows, gate_at].astype(F32), z[l, rows, up_at].astype(F32)
                d = om[rows, lanes(dim + i * STRIP, STRIP)].astype(F32)
                sig = jax.nn.sigmoid(gate)
                du = d * up
                z[l, rows, gate_at] = (du * sig + du * gate * (sig * (1.0 - sig))).astype(BF)
                z[l, rows, up_at] = (d * (gate * sig)).astype(BF)

    def back_heads(l):
        key_lo, key_hi, val_lo, val_hi = heads(l)
        slot_rows(ksl, key_lo, key_hi)
        slot_rows(vsl, val_lo, val_hi)
        slot_cols(kts, key_lo)
        dkv[ALL] = jnp.zeros(dkv.shape, F32)
        flip(lambda at: qr[l, :, lanes(at, WIDE)], qt, dim)
        for at in range(0, dim, LANE):
            pair = slice(at, at + LANE)
            turned_q[:, pair] = pltpu.roll(qr[l, :, pair].astype(F32), HEAD, 1).astype(BF)
            turned_o[:, pair] = pltpu.roll(om[:, pair].astype(F32), HEAD, 1).astype(BF)

    def back_quad(l):
        @pl.loop(0, dim // WIDE)
        def _(g):
            quad(l, g)

    def quad(l, g):
        cols = pl.ds(pl.multiple_of(g * WIDE, WIDE), WIDE)
        scores[ALL] = product(ksl[ALL], qt[cols])
        dscores[ALL] = product(vsl[ALL], dot_heads[cols])

        @pl.loop(0, SIDE)
        def _(i):
            for half in range(PAIR):
                keys, at, p = chances(i, half)
                pcat[keys, at] = p.astype(BF)
                pd = p * dscores[keys, at].astype(BF).astype(F32)
                dscat[keys, at] = (pd - p * jnp.sum(pd, axis=0, keepdims=True)).astype(BF)
        dq = product(kts[ALL], dscat[ALL]).astype(BF).T
        back = dq.astype(F32) * cos_ref[ALL] - product(dq, turn_ref[ALL]) * sin_ref[ALL]
        z[l, :, cols] = (back * 0.125).astype(BF)
        for i in range(SIDE):
            keys, pair = slice(i * seq, (i + 1) * seq), lanes(g * WIDE + i // PAIR * LANE, LANE)
            even = i % PAIR == 0
            dkv[0] += product(dscat[keys], qr[l, :, pair] if even else turned_q[:, pair])
            dkv[1] += product(pcat[keys], turned_o[:, pair] if even else om[:, pair])

    def back_keys(l):
        dk = dkv[0].astype(BF)
        turned = dk.astype(F32) * cos_ref[:, :LANE] - product(dk, turn_ref[:LANE, :LANE]) * sin_ref[:, :LANE]
        first = lax.broadcasted_iota(jnp.int32, turned.shape, 1) < HEAD
        z[l, :, dim:dim + LANE] = jnp.where(first, turned, dkv[1]).astype(BF)

    def back_in(l, half):
        width = wi.shape[PAIR] // 5
        if half == 0:
            dht[ALL] = jnp.zeros(dht.shape, F32)

        @pl.loop(PAIR * half, PAIR + 3 * half)
        def _(i):
            at = lanes(i * width, width)
            dht[ALL] += product(wi[l, :, at], z[l, :, at], ((1,), (1,)))

    def back_norm(l):
        dy, dst = upstream[l], (gx_ref, middle)[l]
        for i in range(dim // WIDE):
            cols = slice(i * WIDE, (i + 1) * WIDE)
            h[l, :, cols] = dht[cols].T.astype(BF)
        sc[l] = jnp.zeros(sc.shape[1:], F32)

        @pl.loop(0, seq // BAND, unroll=SIDE)
        def _(r):
            rows = pl.ds(pl.multiple_of(r * BAND, BAND), BAND)
            v = entry[l][rows].astype(F32)
            v = v - jnp.mean(v, axis=-1, keepdims=True)
            scale = lax.rsqrt(jnp.mean(v * v, axis=-1, keepdims=True) + 1e-6)
            hat = v * scale
            d = h[l, rows].astype(F32)
            each = (d * hat).reshape(SIDE, ROW, dim)
            sc[l] += (each[0] + each[1]) + (each[PAIR] + each[3])
            d = d * gain_ref[l:l + 1]
            d = scale * (d - jnp.mean(d, axis=-1, keepdims=True) - hat * jnp.mean(d * hat, axis=-1, keepdims=True))
            dst[rows] = (dy[rows].astype(F32) + d.astype(BF).astype(F32)).astype(BF)

    def do_norm(l):
        if l == 0:
            for k, (_, f) in enumerate(others):
                links.arrive(("sc", k), gains.at[rem(me + 7 - k, ROW)])
            gain_ref[ALL] = jnp.sum(gains[ALL], axis=0)
        normalise(l, entry[l])
        for i in range(dim // WIDE):
            flat = h[l, :, i * WIDE:(i + 1) * WIDE].T
            size = ht.shape[3]
            for b in range(ROW):
                lo, hi = max(b * size, i * WIDE), min((b + 1) * size, (i + 1) * WIDE)
                if lo < hi:
                    ht[l, b // PAIR, b % PAIR, lo - b * size:hi - b * size] = flat[lo - i * WIDE:hi - i * WIDE]

    def do_project(l):
        ready(PAIR * l)
        project(l)

    def do_mlp(l):
        mlp(l)
        flip(lambda at: om[:, lanes(at, WIDE)], omt.at[l], om.shape[1], dim)

    def do_put(l):
        ready(PAIR * l + 1)
        put_out(l, hid.at[0] if l == 0 else y_ref)

    stages.update(
        norm=do_norm, project=do_project, attend=attend, mlp=do_mlp, put=do_put, back_out=back_out, back_mlp=back_mlp, back_heads=back_heads,
        back_quad=back_quad, back_keys=back_keys, back_in=back_in, back_norm=back_norm, send_h=send_h, pass_h=pass_h, send_m=send_m,
        pass_m=pass_m, send_y=send_y, pass_y=pass_y, far_y=far_y, send_z=send_z, pass_z=pass_z, twin_z=twin_z, far_z=far_z,
        send_scale=send_scale, own_z=lambda: keep(z.at[0], z_a), own_y=lambda: keep(middle, dy_a))
    for kind, *task in order:
        stages[kind](*task)
    for l in range(PAIR):
        arrive_h(l)
        arrive_m(l)
        arrive_scale(l)
    arrive_y(1)
    for l, axis in z_out:
        arrive_z(l, axis)
    for copy in stored:
        copy.wait()
    shared.drain()
    links.drain()


def run_layers(x, dy, scale, w_in, w_out, freq, starts=(ZERO, 10.0, 20.0, 30.0)):
    seq, dim = x.shape
    proj, cat = w_in.shape[PAIR], ROW * w_out.shape[1]
    wide = proj + LANE
    hbm, vmem = pl.BlockSpec(memory_space=pltpu.HBM), pl.BlockSpec(memory_space=pltpu.VMEM)
    out = lambda *shape, dtype=BF: jax.ShapeDtypeStruct(shape, dtype)
    buffer = lambda *shape, dtype=BF: pltpu.VMEM(shape, dtype)
    sem = pltpu.SemaphoreType.DMA
    line = ROW * seq
    return pl.pallas_call(
        functools.partial(layers_kernel, layers_order(*w_in.shape[1:], *w_out.shape[1:], seq, starts)),
        out_shape=(out(seq, dim), out(seq, dim), *[out(SIDE, dim // ROW, line)] * SIDE, *[out(cat // ROW, line)] * PAIR, out(line, dim),
                   *[out(line, wide // ROW)] * PAIR, out(seq, wide), out(seq, dim), out(PAIR, ROW, ROW, dim, dtype=F32),
                   out(PAIR, PAIR, PAIR, cat // 16, seq), out(PAIR, PAIR, PAIR, seq // PAIR, wide // ROW)),
        in_specs=[vmem, hbm, hbm] + [vmem] * 3,
        out_specs=[vmem] * PAIR + [hbm] * 14,
        scratch_shapes=[
            buffer(PAIR, dim, proj), buffer(PAIR, cat, dim), buffer(PAIR, seq, wide), buffer(seq, cat), buffer(PAIR, seq, dim),
            buffer(PAIR, seq, dim), buffer(PAIR, seq, dim),
            buffer(WIDE, SIDE * seq), buffer(SIDE * seq, WIDE), buffer(SIDE * seq, WIDE), buffer(seq, dim), buffer(seq, dim),
            buffer(SIDE * seq, seq, dtype=F32), buffer(SIDE * seq, seq, dtype=F32), buffer(SIDE * seq, seq), buffer(SIDE * seq, seq),
            buffer(seq, WIDE, dtype=F32), buffer(seq, WIDE, dtype=F32), buffer(WIDE, WIDE),
            buffer(dim, seq), buffer(dim, seq), buffer(dim, seq, dtype=F32), buffer(PAIR, seq, LANE, dtype=F32),
            buffer(PAIR, cat, seq), buffer(PAIR, SIDE, PAIR, dim // ROW, seq), buffer(dim, seq), buffer(PAIR, ROW, dim, dtype=F32),
            buffer(ROW, ROW, dim, dtype=F32), buffer(ROW, dim, dtype=F32),
            sem((SIDE,)), sem((16,)), sem((200,)), sem((200,)), sem((LANE,)), sem((LANE, PAIR)),
        ],
        compiler_params=pltpu.CompilerParams(collective_id=PAIR, has_side_effects=True, vmem_limit_bytes=67043328),
        name="run_layers",
    )(scale, w_in, w_out, x, dy, freq)


PARTS = (("i", "x", "z", "y", 0, STRIP), ("i", "x", "z", "y", STRIP, 384), ("i", "x", "y", "z", 0, STRIP), ("i", "x", "y", "z", STRIP, 384),
         ("o", "y", "z", "y", 0, 384), ("o", "z", "y", "z", 384, 384))


def reduce_order(rows, rows_b, starts):
    rate = 11650.0
    tasks = []
    sizes = {"y": WIDE * 896 / (PAIR * rate), "z": WIDE * 896 / (PAIR * rate), "x": WIDE * 768 / (PAIR * rate)}
    for axis in "yzx":
        tasks.append((("swap", axis), (0, 0), starts[PAIR] if axis == "x" else ZERO, [], [], [((axis, by), sizes[axis] * n) for by, n in ((1, 1), (-1, 1), (1, PAIR))], 0.3))
        for i, o in enumerate(AROUND):
            tasks.append((("near", axis, o), (0, PAIR), ZERO, [(("swap", axis), i)], [], [("chip", 1.6)], 0.2))
    tasks.append((("fetch", 0), (5, 0), ZERO, [], [("make", 1, len(PARTS) - 1)], [], 0.2))
    for l in (1, 0):
        late = 1 - l
        for c, (kind, first, then, last, at, width) in enumerate(PARTS):
            needs, cost = [], 1.6 * width / STRIP
            if l == 0:
                needs = [(("near", last if kind == "i" else "x", o), 0) for o in AROUND]
            tasks.append((("make", l, c), (9 * late, c), starts[late], needs, [] if l else [("fetch", 0)], [], cost))
            full = SIDE * SIDE * (rows if kind == "i" else rows_b) * width / rate
            sends = [[((first, by), full / ROW) for by in BOTH], [((first, by), full / SIDE) for by in BOTH],
                     [((then, o), full / 16) for o in (1, -1, 1)], []]
            piece = full / 16
            sends += [[((then, by), piece) for by in BOTH], [((then, 1 - PAIR * (c % PAIR)), piece)], [((last, by), SIDE * piece) for by in BOTH],
                      [((last, by), PAIR * piece) for by in BOTH], []]
            for s in range(9):
                task = ("sum", l, c, s)
                needs = [(("sum", l, c, s - 1), k) for k in range(len(sends[s - 1]))] if s else []
                tasks.append((task, (late, -s), ZERO, needs, [("make", l, c)] if s == 0 else [("sum", l, c, s - 1)], sends[s], 0.3))
    return plan(tasks)


def reduce_kernel(order, *refs):
    hy, hz, mx = refs[0:PAIR], refs[PAIR:SIDE], refs[SIDE:6]
    yx1, zy1, zz1, z0, y0, sc = refs[6:12]
    oa, ob = refs[12:14]
    n = len(PARTS)
    total, half, full, small, front = (refs[14 + k * n:14 + (k + 1) * n] for k in range(5))
    (hbuf, zbuf, mbuf, ybuf, scbuf, ssem, rsem, isem, osem, zsem) = refs[14 + 5 * n:]
    position = chip_position()
    x, y, zc, core = position
    place = {"x": x, "y": y, "z": zc}
    twin = device_at(x, y, zc, 1 - core)
    spots, peers = around(position)

    def spot(axis, o):
        return spots[axis, o % SIDE]

    def peer(axis, o):
        return peers[axis, o % SIDE]

    seq, wide = z0.shape
    own = wide // ROW
    loads = {}

    def load(key, src, dst):
        copy = pltpu.make_async_copy(src, dst, isem.at[len(loads)])
        copy.start()
        loads[key] = copy

    def fetch(l):
        if l:
            load(("z", 1, "y"), zy1, zbuf.at[1, 0])
        load(("h", l, "y"), hy[l], hbuf.at[l, 0])
        if l:
            load(("z", 1, "z"), zz1, zbuf.at[1, 1])
        load(("h", l, "z"), hz[l], hbuf.at[l, 1])
        load(("m", l), mx[l], mbuf.at[l])
        if l:
            load(("y", 1), yx1, ybuf.at[1])
        load(("s", l), sc.at[l], scbuf.at[l])

    fetch(1)
    done = set()

    def loaded(*keys):
        for key in keys:
            if key not in done:
                loads[key].wait()
                done.add(key)

    announce([peer(axis, o) for axis in "xyz" for o in AROUND] + [twin])
    links = Links(ssem, rsem)

    def columns(axis, o):
        return lanes(((0 if axis == "y" else SIDE) + spot(axis, o)) * own, own)

    def tokens(axis, o, index):
        return pl.ds(pl.multiple_of((PAIR * spot(axis, o) + index) * seq, seq), seq)

    def target(axis):
        return ybuf.at[0] if axis == "x" else zbuf.at[0, "yz".index(axis)]

    def swap(axis):
        def part(o):
            return y0 if axis == "x" else z0.at[:, columns(axis, o)]

        mine = target(axis).at[tokens(axis, 0, core)]
        for o in AROUND:
            links.send(("swap", axis, o), part(o), mine, peer(axis, o))
        links.send(("swap", axis), part(0), mine, twin)
        load(("own", axis), part(0), mine)

    def near(axis, o):
        landed = target(axis).at[tokens(axis, -o, core)]
        links.arrive(("swap", axis, o), landed)
        links.send(("near", axis, o), landed, landed, twin)

    def joined(axis):
        if axis not in done:
            done.add(axis)
            loaded(("own", axis))
            links.arrive(("swap", axis), target(axis).at[tokens(axis, 0, 1 - core)])
            for o in AROUND:
                links.arrive(("near", axis, o), target(axis).at[tokens(axis, -o, 1 - core)])

    def make(l, c):
        kind, first, then, last, at, width = PARTS[c]
        if kind == "i":
            i = "yz".index(last)
            loaded(("h", l, last))
            if l:
                loaded(("z", l, last))
            else:
                joined(last)
            size = total[c].shape[3]
            for lo in range(0, width, WIDE):
                hi = min(width, lo + WIDE)
                part = product(hbuf[l, i].reshape(-1, hbuf.shape[-1]), zbuf[l, i, :, at + lo:at + hi])
                for r in range(16):
                    total[c][l, r // SIDE, r % SIDE, :, lo:hi] = part[r * size:(r + 1) * size]
            return
        loaded(("m", l), ("s", l))
        if l:
            loaded(("y", l))
        else:
            joined("x")
        part = product(mbuf[l], ybuf[l, :, at:at + width])
        size = total[c].shape[3]

        def put(r, value):
            total[c][(l, r // SIDE, r % SIDE) if first == "y" else (l, r % SIDE, r // SIDE)] = value

        for r in range(part.shape[0] // size):
            put(r, part[r * size:(r + 1) * size])
        gain = jnp.sum(jnp.sum(scbuf[l, :, :, at:at + width], axis=0), axis=0, keepdims=True)
        row = lax.broadcasted_iota(jnp.int32, (size, width), 0)
        put(15, jnp.where(row == 0, gain, ZERO))

    def area(l, c, o, whole):
        kind, first, then, last, at, width = PARTS[c]
        inner = (spot(then, whole) if isinstance(whole, int) else whole)
        outer = spot(last, o)
        if kind == "i":
            cols = lanes(((0 if last == "y" else SIDE) + outer) * own + at, width)
            return oa.at[l, inner, :, cols]
        cols = pl.ds(at, width)
        return ob.at[l, outer, inner, :, cols] if last == "y" else ob.at[l, inner, outer, :, cols]

    def add(l, c, s):
        kind, first, then, last, at, width = PARTS[c]
        t = total[c].at[l]
        way = 1 - PAIR * (c % PAIR)
        key = (l, c)
        if s == 0:
            far = t.at[spot(first, PAIR)]
            for k, by in enumerate(BOTH):
                links.send((*key, "half", by), far.at[pl.ds(PAIR * k, PAIR)], half[c].at[l, k], peer(first, by))
        elif s == 1:
            for k, by in enumerate(BOTH):
                links.arrive((*key, "half", by), half[c].at[l, k])
                mine = t.at[spot(first, by)]
                add_into(mine.at[pl.ds(PAIR * k, PAIR)], half[c].at[l, k])
                links.send((*key, "full", by), mine, full[c].at[l, k], peer(first, by))
        elif s == PAIR:
            mine = t.at[spot(first, 0)]
            for k, by in enumerate(BOTH):
                links.arrive((*key, "full", by), full[c].at[l, k])
                add_into(mine, full[c].at[l, k])
            for k, o in enumerate(AROUND):
                links.send((*key, "small", o), mine.at[spot(then, o)], small[c].at[l, k], peer(then, o), (*key, "small", 1), small[c].at[l], (*key, "small"))
        elif s == 3:
            links.arrive((*key, "small", 1), small[c].at[l])
            mine = t.at[spot(first, 0), spot(then, 0)]
            front[c][l] = (mine[ALL] + small[c][l, 0]) + (small[c][l, 1] + small[c][l, PAIR])
        elif s == SIDE:
            src, dst = front[c].at[l], area(l, c, 0, 0)
            for by in BOTH:
                links.send((*key, "a1", by), src, dst, peer(then, by))
            copy = pltpu.make_async_copy(src, dst, osem.at[l, c])
            copy.start()
            loads["front", l, c] = copy
        elif s == 5:
            for by in BOTH:
                landed = area(l, c, 0, -by)
                links.arrive((*key, "a1", by), landed)
                if way == by:
                    links.send((*key, "b1"), landed, landed, peer(then, by))
        elif s == 6:
            loaded(("front", l, c))
            links.arrive((*key, "b1"), area(l, c, 0, PAIR))
            line = area(l, c, 0, slice(None))
            for by in BOTH:
                links.send((*key, "a2", by), line, line, peer(last, by))
        elif s == 7:
            for k, by in enumerate(BOTH):
                links.arrive((*key, "a2", by), area(l, c, -by, slice(None)))
                part = area(l, c, -by, pl.ds(PAIR * k, PAIR))
                links.send((*key, "a3", by), part, part, peer(last, by))
        else:
            for k, by in enumerate(BOTH):
                links.arrive((*key, "a3", by), area(l, c, PAIR, pl.ds(PAIR * k, PAIR)))

    stages = {"swap": swap, "near": near, "fetch": fetch, "make": make, "sum": add}
    for kind, *task in order:
        stages[kind](*task)
    links.drain()


def add_into(dst, src):
    @pl.loop(0, dst.shape[0])
    def _(i):
        if len(dst.shape) == SIDE:
            for j in range(dst.shape[1]):
                dst[i, j] += src[i, j]
        else:
            dst[i] += src[i]


def around(position):
    place, core = dict(zip("xyz", position)), position[3]
    spots = {(axis, o): step(place[axis], o) for axis in "xyz" for o in range(SIDE)}
    peers = {}
    for axis in "xyz":
        for o in range(1, SIDE):
            moved = {**place, axis: spots[axis, o]}
            peers[axis, o] = device_at(moved["x"], moved["y"], moved["z"], core)
    return spots, peers


def reduce_gradients(operands, starts=(ZERO, ZERO, ZERO)):
    hbm = pl.BlockSpec(memory_space=pltpu.HBM)
    h_rows, m_rows, y_cols, z_cols, z_own, y_own, scale_parts = operands
    part, part_b = h_rows[0].shape[1] // SIDE, (m_rows[0].shape[0] + BAND) // 16
    (line, dim), wide = y_cols.shape, z_own.shape[1]
    out = lambda *shape: jax.ShapeDtypeStruct(shape, F32)
    sem = pltpu.SemaphoreType.DMA

    def buffers(*lead):
        return [pltpu.VMEM((PAIR, *lead, part if e[0] == "i" else part_b, e[5]), F32) for e in PARTS]

    return pl.pallas_call(
        functools.partial(reduce_kernel, reduce_order(part, part_b, starts)),
        out_shape=(out(PAIR, SIDE, part, wide), out(PAIR, SIDE, SIDE, part_b, dim)),
        in_specs=[hbm] * 12,
        out_specs=[hbm] * PAIR,
        scratch_shapes=[
            *buffers(SIDE, SIDE), *buffers(PAIR, PAIR), *buffers(PAIR, SIDE), *buffers(3), *buffers(),
            pltpu.VMEM((PAIR, PAIR, *h_rows[0].shape), BF), pltpu.VMEM((PAIR, PAIR, line, wide // ROW), BF), pltpu.VMEM((PAIR, *m_rows[0].shape), BF),
            pltpu.VMEM((PAIR, line, dim), BF), pltpu.VMEM(scale_parts.shape, F32),
            sem((WIDE,)), sem((WIDE,)), sem((BAND,)), sem((PAIR, len(PARTS))), sem((PAIR,)),
        ],
        compiler_params=pltpu.CompilerParams(collective_id=1, has_side_effects=True, vmem_limit_bytes=67043328),
        name="reduce_gradients",
    )(*h_rows, *m_rows, y_cols, *z_cols, z_own, y_own, scale_parts)


def solution(mesh):
    fsdp_size = mesh.shape["fsdp"]
    batch_spec = P(("dp", "fsdp"), None, None)
    scale_spec = P(None, "fsdp")
    weight_spec = P(None, "fsdp", None)

    def device_step(x_in, grad_y, norm_scale, w_in, w_out):
        n_layers = w_in.shape[0]
        seq_len, model_dim = x_in.shape[1:]
        proj_dim = w_in.shape[PAIR]
        ff_dim = w_out.shape[1] * fsdp_size - model_dim
        head_dim = (proj_dim - model_dim - PAIR * ff_dim) // PAIR
        rows, rows_out = norm_scale.shape[1], w_out.shape[1]
        scale_rows = jnp.zeros((ROW, model_dim), jnp.float32)
        scale_rows = lax.dynamic_update_slice(scale_rows, norm_scale.astype(jnp.float32), (0, lax.axis_index("fsdp") * rows))
        half_dim = head_dim // PAIR
        freq = 10000.0 ** (-(jnp.arange(half_dim, dtype=jnp.float32) * 2.0 / head_dim))
        freq = jnp.broadcast_to(jnp.tile(freq, LANE // half_dim), (ROW, LANE))
        hidden, grad_hidden, *rest = run_layers(x_in[0], grad_y[0], scale_rows, w_in, w_out, freq)
        in_sums, out_sums = reduce_gradients((rest[0:SIDE], rest[SIDE:6], rest[6], rest[7:9], rest[9], rest[10], rest[11]))
        in_grads = in_sums.reshape(n_layers, rows, -1)[:, :, :proj_dim]
        out_rows = out_sums.reshape(n_layers, -1, model_dim)
        scale_grads = lax.dynamic_slice(out_rows[:, rows_out], (0, lax.axis_index("fsdp") * rows), (n_layers, rows))
        out_grads = out_rows[:, :rows_out]
        return hidden[None], grad_hidden[None], scale_grads, in_grads, out_grads

    return jax.shard_map(
        device_step,
        mesh=mesh,
        in_specs=(batch_spec, batch_spec, scale_spec, weight_spec, weight_spec),
        out_specs=(batch_spec, batch_spec, scale_spec, weight_spec, weight_spec),
        check_vma=False,
    )
```

profile of v0, /device:TPU:0, one launch (start us, length us, event | category | flops | bytes accessed | tf_op | source)
XLA Modules:
  0.0 261.1 jit_solution(3066623065269637320)
XLA Ops:
  0.6 0.7 convert_element_type.3
  1.3 0.1 tile.10
  1.4 0.6 broadcast_in_dim.13.freq_ref
  2.0 0.6 broadcast_in_dim.12
  2.6 1.4 dynamic_update_slice.3.sc_ref
  4.0 136.4 %run_layers.1 = (bf16[256,768]{1,0:T(8,128)(2,1)}, bf16[256,768]{1,0:T(8,128)(2,1)}, bf16[4,96,2048]{2,1,0:T(8,128)(2,1)}, bf16[4,96,2048]{2,1,0:T(8,128)(2,1)},...) custom-call(f32[8,768]{1,0:T(8,128)} %dynamic_update_slice.3.sc_ref,, ...), custom_call_target="tpu_custom_call" | custom-call | tf_op jit(solution)/shard_map/run_layers/pallas_call | solution.py:752
  140.4 111.3 %reduce_gradients.1 = (f32[2,4,24,7168]{3,2,1,0:T(8,128)}, f32[2,4,4,32,768]{4,3,2,1,0:T(8,128)}) custom-call(bf16[4,96,2048]{2,1,0:T(8,128)(2,1)} %get-tuple-element.23.refs_0_, bf16[4,96,2048]{2,1,0:T(8,128)(2,1)} %get-tuple-element.24.refs_1_, bf16[4,96,2048]{2,1,0:T(8,128)(2,1)} %get-tuple-element.25.refs_2_, ...), custom_call_target="tpu_custom_call" | custom-call | tf_op jit(solution)/shard_map/reduce_gradients/pallas_call | solution.py:1027
  251.7 0.0 copy-start
  251.7 5.4 %slice.13 = f32[2,96,7040]{2,1,0:T(8,128)} slice(f32[2,96,7168]{2,1,0:T(8,128)} %bitcast.7), slice={[0:2], [0:96], [0:7040]} | slice | bytes 10813440 | tf_op jit(solution)/shard_map/slice | solution.py:1063
  257.2 0.0 copy-done
  257.2 0.0 copy-start.2
  257.2 0.0 copy-start.1
  257.2 1.8 slice.14
  259.0 0.6 constant_dynamic-slice_fusion
  259.6 0.0 copy-done.2
  259.6 0.7 copy.13
  260.4 0.0 copy-done.1
  260.4 0.7 copy.14
  (3 shorter events, 0.0 us)
Async XLA Ops:
  251.7 5.5 %copy-start = (f32[2,4,4,32,768]{4,3,2,1,0:T(8,128)S(1)}, f32[2,4,4,32,768]{4,3,2,1,0:T(8,128)}, u32[]{:S(2)}) copy-start(f32[2,4,4,32,768]{4,3,2,1,0:T(8,128)} %get-tuple-element.35) | copy-start | bytes 9437188
  257.2 2.4 copy-start.2
  257.2 3.2 %copy-start.1 = (bf16[256,768]{1,0:T(8,128)(2,1)S(1)}, bf16[256,768]{1,0:T(8,128)(2,1)}, u32[]{:S(2)}) copy-start(bf16[256,768]{1,0:T(8,128)(2,1)} %get-tuple-element.22) | copy-start | bytes 1179652
where the time goes:
time: 262 us; the launch traced here: 261 us
  Pallas kernels  248 us (95%)
  local copies, waits for them, and re-layouts  12 us (5%)
    pallas_call x1, Pallas kernels, run_layers(): pl.pallas_call(functools.partial(layers_kernel, layers_order(*w_in.shape[...  136 us
    pallas_call x1, Pallas kernels, reduce_gradients(): pl.pallas_call(functools.partial(reduce_kernel, reduce_order(part, part_b...  111 us
    slice x1, local copies, waits for them, and re-layouts, device_step(): in_grads = in_sums.reshape(n_layers, rows, -1)[:, :, :proj_dim]  5.44 us

commit v1 on v0

--- a/solution.py
+++ b/solution.py
@@ -1,6 +1,7 @@
 import functools
 import jax
 import jax.numpy as jnp
+import numpy as np
 from jax import lax
 from jax.experimental import pallas as pl
 from jax.experimental.pallas import tpu as pltpu
@@ -18,23 +19,24 @@
 class Links:
     def __init__(self, send_sems, recv_sems):
         self.send_sems, self.recv_sems = send_sems, recv_sems
-        self.slots, self.batches, self.sent = {}, {}, {}
+        self.slots, self.batches, self.sent, self.count = {}, {}, {}, 0
+
+    def _landing(self, key, lane):
+        if key not in self.slots:
+            self.slots[key] = self.count
+            self.count += 1 if lane is None else PAIR
+        return self.recv_sems.at[self.slots[key] + (0 if lane is None else lane)]
 
     def send(self, key, src, dst, device, landing=None, whole=None, batch=None, lane=None):
-        slot = self.slots.setdefault(landing or key, len(self.slots))
         leaving = self.batches.setdefault(batch or key, len(self.batches))
         copy = pltpu.make_async_remote_copy(
-            src_ref=src, dst_ref=dst, send_sem=self.send_sems.at[leaving], recv_sem=self._landing(slot, lane),
+            src_ref=src, dst_ref=dst, send_sem=self.send_sems.at[leaving], recv_sem=self._landing(landing or key, lane),
             device_id=device, device_id_type=MESH_ID)
         copy.start()
-        self.sent[batch or key] = (whole or src, leaving)
-
-    def _landing(self, slot, lane):
-        return self.recv_sems.at[slot] if lane is None else self.recv_sems.at[slot, lane]
+        self.sent[batch or key] = (src if whole is None else whole, leaving)
 
     def arrive(self, key, landed, lane=None):
-        slot = self.slots.setdefault(key, len(self.slots))
-        pltpu.make_async_copy(landed, landed, self._landing(slot, lane)).wait()
+        pltpu.make_async_copy(landed, landed, self._landing(key, lane)).wait()
 
     def drain(self):
         for left, leaving in self.sent.values():
@@ -234,20 +236,22 @@
         _, out, size, _ = mats[m]
         return out.at[pl.ds(pl.multiple_of((PAIR * xb + index) * size, BAND), size)]
 
-    def colors(m):
-        return "yzx" if mats[m][3] else "yz"
+    def group(m, color):
+        _, out, _, is_in = mats[m]
+        (_, nr), (c, nc) = region(is_in, color, 0)[0]
+        return dict(batch=(m, color), whole=out.at[pl.ds(0, nr * (3 if color == "x" else 12)), pl.ds(c, nc)])
 
     def reach(m, color):
         src, _, _, is_in = mats[m]
         area = region(is_in, color, place[color])[0]
         for by in BOTH:
-            links.send((m, "x1", color, by), src.at[pl.ds(pl.multiple_of(area[0][0], ROW), area[0][1]), pl.ds(*area[1])], at(m, x, area), peer("x", by))
+            links.send((m, "x1", color, by), src.at[pl.ds(pl.multiple_of(area[0][0], ROW), area[0][1]), pl.ds(*area[1])], at(m, x, area), peer("x", by), **group(m, color))
 
     def launch(m, color, off):
         is_in = mats[m][3]
         moved = at(m, spot("x", off), region(is_in, color, place[color])[0])
         for by in BOTH:
-            links.send((m, "p1", color, off, by), moved, moved, peer(color, by))
+            links.send((m, "p1", color, off, by), moved, moved, peer(color, by), **group(m, color))
 
     def relay(m, color, by):
         is_in = mats[m][3]
@@ -255,15 +259,13 @@
         areas = region(is_in, color, place[color])
         links.arrive((m, "x1", color, by), at(m, xb, areas[0]))
         part = at(m, xb, areas[1] if by == 1 else areas[PAIR])
-        links.send((m, "x2", color, by), part, part, peer("x", by))
+        links.send((m, "x2", color), part, part, peer("x", by), **group(m, color))
         if color != "x":
             launch(m, color, -by)
 
     def far(m, color):
         is_in = mats[m][3]
-        areas = region(is_in, color, place[color])
-        for by in BOTH:
-            links.arrive((m, "x2", color, by), at(m, spot("x", PAIR), areas[1] if by == 1 else areas[PAIR]))
+        links.arrive((m, "x2", color), at(m, spot("x", PAIR), region(is_in, color, place[color])[0]))
         if color != "x":
             launch(m, color, PAIR)
 
@@ -273,17 +275,22 @@
         areas = region(is_in, color, spot(color, -by))
         links.arrive((m, "p1", color, off, by), at(m, xb, areas[0]))
         part = at(m, xb, areas[1] if by == 1 else areas[PAIR])
-        links.send((m, "p2", color, off, by), part, part, peer(color, by))
+        links.send((m, "p2", color, off), part, part, peer(color, by), **group(m, color))
 
     def close(m, color, off):
         is_in = mats[m][3]
-        areas = region(is_in, color, spot(color, PAIR))
-        for by in BOTH:
-            links.arrive((m, "p2", color, off, by), at(m, spot("x", off), areas[1] if by == 1 else areas[PAIR]))
+        links.arrive((m, "p2", color, off), at(m, spot("x", off), region(is_in, color, spot(color, PAIR))[0]))
+
+    def four(m):
+        _, out, size, _ = mats[m]
+        return out.at[pl.ds(0, SIDE * size)]
+
+    def give(m, src, dst):
+        links.send((m, "chip"), src, dst, twin, batch=(m, "chip"), whole=four(m))
 
     def hand(m, off):
         whole = block(m, spot("x", off), core)
-        links.send((m, "d2d", off), whole, whole, twin)
+        give(m, whole, whole)
 
     owns = []
 
@@ -292,12 +299,11 @@
             copy = pltpu.make_async_copy(src, block(m, x, core), lsem.at[m])
             copy.start()
             owns.append(copy)
-            links.send((m, "d2d", 0), src, block(m, x, core), twin)
+            give(m, src, block(m, x, core))
 
     def ready(m):
         owns[m].wait()
-        for off in (0, -1, 1, PAIR):
-            links.arrive((m, "d2d", off), block(m, spot("x", off), 1 - core))
+        links.arrive((m, "chip"), four(m))
 
     return begin, ready, peer, {"reach": reach, "relay": relay, "far": far, "pass": pass_on, "close": close, "hand": hand}
 
@@ -316,7 +322,7 @@
 def layers_kernel(order, sc_ref, wi_ref, wo_ref, x_ref, dy_ref, freq_ref,
                   y_ref, gx_ref, hy_a, hy_b, hz_a, hz_b, mx_a, mx_b, yx_b, zy_b, zz_b, z_a, dy_a, sc_out, relay_m, relay_z,
                   wi, wo, z, om, h, hid, qr, kts, vsl, ksl, turned_q, turned_o, scores, dscores, pcat, dscat, cos_ref, sin_ref, turn_ref,
-                  dot_heads, qt, dht, dkv, omt, ht, dyt, sc, gains, gain_ref, load_sems, own_sems, send_sems, recv_sems,
+                  dot_heads, qt, dht, dkv, omt, ht, dyt, sc, gains, own_gain, gain_ref, load_sems, own_sems, send_sems, recv_sems,
                   share_send_sems, share_recv_sems):
     seq, dim = x_ref.shape
     ff = (wi.shape[PAIR] - dim - LANE) // PAIR
@@ -339,10 +345,16 @@
         moved = {"x": x, "y": y, "z": zc, axis: spot(axis, o)}
         return device_at(moved["x"], moved["y"], moved["z"], index)
 
+    own_gain[ALL] = jnp.zeros(own_gain.shape, F32)
+    count = sc_ref.shape[1]
+    for f in range(ROW):
+        @pl.when(me == f)
+        def _():
+            own_gain[0:PAIR, f * count:(f + 1) * count] = sc_ref[ALL].astype(F32)
     announce(others + [device(axis, o, index) for axis in "yz" for o in AROUND for index in range(PAIR)])
     begin()
     for k, far in enumerate(others):
-        links.send(("sc", k), sc_ref, gains.at[me], far)
+        links.send(("sc",), own_gain, gains.at[me], far, batch=("sc",), whole=gains.at[pl.ds(0, 7)])
 
     def keep(src, dst):
         copy = pltpu.make_async_copy(src, dst, own_sems.at[len(stored)])
@@ -356,26 +368,27 @@
         size = z.shape[PAIR] // ROW
         return lanes(((0 if axis == "y" else SIDE) + spot(axis, o)) * size, size)
 
+    def several(batch, ref, n):
+        whole = ref.at[pl.ds(0, n * seq)] if batch[0][0] in "yz" else ref.at[(slice(None),) * (len(ref.shape) - 1) + (pl.ds(0, n * seq),)]
+        return dict(batch=batch, whole=whole)
+
     def send_h(l, axis):
         out = h_out[axis][l].at[:, :, tokens(axis, 0, core)]
         for by in BOTH:
             for index in range(PAIR):
-                shared.send(("h", l, axis, by), ht.at[l, :, index], out, device(axis, by, index), batch=("h", l, axis, by, index), lane=core)
-        shared.send(("h", l, axis), ht.at[l, :, 1 - core], out, twin, lane=0)
+                shared.send(("h", l, axis, by), ht.at[l, :, index], out, device(axis, by, index), lane=core, **several(("h", l, axis), h_out[axis][l], 7))
+        shared.send(("h", l, axis), ht.at[l, :, 1 - core], out, twin, **several(("h", l, axis), h_out[axis][l], 7))
         keep(ht.at[l, :, core], out)
 
     def pass_h(l, axis, by, index):
         out = h_out[axis][l]
         shared.arrive(("h", l, axis, by), out.at[:, :, tokens(axis, -by, index)], index)
         part = out.at[pl.ds(1 - by, PAIR), :, tokens(axis, -by, index)]
-        shared.send(("h2", l, axis, by), part, part, device(axis, by, core), batch=("h2", l, axis, by, index), lane=index)
+        shared.send(("h", l, axis), part, part, device(axis, by, core), **several(("h", l, axis), out, 7))
 
     def arrive_h(l):
         for axis in "yz":
-            for by in BOTH:
-                for index in range(PAIR):
-                    shared.arrive(("h2", l, axis, by), h_out[axis][l].at[pl.ds(1 - by, PAIR), :, tokens(axis, PAIR, index)], index)
-            shared.arrive(("h", l, axis), h_out[axis][l].at[:, :, tokens(axis, 0, 1 - core)], 0)
+            shared.arrive(("h", l, axis), h_out[axis][l].at[:, :, pl.ds(0, 3 * seq)])
 
     def row_block(l, o, index, part=None):
         size = omt.shape[1] // ROW
@@ -393,25 +406,21 @@
         out = m_out[l].at[:, tokens("x", 0, core)]
         for k, by in enumerate(BOTH):
             for index in range(PAIR):
-                shared.send(("mr", l, by), row_block(l, PAIR, index, k), relay_m.at[l, k, core], device("x", by, index), batch=("mr", l, by, index), lane=core)
+                shared.send(("mr", l, by), row_block(l, PAIR, index, k), relay_m.at[l, k, core], device("x", by, index), lane=core, **several(("m", l), m_out[l], 7))
         for by in BOTH:
             for index in range(PAIR):
-                shared.send(("m", l, by), row_block(l, by, index), out, device("x", by, index), batch=("m", l, by, index), lane=core)
-        shared.send(("m", l), row_block(l, 0, 1 - core), out, twin, lane=0)
+                shared.send(("m", l), row_block(l, by, index), out, device("x", by, index), **several(("m", l), m_out[l], 7))
+        shared.send(("m", l), row_block(l, 0, 1 - core), out, twin, **several(("m", l), m_out[l], 7))
         keep(row_block(l, 0, core), out)
 
     def pass_m(l, by, index):
         k = (1 - by) // PAIR
         shared.arrive(("mr", l, by), relay_m.at[l, k, index], index)
-        shared.send(("m2", l, by), relay_m.at[l, k, index], m_out[l].at[row_half(k), tokens("x", -by, index)], device("x", by, core),
-                    batch=("m2", l, by, index), lane=index)
+        shared.send(("m", l), relay_m.at[l, k, index], m_out[l].at[row_half(k), tokens("x", -by, index)], device("x", by, core),
+                    **several(("m2", l), m_out[l], PAIR))
 
     def arrive_m(l):
-        for k, by in enumerate(BOTH):
-            for index in range(PAIR):
-                shared.arrive(("m", l, by), m_out[l].at[:, tokens("x", -by, index)], index)
-                shared.arrive(("m2", l, by), m_out[l].at[row_half(k), tokens("x", PAIR, index)], index)
-        shared.arrive(("m", l), m_out[l].at[:, tokens("x", 0, 1 - core)], 0)
+        shared.arrive(("m", l), m_out[l].at[:, pl.ds(0, 7 * seq)])
 
     def token_half(axis, o, k):
         return pl.ds(pl.multiple_of((PAIR * spot(axis, o) + core) * seq + k * (seq // PAIR), seq // PAIR), seq // PAIR)
@@ -419,69 +428,62 @@
     def send_y(l):
         src, out = dy_ref, y_out[l].at[tokens("x", 0, core)]
         for by in BOTH:
-            shared.send(("y", l, by), src, out, device("x", by, core), lane=0)
-        shared.send(("y", l), src, out, twin, lane=0)
+            shared.send(("y", l, by), src, out, device("x", by, core), **several(("y", l), y_out[l], 7))
+        shared.send(("y", l), src, out, twin, **several(("y", l), y_out[l], 7))
         keep(src, out)
 
     def pass_y(l, by):
         landed, part = y_out[l].at[tokens("x", -by, core)], y_out[l].at[token_half("x", -by, (1 - by) // PAIR)]
-        shared.arrive(("y", l, by), landed, 0)
-        shared.send(("y2", l, by), part, part, device("x", by, core), lane=0)
-        shared.send(("yp", l, by), landed, landed, twin, lane=0)
+        shared.arrive(("y", l, by), landed)
+        shared.send(("y2", l), part, part, device("x", by, core), **several(("y", l), y_out[l], 7))
+        shared.send(("y", l), landed, landed, twin, **several(("y", l), y_out[l], 7))
 
     def far_y(l):
-        for k, by in enumerate(BOTH):
-            shared.arrive(("y2", l, by), y_out[l].at[token_half("x", PAIR, k)], 0)
         landed = y_out[l].at[tokens("x", PAIR, core)]
-        shared.send(("yp", l, PAIR), landed, landed, twin, lane=0)
+        shared.arrive(("y2", l), landed)
+        shared.send(("y", l), landed, landed, twin, **several(("y", l), y_out[l], 7))
 
     def arrive_y(l):
-        for o in AROUND:
-            shared.arrive(("yp", l, o), y_out[l].at[tokens("x", -o, 1 - core)], 0)
-        shared.arrive(("y", l), y_out[l].at[tokens("x", 0, 1 - core)], 0)
+        shared.arrive(("y", l), y_out[l].at[pl.ds(0, SIDE * seq)])
 
     def send_z(l, axis):
         out = z_out[l, axis].at[tokens(axis, 0, core)]
         for k, by in enumerate(BOTH):
             shared.send(("zr", l, axis, by), z.at[l, pl.ds(k * (seq // PAIR), seq // PAIR), columns(axis, PAIR)], relay_z.at[l, "yz".index(axis), k],
-                        device(axis, by, core), lane=0)
+                        device(axis, by, core), **several(("z", l, axis), z_out[l, axis], ROW))
         for by in BOTH:
-            shared.send(("z", l, axis, by), z.at[l, :, columns(axis, by)], out, device(axis, by, core), lane=0)
-        shared.send(("z", l, axis), z.at[l, :, columns(axis, 0)], out, twin, lane=0)
+            shared.send(("z", l, axis, by), z.at[l, :, columns(axis, by)], out, device(axis, by, core), **several(("z", l, axis), z_out[l, axis], ROW))
+        shared.send(("z", l, axis), z.at[l, :, columns(axis, 0)], out, twin, **several(("z", l, axis), z_out[l, axis], ROW))
         keep(z.at[l, :, columns(axis, 0)], out)
 
     def pass_z(l, axis, by):
         k = (1 - by) // PAIR
         half = relay_z.at[l, "yz".index(axis), k]
-        shared.arrive(("zr", l, axis, by), half, 0)
-        shared.send(("z2", l, axis, by), half, z_out[l, axis].at[token_half(axis, -by, k)], device(axis, by, core), lane=0)
+        shared.arrive(("zr", l, axis, by), half)
+        shared.send(("z2", l, axis), half, z_out[l, axis].at[token_half(axis, -by, k)], device(axis, by, core), **several(("z", l, axis), z_out[l, axis], ROW))
 
     def twin_z(l, axis, by):
         landed = z_out[l, axis].at[tokens(axis, -by, core)]
-        shared.arrive(("z", l, axis, by), landed, 0)
-        shared.send(("zp", l, axis, by), landed, landed, twin, lane=0)
+        shared.arrive(("z", l, axis, by), landed)
+        shared.send(("z", l, axis), landed, landed, twin, **several(("z", l, axis), z_out[l, axis], ROW))
 
     def far_z(l, axis):
-        for k, by in enumerate(BOTH):
-            shared.arrive(("z2", l, axis, by), z_out[l, axis].at[token_half(axis, PAIR, k)], 0)
         landed = z_out[l, axis].at[tokens(axis, PAIR, core)]
-        shared.send(("zp", l, axis, PAIR), landed, landed, twin, lane=0)
+        shared.arrive(("z2", l, axis), landed)
+        shared.send(("z", l, axis), landed, landed, twin, **several(("z", l, axis), z_out[l, axis], ROW))
 
     def arrive_z(l, axis):
-        for o in AROUND:
-            shared.arrive(("zp", l, axis, o), z_out[l, axis].at[tokens(axis, -o, 1 - core)], 0)
-        shared.arrive(("z", l, axis), z_out[l, axis].at[tokens(axis, 0, 1 - core)], 0)
+        shared.arrive(("z", l, axis), z_out[l, axis].at[pl.ds(0, SIDE * seq)])
 
     def send_scale(l):
-        for k, far in enumerate(others):
-            shared.send(("scale", l, k), sc.at[l], sc_out.at[l, me], far, lane=0)
+        for far in others:
+            shared.send(("scale", l), sc.at[l], sc_out.at[l, me], far, batch=("scale", l), whole=sc_out.at[l, pl.ds(0, 7)])
         keep(sc.at[l], sc_out.at[l, me])
 
     def arrive_scale(l):
-        for k in range(len(others)):
-            shared.arrive(("scale", l, k), sc_out.at[l, rem(me + 7 - k, ROW)], 0)
-
-    gains[me] = sc_ref[ALL]
+        shared.arrive(("scale", l), sc_out.at[l, pl.ds(0, 7)])
+
+    gains[me] = own_gain[ALL]
     z[:, :, wi.shape[PAIR]:] = jnp.zeros((PAIR, seq, z.shape[PAIR] - wi.shape[PAIR]), BF)
     entry = (x_ref, hid.at[0])
     angle = lax.broadcasted_iota(jnp.int32, (seq, LANE), 0).astype(F32) * freq_ref[0:1]
@@ -665,13 +667,9 @@
 
     def back_in(l, half):
         width = wi.shape[PAIR] // 5
-        if half == 0:
-            dht[ALL] = jnp.zeros(dht.shape, F32)
-
-        @pl.loop(PAIR * half, PAIR + 3 * half)
-        def _(i):
-            at = lanes(i * width, width)
-            dht[ALL] += product(wi[l, :, at], z[l, :, at], ((1,), (1,)))
+        at = slice(PAIR * half * width, (PAIR + 3 * half) * width)
+        part = product(wi[l, :, at], z[l, :, at], ((1,), (1,)))
+        dht[ALL] = dht[ALL] + part if half else part
 
     def back_norm(l):
         dy, dst = upstream[l], (gx_ref, middle)[l]
@@ -696,8 +694,7 @@
 
     def do_norm(l):
         if l == 0:
-            for k, (_, f) in enumerate(others):
-                links.arrive(("sc", k), gains.at[rem(me + 7 - k, ROW)])
+            links.arrive(("sc",), gains.at[pl.ds(0, 7)])
             gain_ref[ALL] = jnp.sum(gains[ALL], axis=0)
         normalise(l, entry[l])
         for i in range(dim // WIDE):
@@ -764,8 +761,8 @@
             buffer(seq, WIDE, dtype=F32), buffer(seq, WIDE, dtype=F32), buffer(WIDE, WIDE),
             buffer(dim, seq), buffer(dim, seq), buffer(dim, seq, dtype=F32), buffer(PAIR, seq, LANE, dtype=F32),
             buffer(PAIR, cat, seq), buffer(PAIR, SIDE, PAIR, dim // ROW, seq), buffer(dim, seq), buffer(PAIR, ROW, dim, dtype=F32),
-            buffer(ROW, ROW, dim, dtype=F32), buffer(ROW, dim, dtype=F32),
-            sem((SIDE,)), sem((16,)), sem((200,)), sem((200,)), sem((LANE,)), sem((LANE, PAIR)),
+            buffer(ROW, ROW, dim, dtype=F32), buffer(ROW, dim, dtype=F32), buffer(ROW, dim, dtype=F32),
+            sem((SIDE,)), sem((13,)), sem((15,)), sem((107,)), sem((13,)), sem((HEAD,)),
         ],
         compiler_params=pltpu.CompilerParams(collective_id=PAIR, has_side_effects=True, vmem_limit_bytes=67043328),
         name="run_layers",
@@ -811,7 +808,7 @@
     oa, ob = refs[12:14]
     n = len(PARTS)
     total, half, full, small, front = (refs[14 + k * n:14 + (k + 1) * n] for k in range(5))
-    (hbuf, zbuf, mbuf, ybuf, scbuf, ssem, rsem, isem, osem, zsem) = refs[14 + 5 * n:]
+    (hbuf, zbuf, mbuf, ybuf, scbuf, ssem, rsem, isem, osem) = refs[14 + 5 * n:]
     position = chip_position()
     x, y, zc, core = position
     place = {"x": x, "y": y, "z": zc}
@@ -826,10 +823,11 @@
 
     seq, wide = z0.shape
     own = wide // ROW
-    loads = {}
+    loads, moving = {}, []
 
     def load(key, src, dst):
-        copy = pltpu.make_async_copy(src, dst, isem.at[len(loads)])
+        copy = pltpu.make_async_copy(src, dst, isem.at[len(moving)])
+        moving.append(key)
         copy.start()
         loads[key] = copy
 
@@ -866,28 +864,29 @@
     def target(axis):
         return ybuf.at[0] if axis == "x" else zbuf.at[0, "yz".index(axis)]
 
+    def seven(axis):
+        return dict(batch=("swap", axis), whole=target(axis).at[pl.ds(0, 7 * seq)])
+
     def swap(axis):
         def part(o):
             return y0 if axis == "x" else z0.at[:, columns(axis, o)]
 
         mine = target(axis).at[tokens(axis, 0, core)]
         for o in AROUND:
-            links.send(("swap", axis, o), part(o), mine, peer(axis, o))
-        links.send(("swap", axis), part(0), mine, twin)
+            links.send(("swap", axis, o), part(o), mine, peer(axis, o), **seven(axis))
+        links.send(("near", axis), part(0), mine, twin, **seven(axis))
         load(("own", axis), part(0), mine)
 
     def near(axis, o):
         landed = target(axis).at[tokens(axis, -o, core)]
         links.arrive(("swap", axis, o), landed)
-        links.send(("near", axis, o), landed, landed, twin)
+        links.send(("near", axis), landed, landed, twin, **seven(axis))
 
     def joined(axis):
         if axis not in done:
             done.add(axis)
             loaded(("own", axis))
-            links.arrive(("swap", axis), target(axis).at[tokens(axis, 0, 1 - core)])
-            for o in AROUND:
-                links.arrive(("near", axis, o), target(axis).at[tokens(axis, -o, 1 - core)])
+            links.arrive(("near", axis), target(axis).at[pl.ds(0, SIDE * seq)])
 
     def make(l, c):
         kind, first, then, last, at, width = PARTS[c]
@@ -936,55 +935,54 @@
         kind, first, then, last, at, width = PARTS[c]
         t = total[c].at[l]
         way = 1 - PAIR * (c % PAIR)
-        key = (l, c)
+        sums = dict(batch=(l, c, 0), whole=t)
+        wide_ones = dict(batch=(l, c, 1), whole=t.at[pl.ds(0, 3)])
+        narrow = dict(batch=(l, c, PAIR), whole=t.at[0, pl.ds(0, PAIR)])
         if s == 0:
             far = t.at[spot(first, PAIR)]
             for k, by in enumerate(BOTH):
-                links.send((*key, "half", by), far.at[pl.ds(PAIR * k, PAIR)], half[c].at[l, k], peer(first, by))
+                links.send((l, c, "half"), far.at[pl.ds(PAIR * k, PAIR)], half[c].at[l, k], peer(first, by), **sums)
         elif s == 1:
+            links.arrive((l, c, "half"), half[c].at[l])
             for k, by in enumerate(BOTH):
-                links.arrive((*key, "half", by), half[c].at[l, k])
                 mine = t.at[spot(first, by)]
                 add_into(mine.at[pl.ds(PAIR * k, PAIR)], half[c].at[l, k])
-                links.send((*key, "full", by), mine, full[c].at[l, k], peer(first, by))
+                links.send((l, c, "full"), mine, full[c].at[l, k], peer(first, by), **sums)
         elif s == PAIR:
             mine = t.at[spot(first, 0)]
-            for k, by in enumerate(BOTH):
-                links.arrive((*key, "full", by), full[c].at[l, k])
+            links.arrive((l, c, "full"), full[c].at[l])
+            for k in range(PAIR):
                 add_into(mine, full[c].at[l, k])
             for k, o in enumerate(AROUND):
-                links.send((*key, "small", o), mine.at[spot(then, o)], small[c].at[l, k], peer(then, o), (*key, "small", 1), small[c].at[l], (*key, "small"))
+                links.send((l, c, "small"), mine.at[spot(then, o)], small[c].at[l, k], peer(then, o), **wide_ones)
         elif s == 3:
-            links.arrive((*key, "small", 1), small[c].at[l])
+            links.arrive((l, c, "small"), small[c].at[l])
             mine = t.at[spot(first, 0), spot(then, 0)]
             front[c][l] = (mine[ALL] + small[c][l, 0]) + (small[c][l, 1] + small[c][l, PAIR])
         elif s == SIDE:
             src, dst = front[c].at[l], area(l, c, 0, 0)
             for by in BOTH:
-                links.send((*key, "a1", by), src, dst, peer(then, by))
+                links.send((l, c, "a1"), src, dst, peer(then, by), **narrow)
             copy = pltpu.make_async_copy(src, dst, osem.at[l, c])
             copy.start()
             loads["front", l, c] = copy
         elif s == 5:
-            for by in BOTH:
-                landed = area(l, c, 0, -by)
-                links.arrive((*key, "a1", by), landed)
-                if way == by:
-                    links.send((*key, "b1"), landed, landed, peer(then, by))
+            links.arrive((l, c, "a1"), t.at[0, pl.ds(0, PAIR)])
+            landed = area(l, c, 0, -way)
+            links.send((l, c, "b1"), landed, landed, peer(then, way), **wide_ones)
         elif s == 6:
             loaded(("front", l, c))
-            links.arrive((*key, "b1"), area(l, c, 0, PAIR))
+            links.arrive((l, c, "b1"), area(l, c, 0, PAIR))
             line = area(l, c, 0, slice(None))
             for by in BOTH:
-                links.send((*key, "a2", by), line, line, peer(last, by))
+                links.send((l, c, "a2"), line, line, peer(last, by), **wide_ones)
         elif s == 7:
+            links.arrive((l, c, "a2"), t.at[pl.ds(0, PAIR)])
             for k, by in enumerate(BOTH):
-                links.arrive((*key, "a2", by), area(l, c, -by, slice(None)))
                 part = area(l, c, -by, pl.ds(PAIR * k, PAIR))
-                links.send((*key, "a3", by), part, part, peer(last, by))
+                links.send((l, c, "a3"), part, part, peer(last, by), **sums)
         else:
-            for k, by in enumerate(BOTH):
-                links.arrive((*key, "a3", by), area(l, c, PAIR, pl.ds(PAIR * k, PAIR)))
+            links.arrive((l, c, "a3"), area(l, c, PAIR, slice(None)))
 
     stages = {"swap": swap, "near": near, "fetch": fetch, "make": make, "sum": add}
     for kind, *task in order:
@@ -1033,7 +1031,7 @@
             *buffers(SIDE, SIDE), *buffers(PAIR, PAIR), *buffers(PAIR, SIDE), *buffers(3), *buffers(),
             pltpu.VMEM((PAIR, PAIR, *h_rows[0].shape), BF), pltpu.VMEM((PAIR, PAIR, line, wide // ROW), BF), pltpu.VMEM((PAIR, *m_rows[0].shape), BF),
             pltpu.VMEM((PAIR, line, dim), BF), pltpu.VMEM(scale_parts.shape, F32),
-            sem((WIDE,)), sem((WIDE,)), sem((BAND,)), sem((PAIR, len(PARTS))), sem((PAIR,)),
+            sem((39,)), sem((96,)), sem((14,)), sem((PAIR, len(PARTS))),
         ],
         compiler_params=pltpu.CompilerParams(collective_id=1, has_side_effects=True, vmem_limit_bytes=67043328),
         name="reduce_gradients",
@@ -1053,12 +1051,10 @@
         ff_dim = w_out.shape[1] * fsdp_size - model_dim
         head_dim = (proj_dim - model_dim - PAIR * ff_dim) // PAIR
         rows, rows_out = norm_scale.shape[1], w_out.shape[1]
-        scale_rows = jnp.zeros((ROW, model_dim), jnp.float32)
-        scale_rows = lax.dynamic_update_slice(scale_rows, norm_scale.astype(jnp.float32), (0, lax.axis_index("fsdp") * rows))
         half_dim = head_dim // PAIR
-        freq = 10000.0 ** (-(jnp.arange(half_dim, dtype=jnp.float32) * 2.0 / head_dim))
-        freq = jnp.broadcast_to(jnp.tile(freq, LANE // half_dim), (ROW, LANE))
-        hidden, grad_hidden, *rest = run_layers(x_in[0], grad_y[0], scale_rows, w_in, w_out, freq)
+        freq = 10000.0 ** (-np.arange(half_dim, dtype=np.float32) * 2.0 / head_dim)
+        freq = jnp.asarray(np.tile(freq.astype(np.float32), (ROW, LANE // half_dim)))
+        hidden, grad_hidden, *rest = run_layers(x_in[0], grad_y[0], norm_scale, w_in, w_out, freq)
         in_sums, out_sums = reduce_gradients((rest[0:SIDE], rest[SIDE:6], rest[6], rest[7:9], rest[9], rest[10], rest[11]))
         in_grads = in_sums.reshape(n_layers, rows, -1)[:, :, :proj_dim]
         out_rows = out_sums.reshape(n_layers, -1, model_dim)

time: 262 us -> 248 us (0.947)
  Pallas kernels: 248 us -> 237 us
    pallas_call x1, Pallas kernels: 136 us -> 129 us  [run_layers(): pl.pallas_call(functools.partial(layers_kernel, layers_order(*w_in.shape[...]
    pallas_call x1, Pallas kernels: 111 us -> 108 us  [reduce_gradients(): pl.pallas_call(functools.partial(reduce_kernel, reduce_order(part, part_b...]
where the time goes in v1:
time: 248 us
  Pallas kernels  237 us (96%)
  local copies, waits for them, and re-layouts  10.2 us (4%)
    pallas_call x1, Pallas kernels, run_layers(): pl.pallas_call(functools.partial(layers_kernel, layers_order(*w_in.shape[...  129 us
    pallas_call x1, Pallas kernels, reduce_gradients(): pl.pallas_call(functools.partial(reduce_kernel, reduce_order(part, part_b...  108 us
    slice x1, local copies, waits for them, and re-layouts, device_step(): in_grads = in_sums.reshape(n_layers, rows, -1)[:, :, :proj_dim]  5.44 us

profile of v1, /device:TPU:0, one launch (start us, length us, event | category | flops | bytes accessed | tf_op | source)
XLA Modules:
  0.0 247.8 jit_solution(1261219953500235413)
XLA Ops:
  0.6 129.4 %run_layers.1 = (bf16[256,768]{1,0:T(8,128)(2,1)}, bf16[256,768]{1,0:T(8,128)(2,1)}, bf16[4,96,2048]{2,1,0:T(8,128)(2,1)}, bf16[4,96,2048]{2,1,0:T(8,128)(2,1)},...) custom-call(bf16[2,96]{1,0:T(2,128)(2,1)} %sc_ref.1, ...), custom_call_target="tpu_custom_call" | custom-call | tf_op jit(solution)/shard_map/run_layers/pallas_call | solution.py:749
  130.0 107.6 %reduce_gradients.1 = (f32[2,4,24,7168]{3,2,1,0:T(8,128)}, f32[2,4,4,32,768]{4,3,2,1,0:T(8,128)}) custom-call(bf16[4,96,2048]{2,1,0:T(8,128)(2,1)} %get-tuple-element.23.refs_0_, bf16[4,96,2048]{2,1,0:T(8,128)(2,1)} %get-tuple-element.24.refs_1_, bf16[4,96,2048]{2,1,0:T(8,128)(2,1)} %get-tuple-element.25.refs_2_, ...), custom_call_target="tpu_custom_call" | custom-call | tf_op jit(solution)/shard_map/reduce_gradients/pallas_call | solution.py:1025
  237.6 0.8 slice.12
  238.4 0.6 constant_dynamic-slice_fusion
  239.0 0.0 copy-start
  239.0 5.4 %slice.13 = f32[2,96,7040]{2,1,0:T(8,128)} slice(f32[2,96,7168]{2,1,0:T(8,128)} %bitcast.7), slice={[0:2], [0:96], [0:7040]} | slice | bytes 10813440 | tf_op jit(solution)/shard_map/slice | solution.py:1059
  244.5 0.0 copy-done
  244.5 0.0 copy-start.2
  244.5 0.0 copy-start.1
  244.5 1.8 slice.14
  246.3 0.0 copy-done.2
  246.3 0.7 copy.13
  247.0 0.0 copy-done.1
  247.0 0.7 copy.14
Async XLA Ops:
  239.0 5.4 %copy-start = (f32[2,4,4,32,768]{4,3,2,1,0:T(8,128)S(1)}, f32[2,4,4,32,768]{4,3,2,1,0:T(8,128)}, u32[]{:S(2)}) copy-start(f32[2,4,4,32,768]{4,3,2,1,0:T(8,128)} %get-tuple-element.35) | copy-start | bytes 9437188
  244.5 1.8 copy-start.2
  244.5 2.5 %copy-start.1 = (bf16[256,768]{1,0:T(8,128)(2,1)S(1)}, bf16[256,768]{1,0:T(8,128)(2,1)}, u32[]{:S(2)}) copy-start(bf16[256,768]{1,0:T(8,128)(2,1)} %get-tuple-element.22) | copy-start | bytes 1179652

commit v2 on v1

--- a/solution.py
+++ b/solution.py
@@ -96,7 +96,8 @@
         edge = cols_i // LANE * SIDE // 9 // PAIR * WIDE
         size = {"y": rows_i // SIDE * edge, "x": rows_i * (cols_i - PAIR * edge)} if is_in else {"y": rows_o // SIDE * cols_o // PAIR}
         size["z"] = size["y"]
-        for color in "yzx" if is_in else "yz":
+        colors = "yzx" if is_in else "yz"
+        for color in colors:
             cost = size[color] / rate
             both = [(("x", by), cost) for by in BOTH]
             spread = [((color, by), cost) for by in BOTH] if color != "x" else []
@@ -112,32 +113,32 @@
                     tasks.append((("pass", m, color, off, by), m, ZERO, [(source, first + i)], [], [((color, by), cost / PAIR)], 0.2))
                 halves = [(("pass", m, color, off, by), 0) for by in BOTH]
                 tasks.append((("close", m, color, off), m, ZERO, halves, [], [], 0.2))
-        for off in (-1, 1, PAIR):
-            last = [("close", m, color, off) for color in "yz"]
-            if is_in:
-                last.append(("far", m, "x") if off == PAIR else ("relay", m, "x", -off))
-            tasks.append((("hand", m, off), m, ZERO, [], last, [("chip", (rows_i * cols_i if is_in else rows_o * cols_o) / 150000.0)], 0.2))
+        for color in colors:
+            part = size[color] * (1 if color == "x" else SIDE)
+            for off in (-1, 1, PAIR):
+                last = (("far", m, "x") if off == PAIR else ("relay", m, "x", -off)) if color == "x" else ("close", m, color, off)
+                tasks.append((("hand", m, color, off), m, ZERO, [], [last], [("chip", part / 150000.0)], 0.2))
     before = []
 
     def work(name, cost, mats=()):
-        needs = [(("hand", m, off), 0) for m in mats for off in (-1, 1, PAIR)]
+        needs = [(("hand", m, color, off), 0) for m in mats for color in ("yz" if m % PAIR else "yzx") for off in (-1, 1, PAIR)]
         tasks.append((name, 99, ZERO, needs, list(before), [], cost))
         before[:] = [name]
 
     for l in range(PAIR):
         work(("norm", l), 0.8)
         work(("project", l), 4.0, [PAIR * l])
-        work(("attend", l), 3.0)
-        work(("mlp", l), 2.4)
+        work(("attend", l), 4.2)
+        work(("mlp", l), 2.2)
         work(("put", l), 1.6, [PAIR * l + 1])
     for l in (1, 0):
         work(("back_out", l), 2.9)
         work(("back_mlp", l), 2.0)
         work(("back_heads", l), 1.0)
-        work(("back_quad", l), 4.8)
+        work(("back_quad", l), 6.0)
         work(("back_keys", l), 0.2)
         for i in range(PAIR):
-            work(("back_in", l, i), 1.3 + 0.7 * i)
+            work(("back_in", l, i), 1.3 + 0.6 * i)
         work(("back_norm", l), 1.0)
     def send(name, rank, start, after, sends):
         tasks.append((name, rank, start, [], [after] if after else [], sends, 0.4))
@@ -173,7 +174,10 @@
         for axis in "zy":
             name = ("send_z", l, axis)
             share = seq * (cols_i + LANE) / ROW
-            send(name, 13, ZERO, ("back_mlp", l) if axis == "z" else ("back_keys", l), both(axis, share / PAIR) + both(axis, share))
+            send(name, 13, ZERO, ("back_mlp", l), both(axis, share / PAIR) + both(axis, share))
+            if axis == "y":
+                name = ("rest_z", l)
+                send(name, 13, ZERO, ("back_keys", l), both(axis, share / ROW) + both(axis, share / SIDE))
             for i, by in enumerate(BOTH):
                 follow(("pass_z", l, axis, by), 13, [(name, i)], [((axis, by), share / PAIR / rate)])
                 follow(("twin_z", l, axis, by), 14, [(name, PAIR + i)], [])
@@ -288,9 +292,12 @@
     def give(m, src, dst):
         links.send((m, "chip"), src, dst, twin, batch=(m, "chip"), whole=four(m))
 
-    def hand(m, off):
-        whole = block(m, spot("x", off), core)
-        give(m, whole, whole)
+    def hand(m, color, off):
+        _, out, size, is_in = mats[m]
+        _, (c, nc) = region(is_in, color, 0)[0]
+        rows = pl.ds(pl.multiple_of((PAIR * spot("x", off) + core) * size, BAND), size)
+        part = out.at[rows, pl.ds(c, nc)]
+        give(m, part, part)
 
     owns = []
 
@@ -446,15 +453,38 @@
     def arrive_y(l):
         shared.arrive(("y", l), y_out[l].at[pl.ds(0, SIDE * seq)])
 
+    def push_z(l, axis, o, ready):
+        out = z_out[l, axis].at[tokens(axis, 0, core)]
+        batch = several(("z", l, axis), z_out[l, axis], ROW)
+
+        def start():
+            if o != PAIR:
+                shared.send(("z", l, axis, o), z.at[l, :, columns(axis, o)], out, device(axis, o, core), **batch)
+                return
+            for k, by in enumerate(BOTH):
+                shared.send(("zr", l, axis, by), z.at[l, pl.ds(k * (seq // PAIR), seq // PAIR), columns(axis, PAIR)], relay_z.at[l, "yz".index(axis), k],
+                            device(axis, by, core), **batch)
+
+        if ready is None:
+            start()
+        else:
+            pl.when(ready)(start)
+
+    def own_part(l, axis):
+        out, mine = z_out[l, axis].at[tokens(axis, 0, core)], z.at[l, :, columns(axis, 0)]
+        shared.send(("z", l, axis), mine, out, twin, **several(("z", l, axis), z_out[l, axis], ROW))
+        keep(mine, out)
+
     def send_z(l, axis):
-        out = z_out[l, axis].at[tokens(axis, 0, core)]
-        for k, by in enumerate(BOTH):
-            shared.send(("zr", l, axis, by), z.at[l, pl.ds(k * (seq // PAIR), seq // PAIR), columns(axis, PAIR)], relay_z.at[l, "yz".index(axis), k],
-                        device(axis, by, core), **several(("z", l, axis), z_out[l, axis], ROW))
-        for by in BOTH:
-            shared.send(("z", l, axis, by), z.at[l, :, columns(axis, by)], out, device(axis, by, core), **several(("z", l, axis), z_out[l, axis], ROW))
-        shared.send(("z", l, axis), z.at[l, :, columns(axis, 0)], out, twin, **several(("z", l, axis), z_out[l, axis], ROW))
-        keep(z.at[l, :, columns(axis, 0)], out)
+        for o in (PAIR, 1, -1):
+            push_z(l, axis, o, spot(axis, o) != 0 if axis == "y" else None)
+        if axis == "z":
+            own_part(l, axis)
+
+    def rest_z(l):
+        for o in (PAIR, 1, -1):
+            push_z(l, "y", o, spot("y", o) == 0)
+        own_part(l, "y")
 
     def pass_z(l, axis, by):
         k = (1 - by) // PAIR
@@ -540,13 +570,15 @@
             ref[HEAD * i:HEAD * (i + 1), i * seq:(i + 1) * seq] = flat
 
     def chances(i, half):
-        n, at = LANE * (half + 1), slice(LANE * half, LANE * (half + 1))
-        rows = pl.ds(pl.multiple_of(i * seq, seq), n)
-        s = scores[rows, at]
-        query = lax.broadcasted_iota(jnp.int32, s.shape, 1) + LANE * half
-        s = jnp.where(query >= lax.broadcasted_iota(jnp.int32, s.shape, 0), s, -1e30)
-        e = jnp.exp(s - jnp.max(s, axis=0, keepdims=True))
-        return rows, at, e * (1.0 / jnp.sum(e, axis=0, keepdims=True))
+        at = slice(LANE * half, LANE * (half + 1))
+        blocks = [pl.ds(pl.multiple_of(i * seq + LANE * k, LANE), LANE) for k in range(half + 1)]
+        s = [scores[keys, at] for keys in blocks]
+        lower = lax.broadcasted_iota(jnp.int32, s[-1].shape, 1) >= lax.broadcasted_iota(jnp.int32, s[-1].shape, 0)
+        s[-1] = jnp.where(lower, s[-1], -1e30)
+        top = functools.reduce(jnp.maximum, [jnp.max(v, axis=0, keepdims=True) for v in s])
+        e = [jnp.exp(v - top) for v in s]
+        scale = 1.0 / sum(jnp.sum(v, axis=0, keepdims=True) for v in e)
+        return at, [(keys, v * scale) for keys, v in zip(blocks, e)]
 
     def attend(l):
         key_lo, key_hi, val_lo, _ = heads(l)
@@ -562,8 +594,9 @@
             @pl.loop(0, SIDE)
             def _(i):
                 for half in range(PAIR):
-                    keys, at, p = chances(i, half)
-                    pcat[keys, at] = p.astype(BF)
+                    at, blocks = chances(i, half)
+                    for keys, p in blocks:
+                        pcat[keys, at] = p.astype(BF)
             flat = product(kts[ALL], pcat[ALL]).astype(BF)
             omt[l, rows] = flat
             om[:, lanes(g * WIDE, WIDE)] = flat.T
@@ -646,10 +679,12 @@
         @pl.loop(0, SIDE)
         def _(i):
             for half in range(PAIR):
-                keys, at, p = chances(i, half)
-                pcat[keys, at] = p.astype(BF)
-                pd = p * dscores[keys, at].astype(BF).astype(F32)
-                dscat[keys, at] = (pd - p * jnp.sum(pd, axis=0, keepdims=True)).astype(BF)
+                at, blocks = chances(i, half)
+                given = [p * dscores[keys, at].astype(BF).astype(F32) for keys, p in blocks]
+                total = sum(jnp.sum(v, axis=0, keepdims=True) for v in given)
+                for (keys, p), v in zip(blocks, given):
+                    pcat[keys, at] = p.astype(BF)
+                    dscat[keys, at] = (v - p * total).astype(BF)
         dq = product(kts[ALL], dscat[ALL]).astype(BF).T
         back = dq.astype(F32) * cos_ref[ALL] - product(dq, turn_ref[ALL]) * sin_ref[ALL]
         z[l, :, cols] = (back * 0.125).astype(BF)
@@ -720,7 +755,7 @@
     stages.update(
         norm=do_norm, project=do_project, attend=attend, mlp=do_mlp, put=do_put, back_out=back_out, back_mlp=back_mlp, back_heads=back_heads,
         back_quad=back_quad, back_keys=back_keys, back_in=back_in, back_norm=back_norm, send_h=send_h, pass_h=pass_h, send_m=send_m,
-        pass_m=pass_m, send_y=send_y, pass_y=pass_y, far_y=far_y, send_z=send_z, pass_z=pass_z, twin_z=twin_z, far_z=far_z,
+        pass_m=pass_m, send_y=send_y, pass_y=pass_y, far_y=far_y, send_z=send_z, rest_z=rest_z, pass_z=pass_z, twin_z=twin_z, far_z=far_z,
         send_scale=send_scale, own_z=lambda: keep(z.at[0], z_a), own_y=lambda: keep(middle, dy_a))
     for kind, *task in order:
         stages[kind](*task)
@@ -778,7 +813,7 @@
     tasks = []
     sizes = {"y": WIDE * 896 / (PAIR * rate), "z": WIDE * 896 / (PAIR * rate), "x": WIDE * 768 / (PAIR * rate)}
     for axis in "yzx":
-        tasks.append((("swap", axis), (0, 0), starts[PAIR] if axis == "x" else ZERO, [], [], [((axis, by), sizes[axis] * n) for by, n in ((1, 1), (-1, 1), (1, PAIR))], 0.3))
+        tasks.append((("swap", axis), (0, 0), starts[PAIR] if axis == "x" else starts[3], [], [], [((axis, by), sizes[axis] * n) for by, n in ((1, 1), (-1, 1), (1, PAIR))], 0.3))
         for i, o in enumerate(AROUND):
             tasks.append((("near", axis, o), (0, PAIR), ZERO, [(("swap", axis), i)], [], [("chip", 1.6)], 0.2))
     tasks.append((("fetch", 0), (5, 0), ZERO, [], [("make", 1, len(PARTS) - 1)], [], 0.2))
@@ -1011,7 +1046,7 @@
     return spots, peers
 
 
-def reduce_gradients(operands, starts=(ZERO, ZERO, ZERO)):
+def reduce_gradients(operands, starts=(ZERO, ZERO, 20.0, ZERO)):
     hbm = pl.BlockSpec(memory_space=pltpu.HBM)
     h_rows, m_rows, y_cols, z_cols, z_own, y_own, scale_parts = operands
     part, part_b = h_rows[0].shape[1] // SIDE, (m_rows[0].shape[0] + BAND) // 16

time: 248 us -> 251 us (1.012)
  no operation moved by 1% of the time
where the time goes in v2:
time: 251 us; the launch traced here: 248 us
  Pallas kernels  238 us (95%)
  local copies, waits for them, and re-layouts  10.2 us (4%)
    pallas_call x1, Pallas kernels, run_layers(): pl.pallas_call(functools.partial(layers_kernel, layers_order(*w_in.shape[...  132 us
    pallas_call x1, Pallas kernels, reduce_gradients(): pl.pallas_call(functools.partial(reduce_kernel, reduce_order(part, part_b...  106 us
    slice x1, local copies, waits for them, and re-layouts, device_step(): in_grads = in_sums.reshape(n_layers, rows, -1)[:, :, :proj_dim]  5.44 us

profile of v2, /device:TPU:0, one launch (start us, length us, event | category | flops | bytes accessed | tf_op | source)
XLA Modules:
  0.0 248.4 jit_solution(6508212915305016577)
XLA Ops:
  0.6 131.7 %run_layers.1 = (bf16[256,768]{1,0:T(8,128)(2,1)}, bf16[256,768]{1,0:T(8,128)(2,1)}, bf16[4,96,2048]{2,1,0:T(8,128)(2,1)}, bf16[4,96,2048]{2,1,0:T(8,128)(2,1)},...) custom-call(bf16[2,96]{1,0:T(2,128)(2,1)} %sc_ref.1, ...), custom_call_target="tpu_custom_call" | custom-call | tf_op jit(solution)/shard_map/run_layers/pallas_call | solution.py:784
  132.3 105.9 %reduce_gradients.1 = (f32[2,4,24,7168]{3,2,1,0:T(8,128)}, f32[2,4,4,32,768]{4,3,2,1,0:T(8,128)}) custom-call(bf16[4,96,2048]{2,1,0:T(8,128)(2,1)} %get-tuple-element.23.refs_0_, bf16[4,96,2048]{2,1,0:T(8,128)(2,1)} %get-tuple-element.24.refs_1_, bf16[4,96,2048]{2,1,0:T(8,128)(2,1)} %get-tuple-element.25.refs_2_, ...), custom_call_target="tpu_custom_call" | custom-call | tf_op jit(solution)/shard_map/reduce_gradients/pallas_call | solution.py:1060
  238.2 0.8 slice.12
  239.0 0.6 constant_dynamic-slice_fusion
  239.7 0.0 copy-start
  239.7 5.4 %slice.13 = f32[2,96,7040]{2,1,0:T(8,128)} slice(f32[2,96,7168]{2,1,0:T(8,128)} %bitcast.7), slice={[0:2], [0:96], [0:7040]} | slice | bytes 10813440 | tf_op jit(solution)/shard_map/slice | solution.py:1094
  245.1 0.0 copy-done
  245.1 0.0 copy-start.2
  245.1 0.0 copy-start.1
  245.1 1.8 slice.14
  246.9 0.0 copy-done.2
  246.9 0.7 copy.13
  247.7 0.0 copy-done.1
  247.7 0.7 copy.14
Async XLA Ops:
  239.7 5.4 %copy-start = (f32[2,4,4,32,768]{4,3,2,1,0:T(8,128)S(1)}, f32[2,4,4,32,768]{4,3,2,1,0:T(8,128)}, u32[]{:S(2)}) copy-start(f32[2,4,4,32,768]{4,3,2,1,0:T(8,128)} %get-tuple-element.35) | copy-start | bytes 9437188
  245.1 1.8 copy-start.2
  245.1 2.5 %copy-start.1 = (bf16[256,768]{1,0:T(8,128)(2,1)S(1)}, bf16[256,768]{1,0:T(8,128)(2,1)}, u32[]{:S(2)}) copy-start(bf16[256,768]{1,0:T(8,128)(2,1)} %get-tuple-element.22) | copy-start | bytes 1179652

commit v3 on v2

--- a/solution.py
+++ b/solution.py
@@ -113,15 +113,15 @@
                     tasks.append((("pass", m, color, off, by), m, ZERO, [(source, first + i)], [], [((color, by), cost / PAIR)], 0.2))
                 halves = [(("pass", m, color, off, by), 0) for by in BOTH]
                 tasks.append((("close", m, color, off), m, ZERO, halves, [], [], 0.2))
-        for color in colors:
-            part = size[color] * (1 if color == "x" else SIDE)
-            for off in (-1, 1, PAIR):
-                last = (("far", m, "x") if off == PAIR else ("relay", m, "x", -off)) if color == "x" else ("close", m, color, off)
-                tasks.append((("hand", m, color, off), m, ZERO, [], [last], [("chip", part / 150000.0)], 0.2))
+        for off in (-1, 1, PAIR):
+            last = [("close", m, color, off) for color in "yz"]
+            if is_in:
+                last.append(("far", m, "x") if off == PAIR else ("relay", m, "x", -off))
+            tasks.append((("hand", m, off), m, ZERO, [], last, [("chip", (rows_i * cols_i if is_in else rows_o * cols_o) / 150000.0)], 0.2))
     before = []
 
     def work(name, cost, mats=()):
-        needs = [(("hand", m, color, off), 0) for m in mats for color in ("yz" if m % PAIR else "yzx") for off in (-1, 1, PAIR)]
+        needs = [(("hand", m, off), 0) for m in mats for off in (-1, 1, PAIR)]
         tasks.append((name, 99, ZERO, needs, list(before), [], cost))
         before[:] = [name]
 
@@ -292,12 +292,9 @@
     def give(m, src, dst):
         links.send((m, "chip"), src, dst, twin, batch=(m, "chip"), whole=four(m))
 
-    def hand(m, color, off):
-        _, out, size, is_in = mats[m]
-        _, (c, nc) = region(is_in, color, 0)[0]
-        rows = pl.ds(pl.multiple_of((PAIR * spot("x", off) + core) * size, BAND), size)
-        part = out.at[rows, pl.ds(c, nc)]
-        give(m, part, part)
+    def hand(m, off):
+        whole = block(m, spot("x", off), core)
+        give(m, whole, whole)
 
     owns = []
 
@@ -813,7 +810,7 @@
     tasks = []
     sizes = {"y": WIDE * 896 / (PAIR * rate), "z": WIDE * 896 / (PAIR * rate), "x": WIDE * 768 / (PAIR * rate)}
     for axis in "yzx":
-        tasks.append((("swap", axis), (0, 0), starts[PAIR] if axis == "x" else starts[3], [], [], [((axis, by), sizes[axis] * n) for by, n in ((1, 1), (-1, 1), (1, PAIR))], 0.3))
+        tasks.append((("swap", axis), (0, 0), starts[PAIR] if axis == "x" else ZERO, [], [], [((axis, by), sizes[axis] * n) for by, n in ((1, 1), (-1, 1), (1, PAIR))], 0.3))
         for i, o in enumerate(AROUND):
             tasks.append((("near", axis, o), (0, PAIR), ZERO, [(("swap", axis), i)], [], [("chip", 1.6)], 0.2))
     tasks.append((("fetch", 0), (5, 0), ZERO, [], [("make", 1, len(PARTS) - 1)], [], 0.2))
@@ -1046,7 +1043,7 @@
     return spots, peers
 
 
-def reduce_gradients(operands, starts=(ZERO, ZERO, 20.0, ZERO)):
+def reduce_gradients(operands, starts=(ZERO, ZERO, ZERO)):
     hbm = pl.BlockSpec(memory_space=pltpu.HBM)
     h_rows, m_rows, y_cols, z_cols, z_own, y_own, scale_parts = operands
     part, part_b = h_rows[0].shape[1] // SIDE, (m_rows[0].shape[0] + BAND) // 16

time: 251 us -> 248 us (0.988)
    pallas_call x1, Pallas kernels: 132 us -> 128 us  [run_layers(): pl.pallas_call(functools.partial(layers_kernel, layers_order(*w_in.shape[...]
where the time goes in v3:
time: 248 us; the launch traced here: 247 us
  Pallas kernels  237 us (96%)
  local copies, waits for them, and re-layouts  10.2 us (4%)
    pallas_call x1, Pallas kernels, run_layers(): pl.pallas_call(functools.partial(layers_kernel, layers_order(*w_in.shape[...  128 us
    pallas_call x1, Pallas kernels, reduce_gradients(): pl.pallas_call(functools.partial(reduce_kernel, reduce_order(part, part_b...  108 us
    slice x1, local copies, waits for them, and re-layouts, device_step(): in_grads = in_sums.reshape(n_layers, rows, -1)[:, :, :proj_dim]  5.44 us

profile of v3, /device:TPU:0, one launch (start us, length us, event | category | flops | bytes accessed | tf_op | source)
XLA Modules:
  0.0 247.3 jit_solution(12398964033468577069)
XLA Ops:
  0.6 128.1 %run_layers.1 = (bf16[256,768]{1,0:T(8,128)(2,1)}, bf16[256,768]{1,0:T(8,128)(2,1)}, bf16[4,96,2048]{2,1,0:T(8,128)(2,1)}, bf16[4,96,2048]{2,1,0:T(8,128)(2,1)},...) custom-call(bf16[2,96]{1,0:T(2,128)(2,1)} %sc_ref.1, ...), custom_call_target="tpu_custom_call" | custom-call | tf_op jit(solution)/shard_map/run_layers/pallas_call | solution.py:781
  128.8 108.4 %reduce_gradients.1 = (f32[2,4,24,7168]{3,2,1,0:T(8,128)}, f32[2,4,4,32,768]{4,3,2,1,0:T(8,128)}) custom-call(bf16[4,96,2048]{2,1,0:T(8,128)(2,1)} %get-tuple-element.23.refs_0_, bf16[4,96,2048]{2,1,0:T(8,128)(2,1)} %get-tuple-element.24.refs_1_, bf16[4,96,2048]{2,1,0:T(8,128)(2,1)} %get-tuple-element.25.refs_2_, ...), custom_call_target="tpu_custom_call" | custom-call | tf_op jit(solution)/shard_map/reduce_gradients/pallas_call | solution.py:1057
  237.2 0.8 slice.12
  238.0 0.6 constant_dynamic-slice_fusion
  238.6 0.0 copy-start
  238.6 5.4 %slice.13 = f32[2,96,7040]{2,1,0:T(8,128)} slice(f32[2,96,7168]{2,1,0:T(8,128)} %bitcast.7), slice={[0:2], [0:96], [0:7040]} | slice | bytes 10813440 | tf_op jit(solution)/shard_map/slice | solution.py:1091
  244.0 0.0 copy-done
  244.0 0.0 copy-start.2
  244.0 0.0 copy-start.1
  244.0 1.8 slice.14
  245.8 0.0 copy-done.2
  245.8 0.7 copy.13
  246.6 0.0 copy-done.1
  246.6 0.7 copy.14
Async XLA Ops:
  238.6 5.4 %copy-start = (f32[2,4,4,32,768]{4,3,2,1,0:T(8,128)S(1)}, f32[2,4,4,32,768]{4,3,2,1,0:T(8,128)}, u32[]{:S(2)}) copy-start(f32[2,4,4,32,768]{4,3,2,1,0:T(8,128)} %get-tuple-element.35) | copy-start | bytes 9437188
  244.0 1.8 copy-start.2
  244.0 2.5 %copy-start.1 = (bf16[256,768]{1,0:T(8,128)(2,1)S(1)}, bf16[256,768]{1,0:T(8,128)(2,1)}, u32[]{:S(2)}) copy-start(bf16[256,768]{1,0:T(8,128)(2,1)} %get-tuple-element.22) | copy-start | bytes 1179652

commit v4 on v3

--- a/solution.py
+++ b/solution.py
@@ -82,9 +82,9 @@
         order.append(name)
         now += cost
         landed[name] = []
-        for link, time in sends:
+        for link, time, *more in sends:
             free[link] = max(now, free.get(link, ZERO)) + time
-            landed[name].append(free[link] + latency)
+            landed[name].append(free[link] + latency + sum(more))
     return order
 
 
@@ -147,21 +147,21 @@
         tasks.append((name, rank, ZERO, needs, [], sends, 0.2))
 
     def both(axis, size):
-        return [((axis, by), size / rate) for by in BOTH]
-
-    model = rows_i * ROW
+        return [((axis, by), size / rate, margin) for by in BOTH]
+
+    model, margin = rows_i * ROW, 2.0
     for l in (1, 0):
         for axis in "yz":
             name = ("send_h", l, axis)
             send(name, 20 - l, 58.0, ("norm", l), both(axis, seq * model))
             for i, by in enumerate(BOTH):
                 for index in range(PAIR):
-                    follow(("pass_h", l, axis, by, index), 10, [(name, i)], [((axis, by), seq * model / SIDE / rate)])
+                    follow(("pass_h", l, axis, by, index), 10, [(name, i)], [((axis, by), seq * model / SIDE / rate, margin)])
         name = ("send_m", l)
         send(name, 22 - l, ZERO, ("mlp", l), both("x", seq * rows_o) + both("x", PAIR * seq * rows_o))
         for i, by in enumerate(BOTH):
             for index in range(PAIR):
-                follow(("pass_m", l, by, index), 11, [(name, i)], [(("x", by), seq * rows_o / PAIR / rate)])
+                follow(("pass_m", l, by, index), 11, [(name, i)], [(("x", by), seq * rows_o / PAIR / rate, margin)])
         if l == 0:
             send(("own_y",), 15, ZERO, ("back_norm", 1), [])
             send(("send_scale", l), 15, ZERO, ("back_norm", l), [])
@@ -169,7 +169,7 @@
         name = ("send_y", l)
         send(name, 12, 42.0, None, both("x", seq * model))
         for i, by in enumerate(BOTH):
-            follow(("pass_y", l, by), 12, [(name, i)], [(("x", by), seq * model / PAIR / rate)])
+            follow(("pass_y", l, by), 12, [(name, i)], [(("x", by), seq * model / PAIR / rate, margin)])
         follow(("far_y", l), 12, [(("pass_y", l, by), 0) for by in BOTH], [])
         for axis in "zy":
             name = ("send_z", l, axis)
@@ -179,7 +179,7 @@
                 name = ("rest_z", l)
                 send(name, 13, ZERO, ("back_keys", l), both(axis, share / ROW) + both(axis, share / SIDE))
             for i, by in enumerate(BOTH):
-                follow(("pass_z", l, axis, by), 13, [(name, i)], [((axis, by), share / PAIR / rate)])
+                follow(("pass_z", l, axis, by), 13, [(name, i)], [((axis, by), share / PAIR / rate, margin)])
                 follow(("twin_z", l, axis, by), 14, [(name, PAIR + i)], [])
             follow(("far_z", l, axis), 14, [(("pass_z", l, axis, by), 0) for by in BOTH], [])
         send(("send_scale", l), 15, ZERO, ("back_norm", l), [])
@@ -368,16 +368,19 @@
     def tokens(axis, o, index):
         return pl.ds(pl.multiple_of((PAIR * spot(axis, o) + index) * seq, seq), seq)
 
+    def place(axis, o, index):
+        return PAIR * spot(axis, o) + index
+
     def columns(axis, o):
         size = z.shape[PAIR] // ROW
         return lanes(((0 if axis == "y" else SIDE) + spot(axis, o)) * size, size)
 
     def several(batch, ref, n):
-        whole = ref.at[pl.ds(0, n * seq)] if batch[0][0] in "yz" else ref.at[(slice(None),) * (len(ref.shape) - 1) + (pl.ds(0, n * seq),)]
+        whole = ref.at[pl.ds(0, n * seq if batch[0][0] in "yz" else n)]
         return dict(batch=batch, whole=whole)
 
     def send_h(l, axis):
-        out = h_out[axis][l].at[:, :, tokens(axis, 0, core)]
+        out = h_out[axis][l].at[place(axis, 0, core)]
         for by in BOTH:
             for index in range(PAIR):
                 shared.send(("h", l, axis, by), ht.at[l, :, index], out, device(axis, by, index), lane=core, **several(("h", l, axis), h_out[axis][l], 7))
@@ -386,13 +389,13 @@
 
     def pass_h(l, axis, by, index):
         out = h_out[axis][l]
-        shared.arrive(("h", l, axis, by), out.at[:, :, tokens(axis, -by, index)], index)
-        part = out.at[pl.ds(1 - by, PAIR), :, tokens(axis, -by, index)]
+        shared.arrive(("h", l, axis, by), out.at[place(axis, -by, index)], index)
+        part = out.at[place(axis, -by, index), pl.ds(1 - by, PAIR)]
         shared.send(("h", l, axis), part, part, device(axis, by, core), **several(("h", l, axis), out, 7))
 
     def arrive_h(l):
         for axis in "yz":
-            shared.arrive(("h", l, axis), h_out[axis][l].at[:, :, pl.ds(0, 3 * seq)])
+            shared.arrive(("h", l, axis), h_out[axis][l].at[pl.ds(0, 3)])
 
     def row_block(l, o, index, part=None):
         size = omt.shape[1] // ROW
@@ -403,11 +406,11 @@
         return omt.at[l, pl.ds(pl.multiple_of(start, 16), size)]
 
     def row_half(k):
-        size = m_out[0].shape[0] // PAIR
+        size = m_out[0].shape[1] // PAIR
         return pl.ds(k * size, size)
 
     def send_m(l):
-        out = m_out[l].at[:, tokens("x", 0, core)]
+        out = m_out[l].at[place("x", 0, core)]
         for k, by in enumerate(BOTH):
             for index in range(PAIR):
                 shared.send(("mr", l, by), row_block(l, PAIR, index, k), relay_m.at[l, k, core], device("x", by, index), lane=core, **several(("m", l), m_out[l], 7))
@@ -420,11 +423,11 @@
     def pass_m(l, by, index):
         k = (1 - by) // PAIR
         shared.arrive(("mr", l, by), relay_m.at[l, k, index], index)
-        shared.send(("m", l), relay_m.at[l, k, index], m_out[l].at[row_half(k), tokens("x", -by, index)], device("x", by, core),
+        shared.send(("m", l), relay_m.at[l, k, index], m_out[l].at[place("x", -by, index), row_half(k)], device("x", by, core),
                     **several(("m2", l), m_out[l], PAIR))
 
     def arrive_m(l):
-        shared.arrive(("m", l), m_out[l].at[:, pl.ds(0, 7 * seq)])
+        shared.arrive(("m", l), m_out[l].at[pl.ds(0, 7)])
 
     def token_half(axis, o, k):
         return pl.ds(pl.multiple_of((PAIR * spot(axis, o) + core) * seq + k * (seq // PAIR), seq // PAIR), seq // PAIR)
@@ -780,7 +783,7 @@
     line = ROW * seq
     return pl.pallas_call(
         functools.partial(layers_kernel, layers_order(*w_in.shape[1:], *w_out.shape[1:], seq, starts)),
-        out_shape=(out(seq, dim), out(seq, dim), *[out(SIDE, dim // ROW, line)] * SIDE, *[out(cat // ROW, line)] * PAIR, out(line, dim),
+        out_shape=(out(seq, dim), out(seq, dim), *[out(ROW, SIDE, dim // ROW, seq)] * SIDE, *[out(ROW, cat // ROW, seq)] * PAIR, out(line, dim),
                    *[out(line, wide // ROW)] * PAIR, out(seq, wide), out(seq, dim), out(PAIR, ROW, ROW, dim, dtype=F32),
                    out(PAIR, PAIR, PAIR, cat // 16, seq), out(PAIR, PAIR, PAIR, seq // PAIR, wide // ROW)),
         in_specs=[vmem, hbm, hbm] + [vmem] * 3,
@@ -810,7 +813,7 @@
     tasks = []
     sizes = {"y": WIDE * 896 / (PAIR * rate), "z": WIDE * 896 / (PAIR * rate), "x": WIDE * 768 / (PAIR * rate)}
     for axis in "yzx":
-        tasks.append((("swap", axis), (0, 0), starts[PAIR] if axis == "x" else ZERO, [], [], [((axis, by), sizes[axis] * n) for by, n in ((1, 1), (-1, 1), (1, PAIR))], 0.3))
+        tasks.append((("swap", axis), (0, 0), starts[PAIR] if axis == "x" else starts[3], [], [], [((axis, by), sizes[axis] * n) for by, n in ((1, 1), (-1, 1), (1, PAIR))], 0.3))
         for i, o in enumerate(AROUND):
             tasks.append((("near", axis, o), (0, PAIR), ZERO, [(("swap", axis), i)], [], [("chip", 1.6)], 0.2))
     tasks.append((("fetch", 0), (5, 0), ZERO, [], [("make", 1, len(PARTS) - 1)], [], 0.2))
@@ -920,6 +923,9 @@
             loaded(("own", axis))
             links.arrive(("near", axis), target(axis).at[pl.ds(0, SIDE * seq)])
 
+    def joined_lanes(ref, l, i):
+        return jnp.concatenate([ref[l, i, k].reshape(-1, ref.shape[-1]) for k in range(ROW)], axis=1)
+
     def make(l, c):
         kind, first, then, last, at, width = PARTS[c]
         if kind == "i":
@@ -932,7 +938,7 @@
             size = total[c].shape[3]
             for lo in range(0, width, WIDE):
                 hi = min(width, lo + WIDE)
-                part = product(hbuf[l, i].reshape(-1, hbuf.shape[-1]), zbuf[l, i, :, at + lo:at + hi])
+                part = product(joined_lanes(hbuf, l, i), zbuf[l, i, :, at + lo:at + hi])
                 for r in range(16):
                     total[c][l, r // SIDE, r % SIDE, :, lo:hi] = part[r * size:(r + 1) * size]
             return
@@ -941,7 +947,7 @@
             loaded(("y", l))
         else:
             joined("x")
-        part = product(mbuf[l], ybuf[l, :, at:at + width])
+        part = product(jnp.concatenate([mbuf[l, k] for k in range(ROW)], axis=1), ybuf[l, :, at:at + width])
         size = total[c].shape[3]
 
         def put(r, value):
@@ -1043,10 +1049,10 @@
     return spots, peers
 
 
-def reduce_gradients(operands, starts=(ZERO, ZERO, ZERO)):
+def reduce_gradients(operands, starts=(ZERO, ZERO, ZERO, ZERO)):
     hbm = pl.BlockSpec(memory_space=pltpu.HBM)
     h_rows, m_rows, y_cols, z_cols, z_own, y_own, scale_parts = operands
-    part, part_b = h_rows[0].shape[1] // SIDE, (m_rows[0].shape[0] + BAND) // 16
+    part, part_b = h_rows[0].shape[PAIR] // SIDE, (m_rows[0].shape[1] + BAND) // 16
     (line, dim), wide = y_cols.shape, z_own.shape[1]
     out = lambda *shape: jax.ShapeDtypeStruct(shape, F32)
     sem = pltpu.SemaphoreType.DMA

time: 248 us -> 246 us (level)
  no operation moved by 1% of the time
where the time goes in v4:
time: 246 us
  Pallas kernels  235 us (96%)
  local copies, waits for them, and re-layouts  10.2 us (4%)
    pallas_call x1, Pallas kernels, run_layers(): pl.pallas_call(functools.partial(layers_kernel, layers_order(*w_in.shape[...  127 us
    pallas_call x1, Pallas kernels, reduce_gradients(): pl.pallas_call(functools.partial(reduce_kernel, reduce_order(part, part_b...  108 us
    slice x1, local copies, waits for them, and re-layouts, device_step(): in_grads = in_sums.reshape(n_layers, rows, -1)[:, :, :proj_dim]  5.44 us

profile of v4, /device:TPU:0, one launch (start us, length us, event | category | flops | bytes accessed | tf_op | source)
XLA Modules:
  0.0 246.1 jit_solution(14326441822599928544)
XLA Ops:
  0.6 127.3 %run_layers.1 = (bf16[256,768]{1,0:T(8,128)(2,1)}, bf16[256,768]{1,0:T(8,128)(2,1)}, bf16[8,4,96,256]{3,2,1,0:T(8,128)(2,1)}, bf16[8,4,96,256]{3,2,1,0:T(8,128)(...) custom-call(bf16[2,96]{1,0:T(2,128)(2,1)} %sc_ref.1, ...), custom_call_target="tpu_custom_call" | custom-call | tf_op jit(solution)/shard_map/run_layers/pallas_call | solution.py:784
  128.0 107.9 %reduce_gradients.1 = (f32[2,4,24,7168]{3,2,1,0:T(8,128)}, f32[2,4,4,32,768]{4,3,2,1,0:T(8,128)}) custom-call(bf16[8,4,96,256]{3,2,1,0:T(8,128)(2,1)} %get-tuple-element.23.refs_0_, bf16[8,4,96,256]{3,2,1,0:T(8,128)(2,1)} %get-tuple-element.24.refs_1_, bf16[8,4,96,256]{3,2,1,0:T(8,128)(2,1)} %get-tuple-element.25.refs_2_, ...), custom_call_target="tpu_custom_call" | custom-call | tf_op jit(solution)/shard_map/reduce_gradients/pallas_call | solution.py:1063
  235.9 0.8 slice.12
  236.7 0.6 constant_dynamic-slice_fusion
  237.3 0.0 copy-start
  237.3 5.4 %slice.13 = f32[2,96,7040]{2,1,0:T(8,128)} slice(f32[2,96,7168]{2,1,0:T(8,128)} %bitcast.7), slice={[0:2], [0:96], [0:7040]} | slice | bytes 10813440 | tf_op jit(solution)/shard_map/slice | solution.py:1097
  242.8 0.0 copy-done
  242.8 0.0 copy-start.2
  242.8 0.0 copy-start.1
  242.8 1.8 slice.14
  244.6 0.0 copy-done.2
  244.6 0.7 copy.13
  245.3 0.0 copy-done.1
  245.3 0.7 copy.14
Async XLA Ops:
  237.3 5.4 %copy-start = (f32[2,4,4,32,768]{4,3,2,1,0:T(8,128)S(1)}, f32[2,4,4,32,768]{4,3,2,1,0:T(8,128)}, u32[]{:S(2)}) copy-start(f32[2,4,4,32,768]{4,3,2,1,0:T(8,128)} %get-tuple-element.35) | copy-start | bytes 9437188
  242.8 1.8 copy-start.2
  242.8 2.5 %copy-start.1 = (bf16[256,768]{1,0:T(8,128)(2,1)S(1)}, bf16[256,768]{1,0:T(8,128)(2,1)}, u32[]{:S(2)}) copy-start(bf16[256,768]{1,0:T(8,128)(2,1)} %get-tuple-element.22) | copy-start | bytes 1179652

commit v5 on v4

--- a/solution.py
+++ b/solution.py
@@ -12,8 +12,10 @@
 AROUND = (1, -1, 2)
 PARTS = (True, False)
 ALL, ZERO = ..., 0.0
+OTHERS = 7
+QUICK, SHORT = 0.2, 0.3
 LANE, WIDE, STRIP, HEAD = 128, 256, 512, 64
-ROW, BAND, SIDE, PAIR = 8, 32, 4, 2
+ROW, BAND, SIDE, TRIO, PAIR = 8, 32, 4, 3, 2
 
 
 class Links:
@@ -101,23 +103,23 @@
             cost = size[color] / rate
             both = [(("x", by), cost) for by in BOTH]
             spread = [((color, by), cost) for by in BOTH] if color != "x" else []
-            tasks.append((("reach", m, color), m, starts[m], [], [], both, 0.2))
+            tasks.append((("reach", m, color), m, starts[m], [], [], both, QUICK))
             for i, by in enumerate(BOTH):
-                tasks.append((("relay", m, color, by), m, ZERO, [(("reach", m, color), i)], [], [(("x", by), cost / PAIR)] + spread, 0.2))
+                tasks.append((("relay", m, color, by), m, ZERO, [(("reach", m, color), i)], [], [(("x", by), cost / PAIR)] + spread, QUICK))
             halves = [(("relay", m, color, by), 0) for by in BOTH]
-            tasks.append((("far", m, color), m, ZERO, halves, [], spread, 0.2))
+            tasks.append((("far", m, color), m, ZERO, halves, [], spread, QUICK))
             if color == "x":
                 continue
             for off, source, first in ((-1, ("relay", m, color, 1), 1), (1, ("relay", m, color, -1), 1), (PAIR, ("far", m, color), 0)):
                 for i, by in enumerate(BOTH):
-                    tasks.append((("pass", m, color, off, by), m, ZERO, [(source, first + i)], [], [((color, by), cost / PAIR)], 0.2))
+                    tasks.append((("pass", m, color, off, by), m, ZERO, [(source, first + i)], [], [((color, by), cost / PAIR)], QUICK))
                 halves = [(("pass", m, color, off, by), 0) for by in BOTH]
-                tasks.append((("close", m, color, off), m, ZERO, halves, [], [], 0.2))
+                tasks.append((("close", m, color, off), m, ZERO, halves, [], [], QUICK))
         for off in (-1, 1, PAIR):
             last = [("close", m, color, off) for color in "yz"]
             if is_in:
                 last.append(("far", m, "x") if off == PAIR else ("relay", m, "x", -off))
-            tasks.append((("hand", m, off), m, ZERO, [], last, [("chip", (rows_i * cols_i if is_in else rows_o * cols_o) / 150000.0)], 0.2))
+            tasks.append((("hand", m, off), m, ZERO, [], last, [("chip", (rows_i * cols_i if is_in else rows_o * cols_o) / 150000.0)], QUICK))
     before = []
 
     def work(name, cost, mats=()):
@@ -136,7 +138,7 @@
         work(("back_mlp", l), 2.0)
         work(("back_heads", l), 1.0)
         work(("back_quad", l), 6.0)
-        work(("back_keys", l), 0.2)
+        work(("back_keys", l), QUICK)
         for i in range(PAIR):
             work(("back_in", l, i), 1.3 + 0.6 * i)
         work(("back_norm", l), 1.0)
@@ -144,7 +146,7 @@
         tasks.append((name, rank, start, [], [after] if after else [], sends, 0.4))
 
     def follow(name, rank, needs, sends):
-        tasks.append((name, rank, ZERO, needs, [], sends, 0.2))
+        tasks.append((name, rank, ZERO, needs, [], sends, QUICK))
 
     def both(axis, size):
         return [((axis, by), size / rate, margin) for by in BOTH]
@@ -184,6 +186,7 @@
             follow(("far_z", l, axis), 14, [(("pass_z", l, axis, by), 0) for by in BOTH], [])
         send(("send_scale", l), 15, ZERO, ("back_norm", l), [])
     send(("own_z",), 15, ZERO, ("back_keys", 0), [])
+    send(("late_z",), 14, ZERO, ("back_mlp", 0), [])
     return plan(tasks)
 
 
@@ -243,7 +246,7 @@
     def group(m, color):
         _, out, _, is_in = mats[m]
         (_, nr), (c, nc) = region(is_in, color, 0)[0]
-        return dict(batch=(m, color), whole=out.at[pl.ds(0, nr * (3 if color == "x" else 12)), pl.ds(c, nc)])
+        return dict(batch=(m, color), whole=out.at[pl.ds(0, nr * (TRIO if color == "x" else 12)), pl.ds(c, nc)])
 
     def reach(m, color):
         src, _, _, is_in = mats[m]
@@ -252,13 +255,13 @@
             links.send((m, "x1", color, by), src.at[pl.ds(pl.multiple_of(area[0][0], ROW), area[0][1]), pl.ds(*area[1])], at(m, x, area), peer("x", by), **group(m, color))
 
     def launch(m, color, off):
-        is_in = mats[m][3]
+        is_in = mats[m][TRIO]
         moved = at(m, spot("x", off), region(is_in, color, place[color])[0])
         for by in BOTH:
             links.send((m, "p1", color, off, by), moved, moved, peer(color, by), **group(m, color))
 
     def relay(m, color, by):
-        is_in = mats[m][3]
+        is_in = mats[m][TRIO]
         xb = spot("x", -by)
         areas = region(is_in, color, place[color])
         links.arrive((m, "x1", color, by), at(m, xb, areas[0]))
@@ -268,13 +271,13 @@
             launch(m, color, -by)
 
     def far(m, color):
-        is_in = mats[m][3]
+        is_in = mats[m][TRIO]
         links.arrive((m, "x2", color), at(m, spot("x", PAIR), region(is_in, color, place[color])[0]))
         if color != "x":
             launch(m, color, PAIR)
 
     def pass_on(m, color, off, by):
-        is_in = mats[m][3]
+        is_in = mats[m][TRIO]
         xb = spot("x", off)
         areas = region(is_in, color, spot(color, -by))
         links.arrive((m, "p1", color, off, by), at(m, xb, areas[0]))
@@ -282,7 +285,7 @@
         links.send((m, "p2", color, off), part, part, peer(color, by), **group(m, color))
 
     def close(m, color, off):
-        is_in = mats[m][3]
+        is_in = mats[m][TRIO]
         links.arrive((m, "p2", color, off), at(m, spot("x", off), region(is_in, color, spot(color, PAIR))[0]))
 
     def four(m):
@@ -324,7 +327,7 @@
 
 
 def layers_kernel(order, sc_ref, wi_ref, wo_ref, x_ref, dy_ref, freq_ref,
-                  y_ref, gx_ref, hy_a, hy_b, hz_a, hz_b, mx_a, mx_b, yx_b, zy_b, zz_b, z_a, dy_a, sc_out, relay_m, relay_z,
+                  y_ref, gx_ref, hy_a, hy_b, hz_a, hz_b, mx_a, mx_b, yx_b, zy_b, zz_b, zy_a, zz_a, z_a, dy_a, sc_out, relay_m, relay_z,
                   wi, wo, z, om, h, hid, qr, kts, vsl, ksl, turned_q, turned_o, scores, dscores, pcat, dscat, cos_ref, sin_ref, turn_ref,
                   dot_heads, qt, dht, dkv, omt, ht, dyt, sc, gains, own_gain, gain_ref, load_sems, own_sems, send_sems, recv_sems,
                   share_send_sems, share_recv_sems):
@@ -358,7 +361,7 @@
     announce(others + [device(axis, o, index) for axis in "yz" for o in AROUND for index in range(PAIR)])
     begin()
     for k, far in enumerate(others):
-        links.send(("sc",), own_gain, gains.at[me], far, batch=("sc",), whole=gains.at[pl.ds(0, 7)])
+        links.send(("sc",), own_gain, gains.at[me], far, batch=("sc",), whole=gains.at[pl.ds(0, OTHERS)])
 
     def keep(src, dst):
         copy = pltpu.make_async_copy(src, dst, own_sems.at[len(stored)])
@@ -383,19 +386,19 @@
         out = h_out[axis][l].at[place(axis, 0, core)]
         for by in BOTH:
             for index in range(PAIR):
-                shared.send(("h", l, axis, by), ht.at[l, :, index], out, device(axis, by, index), lane=core, **several(("h", l, axis), h_out[axis][l], 7))
-        shared.send(("h", l, axis), ht.at[l, :, 1 - core], out, twin, **several(("h", l, axis), h_out[axis][l], 7))
+                shared.send(("h", l, axis, by), ht.at[l, :, index], out, device(axis, by, index), lane=core, **several(("h", l, axis), h_out[axis][l], OTHERS))
+        shared.send(("h", l, axis), ht.at[l, :, 1 - core], out, twin, **several(("h", l, axis), h_out[axis][l], OTHERS))
         keep(ht.at[l, :, core], out)
 
     def pass_h(l, axis, by, index):
         out = h_out[axis][l]
         shared.arrive(("h", l, axis, by), out.at[place(axis, -by, index)], index)
         part = out.at[place(axis, -by, index), pl.ds(1 - by, PAIR)]
-        shared.send(("h", l, axis), part, part, device(axis, by, core), **several(("h", l, axis), out, 7))
+        shared.send(("h", l, axis), part, part, device(axis, by, core), **several(("h", l, axis), out, OTHERS))
 
     def arrive_h(l):
         for axis in "yz":
-            shared.arrive(("h", l, axis), h_out[axis][l].at[pl.ds(0, 3)])
+            shared.arrive(("h", l, axis), h_out[axis][l].at[pl.ds(0, TRIO)])
 
     def row_block(l, o, index, part=None):
         size = omt.shape[1] // ROW
@@ -413,11 +416,11 @@
         out = m_out[l].at[place("x", 0, core)]
         for k, by in enumerate(BOTH):
             for index in range(PAIR):
-                shared.send(("mr", l, by), row_block(l, PAIR, index, k), relay_m.at[l, k, core], device("x", by, index), lane=core, **several(("m", l), m_out[l], 7))
+                shared.send(("mr", l, by), row_block(l, PAIR, index, k), relay_m.at[l, k, core], device("x", by, index), lane=core, **several(("m", l), m_out[l], OTHERS))
         for by in BOTH:
             for index in range(PAIR):
-                shared.send(("m", l), row_block(l, by, index), out, device("x", by, index), **several(("m", l), m_out[l], 7))
-        shared.send(("m", l), row_block(l, 0, 1 - core), out, twin, **several(("m", l), m_out[l], 7))
+                shared.send(("m", l), row_block(l, by, index), out, device("x", by, index), **several(("m", l), m_out[l], OTHERS))
+        shared.send(("m", l), row_block(l, 0, 1 - core), out, twin, **several(("m", l), m_out[l], OTHERS))
         keep(row_block(l, 0, core), out)
 
     def pass_m(l, by, index):
@@ -427,7 +430,7 @@
                     **several(("m2", l), m_out[l], PAIR))
 
     def arrive_m(l):
-        shared.arrive(("m", l), m_out[l].at[pl.ds(0, 7)])
+        shared.arrive(("m", l), m_out[l].at[pl.ds(0, OTHERS)])
 
     def token_half(axis, o, k):
         return pl.ds(pl.multiple_of((PAIR * spot(axis, o) + core) * seq + k * (seq // PAIR), seq // PAIR), seq // PAIR)
@@ -435,20 +438,20 @@
     def send_y(l):
         src, out = dy_ref, y_out[l].at[tokens("x", 0, core)]
         for by in BOTH:
-            shared.send(("y", l, by), src, out, device("x", by, core), **several(("y", l), y_out[l], 7))
-        shared.send(("y", l), src, out, twin, **several(("y", l), y_out[l], 7))
+            shared.send(("y", l, by), src, out, device("x", by, core), **several(("y", l), y_out[l], OTHERS))
+        shared.send(("y", l), src, out, twin, **several(("y", l), y_out[l], OTHERS))
         keep(src, out)
 
     def pass_y(l, by):
         landed, part = y_out[l].at[tokens("x", -by, core)], y_out[l].at[token_half("x", -by, (1 - by) // PAIR)]
         shared.arrive(("y", l, by), landed)
-        shared.send(("y2", l), part, part, device("x", by, core), **several(("y", l), y_out[l], 7))
-        shared.send(("y", l), landed, landed, twin, **several(("y", l), y_out[l], 7))
+        shared.send(("y2", l), part, part, device("x", by, core), **several(("y", l), y_out[l], OTHERS))
+        shared.send(("y", l), landed, landed, twin, **several(("y", l), y_out[l], OTHERS))
 
     def far_y(l):
         landed = y_out[l].at[tokens("x", PAIR, core)]
         shared.arrive(("y2", l), landed)
-        shared.send(("y", l), landed, landed, twin, **several(("y", l), y_out[l], 7))
+        shared.send(("y", l), landed, landed, twin, **several(("y", l), y_out[l], OTHERS))
 
     def arrive_y(l):
         shared.arrive(("y", l), y_out[l].at[pl.ds(0, SIDE * seq)])
@@ -481,6 +484,35 @@
         if axis == "z":
             own_part(l, axis)
 
+    def late_z():
+        for axis, out in (("z", zz_a), ("y", zy_a)):
+            for o in AROUND:
+                def start():
+                    shared.send(("late", axis), z.at[0, :, columns(axis, o)], out.at[tokens(axis, 0, core)], device(axis, o, core),
+                                batch=("late", axis), whole=out.at[pl.ds(0, TRIO * seq)])
+
+                if axis == "y":
+                    pl.when(spot("y", o) != 0)(start)
+                else:
+                    start()
+
+    def settle_late():
+        shared.arrive(("late", "z"), zz_a.at[pl.ds(0, TRIO * seq)])
+        _, leaving = shared.sent.pop(("late", "y"))
+
+        def left(n):
+            part = zy_a.at[pl.ds(0, n * seq)]
+            pltpu.make_async_copy(part, part, share_send_sems.at[leaving]).wait()
+
+        @pl.when(y == 0)
+        def _():
+            left(TRIO)
+
+        @pl.when(y != 0)
+        def _():
+            left(PAIR)
+            shared.arrive(("late", "y"), zy_a.at[pl.ds(0, TRIO * seq)])
+
     def rest_z(l):
         for o in (PAIR, 1, -1):
             push_z(l, "y", o, spot("y", o) == 0)
@@ -507,11 +539,11 @@
 
     def send_scale(l):
         for far in others:
-            shared.send(("scale", l), sc.at[l], sc_out.at[l, me], far, batch=("scale", l), whole=sc_out.at[l, pl.ds(0, 7)])
+            shared.send(("scale", l), sc.at[l], sc_out.at[l, me], far, batch=("scale", l), whole=sc_out.at[l, pl.ds(0, OTHERS)])
         keep(sc.at[l], sc_out.at[l, me])
 
     def arrive_scale(l):
-        shared.arrive(("scale", l), sc_out.at[l, pl.ds(0, 7)])
+        shared.arrive(("scale", l), sc_out.at[l, pl.ds(0, OTHERS)])
 
     gains[me] = own_gain[ALL]
     z[:, :, wi.shape[PAIR]:] = jnp.zeros((PAIR, seq, z.shape[PAIR] - wi.shape[PAIR]), BF)
@@ -702,7 +734,7 @@
 
     def back_in(l, half):
         width = wi.shape[PAIR] // 5
-        at = slice(PAIR * half * width, (PAIR + 3 * half) * width)
+        at = slice(PAIR * half * width, (PAIR + TRIO * half) * width)
         part = product(wi[l, :, at], z[l, :, at], ((1,), (1,)))
         dht[ALL] = dht[ALL] + part if half else part
 
@@ -722,19 +754,19 @@
             hat = v * scale
             d = h[l, rows].astype(F32)
             each = (d * hat).reshape(SIDE, ROW, dim)
-            sc[l] += (each[0] + each[1]) + (each[PAIR] + each[3])
+            sc[l] += (each[0] + each[1]) + (each[PAIR] + each[TRIO])
             d = d * gain_ref[l:l + 1]
             d = scale * (d - jnp.mean(d, axis=-1, keepdims=True) - hat * jnp.mean(d * hat, axis=-1, keepdims=True))
             dst[rows] = (dy[rows].astype(F32) + d.astype(BF).astype(F32)).astype(BF)
 
     def do_norm(l):
         if l == 0:
-            links.arrive(("sc",), gains.at[pl.ds(0, 7)])
+            links.arrive(("sc",), gains.at[pl.ds(0, OTHERS)])
             gain_ref[ALL] = jnp.sum(gains[ALL], axis=0)
         normalise(l, entry[l])
         for i in range(dim // WIDE):
             flat = h[l, :, i * WIDE:(i + 1) * WIDE].T
-            size = ht.shape[3]
+            size = ht.shape[TRIO]
             for b in range(ROW):
                 lo, hi = max(b * size, i * WIDE), min((b + 1) * size, (i + 1) * WIDE)
                 if lo < hi:
@@ -755,7 +787,7 @@
     stages.update(
         norm=do_norm, project=do_project, attend=attend, mlp=do_mlp, put=do_put, back_out=back_out, back_mlp=back_mlp, back_heads=back_heads,
         back_quad=back_quad, back_keys=back_keys, back_in=back_in, back_norm=back_norm, send_h=send_h, pass_h=pass_h, send_m=send_m,
-        pass_m=pass_m, send_y=send_y, pass_y=pass_y, far_y=far_y, send_z=send_z, rest_z=rest_z, pass_z=pass_z, twin_z=twin_z, far_z=far_z,
+        pass_m=pass_m, send_y=send_y, pass_y=pass_y, far_y=far_y, send_z=send_z, rest_z=rest_z, late_z=late_z, pass_z=pass_z, twin_z=twin_z, far_z=far_z,
         send_scale=send_scale, own_z=lambda: keep(z.at[0], z_a), own_y=lambda: keep(middle, dy_a))
     for kind, *task in order:
         stages[kind](*task)
@@ -766,6 +798,7 @@
     arrive_y(1)
     for l, axis in z_out:
         arrive_z(l, axis)
+    settle_late()
     for copy in stored:
         copy.wait()
     shared.drain()
@@ -784,10 +817,10 @@
     return pl.pallas_call(
         functools.partial(layers_kernel, layers_order(*w_in.shape[1:], *w_out.shape[1:], seq, starts)),
         out_shape=(out(seq, dim), out(seq, dim), *[out(ROW, SIDE, dim // ROW, seq)] * SIDE, *[out(ROW, cat // ROW, seq)] * PAIR, out(line, dim),
-                   *[out(line, wide // ROW)] * PAIR, out(seq, wide), out(seq, dim), out(PAIR, ROW, ROW, dim, dtype=F32),
+                   *[out(line, wide // ROW)] * SIDE, out(seq, wide), out(seq, dim), out(PAIR, ROW, ROW, dim, dtype=F32),
                    out(PAIR, PAIR, PAIR, cat // 16, seq), out(PAIR, PAIR, PAIR, seq // PAIR, wide // ROW)),
-        in_specs=[vmem, hbm, hbm] + [vmem] * 3,
-        out_specs=[vmem] * PAIR + [hbm] * 14,
+        in_specs=[vmem, hbm, hbm] + [vmem] * TRIO,
+        out_specs=[vmem] * PAIR + [hbm] * 16,
         scratch_shapes=[
             buffer(PAIR, dim, proj), buffer(PAIR, cat, dim), buffer(PAIR, seq, wide), buffer(seq, cat), buffer(PAIR, seq, dim),
             buffer(PAIR, seq, dim), buffer(PAIR, seq, dim),
@@ -797,7 +830,7 @@
             buffer(dim, seq), buffer(dim, seq), buffer(dim, seq, dtype=F32), buffer(PAIR, seq, LANE, dtype=F32),
             buffer(PAIR, cat, seq), buffer(PAIR, SIDE, PAIR, dim // ROW, seq), buffer(dim, seq), buffer(PAIR, ROW, dim, dtype=F32),
             buffer(ROW, ROW, dim, dtype=F32), buffer(ROW, dim, dtype=F32), buffer(ROW, dim, dtype=F32),
-            sem((SIDE,)), sem((13,)), sem((15,)), sem((107,)), sem((13,)), sem((HEAD,)),
+            sem((SIDE,)), sem((13,)), sem((15,)), sem((107,)), sem((15,)), sem((HEAD,)),
         ],
         compiler_params=pltpu.CompilerParams(collective_id=PAIR, has_side_effects=True, vmem_limit_bytes=67043328),
         name="run_layers",
@@ -812,17 +845,20 @@
     rate = 11650.0
     tasks = []
     sizes = {"y": WIDE * 896 / (PAIR * rate), "z": WIDE * 896 / (PAIR * rate), "x": WIDE * 768 / (PAIR * rate)}
-    for axis in "yzx":
-        tasks.append((("swap", axis), (0, 0), starts[PAIR] if axis == "x" else starts[3], [], [], [((axis, by), sizes[axis] * n) for by, n in ((1, 1), (-1, 1), (1, PAIR))], 0.3))
+    tasks.append((("swap", "x"), (0, 0), starts[PAIR], [], [], [(("x", by), sizes["x"] * n) for by, n in ((1, 1), (-1, 1), (1, PAIR))], SHORT))
+    tasks.append((("swap", "z"), (0, 0), starts[TRIO], [], [], [("chip", 1.6)] * SIDE, 0.4))
+    tasks.append((("swap", "y"), (0, 0), starts[TRIO], [], [], [(("y", by), sizes["y"] * n / PAIR) for by, n in ((1, 1), (-1, 1), (1, PAIR))] + [("chip", 1.6)] * SIDE, 0.4))
+    for axis in "yx":
         for i, o in enumerate(AROUND):
-            tasks.append((("near", axis, o), (0, PAIR), ZERO, [(("swap", axis), i)], [], [("chip", 1.6)], 0.2))
-    tasks.append((("fetch", 0), (5, 0), ZERO, [], [("make", 1, len(PARTS) - 1)], [], 0.2))
+            tasks.append((("near", axis, o), (0, PAIR), ZERO, [(("swap", axis), i)], [], [("chip", 1.6)], QUICK))
+    tasks.append((("fetch", 0), (5, 0), ZERO, [], [("make", 1, len(PARTS) - 1)], [], QUICK))
     for l in (1, 0):
         late = 1 - l
         for c, (kind, first, then, last, at, width) in enumerate(PARTS):
             needs, cost = [], 1.6 * width / STRIP
             if l == 0:
-                needs = [(("near", last if kind == "i" else "x", o), 0) for o in AROUND]
+                needs = [(("swap", "z"), k) for k in range(SIDE)] if (kind, last) == ("i", "z") else [
+                    (("near", last if kind == "i" else "x", o), 0) for o in AROUND]
             tasks.append((("make", l, c), (9 * late, c), starts[late], needs, [] if l else [("fetch", 0)], [], cost))
             full = SIDE * SIDE * (rows if kind == "i" else rows_b) * width / rate
             sends = [[((first, by), full / ROW) for by in BOTH], [((first, by), full / SIDE) for by in BOTH],
@@ -833,17 +869,17 @@
             for s in range(9):
                 task = ("sum", l, c, s)
                 needs = [(("sum", l, c, s - 1), k) for k in range(len(sends[s - 1]))] if s else []
-                tasks.append((task, (late, -s), ZERO, needs, [("make", l, c)] if s == 0 else [("sum", l, c, s - 1)], sends[s], 0.3))
+                tasks.append((task, (late, -s), ZERO, needs, [("make", l, c)] if s == 0 else [("sum", l, c, s - 1)], sends[s], SHORT))
     return plan(tasks)
 
 
 def reduce_kernel(order, *refs):
     hy, hz, mx = refs[0:PAIR], refs[PAIR:SIDE], refs[SIDE:6]
-    yx1, zy1, zz1, z0, y0, sc = refs[6:12]
-    oa, ob = refs[12:14]
+    yx1, zy1, zz1, zy0, zz0, z0, y0, sc = refs[6:14]
+    oa, ob = refs[14:16]
     n = len(PARTS)
-    total, half, full, small, front = (refs[14 + k * n:14 + (k + 1) * n] for k in range(5))
-    (hbuf, zbuf, mbuf, ybuf, scbuf, ssem, rsem, isem, osem) = refs[14 + 5 * n:]
+    total, half, full, small, front = (refs[16 + k * n:16 + (k + 1) * n] for k in range(5))
+    (hbuf, zbuf, mbuf, ybuf, scbuf, ssem, rsem, isem, osem, fsem) = refs[16 + 5 * n:]
     position = chip_position()
     x, y, zc, core = position
     place = {"x": x, "y": y, "z": zc}
@@ -899,28 +935,66 @@
     def target(axis):
         return ybuf.at[0] if axis == "x" else zbuf.at[0, "yz".index(axis)]
 
-    def seven(axis):
-        return dict(batch=("swap", axis), whole=target(axis).at[pl.ds(0, 7 * seq)])
+    def seven(axis, n):
+        return dict(batch=("swap", axis), whole=target(axis).at[pl.ds(0, n * seq)])
+
+    batches = {axis: seven(axis, OTHERS if axis == "x" else SIDE) for axis in "xyz"}
+
+    def to_twin(axis, src, o):
+        near_core = device_at(x, y, zc, 1 - core)
+        links.send(("near", axis), src, target(axis).at[tokens(axis, -o, core)], near_core, **batches[axis])
 
     def swap(axis):
         def part(o):
             return y0 if axis == "x" else z0.at[:, columns(axis, o)]
 
         mine = target(axis).at[tokens(axis, 0, core)]
-        for o in AROUND:
-            links.send(("swap", axis, o), part(o), mine, peer(axis, o), **seven(axis))
-        links.send(("near", axis), part(0), mine, twin, **seven(axis))
+        if axis == "x":
+            for o in AROUND:
+                links.send(("swap", axis, o), y0, mine, peer(axis, o), **batches[axis])
+        elif axis == "y":
+            for o in AROUND:
+                @pl.when(spot("y", o) == 0)
+                def _():
+                    links.send(("swap", axis, o), part(o), mine, device_at(x, spot("y", o), zc, core), batch=("first",), whole=mine)
+        to_twin(axis, part(0), 0)
         load(("own", axis), part(0), mine)
+        if axis == "z":
+            for o in AROUND:
+                landed = zz0.at[tokens(axis, -o, core)]
+                to_twin(axis, landed, o)
+                load(("far", axis, o), landed, target(axis).at[tokens(axis, -o, core)])
+        if axis == "y":
+            @pl.when(y != 0)
+            def _():
+                for k, o in enumerate(AROUND):
+                    landed = zy0.at[tokens(axis, -o, core)]
+                    to_twin(axis, landed, o)
+                    pltpu.make_async_copy(landed, target(axis).at[tokens(axis, -o, core)], fsem.at[k]).start()
 
     def near(axis, o):
-        landed = target(axis).at[tokens(axis, -o, core)]
-        links.arrive(("swap", axis, o), landed)
-        links.send(("near", axis), landed, landed, twin, **seven(axis))
+        def go():
+            landed = target(axis).at[tokens(axis, -o, core)]
+            links.arrive(("swap", axis, o), landed)
+            to_twin(axis, landed, o)
+
+        if axis == "x":
+            go()
+        else:
+            pl.when(y == 0)(go)
 
     def joined(axis):
         if axis not in done:
             done.add(axis)
             loaded(("own", axis))
+            if axis == "z":
+                loaded(*[("far", axis, o) for o in AROUND])
+            if axis == "y":
+                @pl.when(y != 0)
+                def _():
+                    for k, o in enumerate(AROUND):
+                        landed = target(axis).at[tokens(axis, -o, core)]
+                        pltpu.make_async_copy(landed, landed, fsem.at[k]).wait()
             links.arrive(("near", axis), target(axis).at[pl.ds(0, SIDE * seq)])
 
     def joined_lanes(ref, l, i):
@@ -935,7 +1009,7 @@
                 loaded(("z", l, last))
             else:
                 joined(last)
-            size = total[c].shape[3]
+            size = total[c].shape[TRIO]
             for lo in range(0, width, WIDE):
                 hi = min(width, lo + WIDE)
                 part = product(joined_lanes(hbuf, l, i), zbuf[l, i, :, at + lo:at + hi])
@@ -948,7 +1022,7 @@
         else:
             joined("x")
         part = product(jnp.concatenate([mbuf[l, k] for k in range(ROW)], axis=1), ybuf[l, :, at:at + width])
-        size = total[c].shape[3]
+        size = total[c].shape[TRIO]
 
         def put(r, value):
             total[c][(l, r // SIDE, r % SIDE) if first == "y" else (l, r % SIDE, r // SIDE)] = value
@@ -974,7 +1048,7 @@
         t = total[c].at[l]
         way = 1 - PAIR * (c % PAIR)
         sums = dict(batch=(l, c, 0), whole=t)
-        wide_ones = dict(batch=(l, c, 1), whole=t.at[pl.ds(0, 3)])
+        wide_ones = dict(batch=(l, c, 1), whole=t.at[pl.ds(0, TRIO)])
         narrow = dict(batch=(l, c, PAIR), whole=t.at[0, pl.ds(0, PAIR)])
         if s == 0:
             far = t.at[spot(first, PAIR)]
@@ -993,7 +1067,7 @@
                 add_into(mine, full[c].at[l, k])
             for k, o in enumerate(AROUND):
                 links.send((l, c, "small"), mine.at[spot(then, o)], small[c].at[l, k], peer(then, o), **wide_ones)
-        elif s == 3:
+        elif s == TRIO:
             links.arrive((l, c, "small"), small[c].at[l])
             mine = t.at[spot(first, 0), spot(then, 0)]
             front[c][l] = (mine[ALL] + small[c][l, 0]) + (small[c][l, 1] + small[c][l, PAIR])
@@ -1014,7 +1088,7 @@
             line = area(l, c, 0, slice(None))
             for by in BOTH:
                 links.send((l, c, "a2"), line, line, peer(last, by), **wide_ones)
-        elif s == 7:
+        elif s == OTHERS:
             links.arrive((l, c, "a2"), t.at[pl.ds(0, PAIR)])
             for k, by in enumerate(BOTH):
                 part = area(l, c, -by, pl.ds(PAIR * k, PAIR))
@@ -1025,6 +1099,13 @@
     stages = {"swap": swap, "near": near, "fetch": fetch, "make": make, "sum": add}
     for kind, *task in order:
         stages[kind](*task)
+    _, leaving = links.sent.pop(("first",))
+
+    @pl.when(y != 0)
+    def _():
+        mine = target("y").at[tokens("y", 0, core)]
+        pltpu.make_async_copy(mine, mine, ssem.at[leaving]).wait()
+
     links.drain()
 
 
@@ -1039,7 +1120,7 @@
 
 
 def around(position):
-    place, core = dict(zip("xyz", position)), position[3]
+    place, core = dict(zip("xyz", position)), position[TRIO]
     spots = {(axis, o): step(place[axis], o) for axis in "xyz" for o in range(SIDE)}
     peers = {}
     for axis in "xyz":
@@ -1049,7 +1130,7 @@
     return spots, peers
 
 
-def reduce_gradients(operands, starts=(ZERO, ZERO, ZERO, ZERO)):
+def reduce_gradients(operands, starts=(ZERO, ZERO, 8.0, ZERO)):
     hbm = pl.BlockSpec(memory_space=pltpu.HBM)
     h_rows, m_rows, y_cols, z_cols, z_own, y_own, scale_parts = operands
     part, part_b = h_rows[0].shape[PAIR] // SIDE, (m_rows[0].shape[1] + BAND) // 16
@@ -1063,13 +1144,13 @@
     return pl.pallas_call(
         functools.partial(reduce_kernel, reduce_order(part, part_b, starts)),
         out_shape=(out(PAIR, SIDE, part, wide), out(PAIR, SIDE, SIDE, part_b, dim)),
-        in_specs=[hbm] * 12,
+        in_specs=[hbm] * 14,
         out_specs=[hbm] * PAIR,
         scratch_shapes=[
-            *buffers(SIDE, SIDE), *buffers(PAIR, PAIR), *buffers(PAIR, SIDE), *buffers(3), *buffers(),
+            *buffers(SIDE, SIDE), *buffers(PAIR, PAIR), *buffers(PAIR, SIDE), *buffers(TRIO), *buffers(),
             pltpu.VMEM((PAIR, PAIR, *h_rows[0].shape), BF), pltpu.VMEM((PAIR, PAIR, line, wide // ROW), BF), pltpu.VMEM((PAIR, *m_rows[0].shape), BF),
             pltpu.VMEM((PAIR, line, dim), BF), pltpu.VMEM(scale_parts.shape, F32),
-            sem((39,)), sem((96,)), sem((14,)), sem((PAIR, len(PARTS))),
+            sem((40,)), sem((96,)), sem((17,)), sem((PAIR, len(PARTS))), sem((TRIO,)),
         ],
         compiler_params=pltpu.CompilerParams(collective_id=1, has_side_effects=True, vmem_limit_bytes=67043328),
         name="reduce_gradients",
@@ -1093,7 +1174,7 @@
         freq = 10000.0 ** (-np.arange(half_dim, dtype=np.float32) * 2.0 / head_dim)
         freq = jnp.asarray(np.tile(freq.astype(np.float32), (ROW, LANE // half_dim)))
         hidden, grad_hidden, *rest = run_layers(x_in[0], grad_y[0], norm_scale, w_in, w_out, freq)
-        in_sums, out_sums = reduce_gradients((rest[0:SIDE], rest[SIDE:6], rest[6], rest[7:9], rest[9], rest[10], rest[11]))
+        in_sums, out_sums = reduce_gradients((rest[0:SIDE], rest[SIDE:6], rest[6], rest[OTHERS:11], rest[11], rest[12], rest[13]))
         in_grads = in_sums.reshape(n_layers, rows, -1)[:, :, :proj_dim]
         out_rows = out_sums.reshape(n_layers, -1, model_dim)
         scale_grads = lax.dynamic_slice(out_rows[:, rows_out], (0, lax.axis_index("fsdp") * rows), (n_layers, rows))

time: 246 us -> 279 us (1.13)
  Pallas kernels: 235 us -> 268 us
    pallas_call x1, Pallas kernels: 108 us -> 130 us  [reduce_gradients(): pl.pallas_call(functools.partial(reduce_kernel, reduce_order(part, part_b...]
    pallas_call x1, Pallas kernels: 127 us -> 137 us  [run_layers(): pl.pallas_call(functools.partial(layers_kernel, layers_order(*w_in.shape[...]
where the time goes in v5:
time: 279 us; the launch traced here: 278 us
  Pallas kernels  268 us (96%)
  local copies, waits for them, and re-layouts  10.2 us (4%)
    pallas_call x1, Pallas kernels, run_layers(): pl.pallas_call(functools.partial(layers_kernel, layers_order(*w_in.shape[...  137 us
    pallas_call x1, Pallas kernels, reduce_gradients(): pl.pallas_call(functools.partial(reduce_kernel, reduce_order(part, part_b...  130 us

profile of v5, /device:TPU:0, one launch (start us, length us, event | category | flops | bytes accessed | tf_op | source)
XLA Modules:
  0.0 278.4 jit_solution(9799912283011364418)
XLA Ops:
  0.6 137.3 %run_layers.1 = (bf16[256,768]{1,0:T(8,128)(2,1)}, bf16[256,768]{1,0:T(8,128)(2,1)}, bf16[8,4,96,256]{3,2,1,0:T(8,128)(2,1)}, bf16[8,4,96,256]{3,2,1,0:T(8,128)(...) custom-call(bf16[2,96]{1,0:T(2,128)(2,1)} %sc_ref.1, ...), custom_call_target="tpu_custom_call" | custom-call | tf_op jit(solution)/shard_map/run_layers/pallas_call | solution.py:817
  137.9 130.3 %reduce_gradients.1 = (f32[2,4,24,7168]{3,2,1,0:T(8,128)}, f32[2,4,4,32,768]{4,3,2,1,0:T(8,128)}) custom-call(bf16[8,4,96,256]{3,2,1,0:T(8,128)(2,1)} %get-tuple-element.25.refs_0_, bf16[8,4,96,256]{3,2,1,0:T(8,128)(2,1)} %get-tuple-element.26.refs_1_, bf16[8,4,96,256]{3,2,1,0:T(8,128)(2,1)} %get-tuple-element.27.refs_2_, ...), custom_call_target="tpu_custom_call" | custom-call | tf_op jit(solution)/shard_map/reduce_gradients/pallas_call | solution.py:1144
  268.3 0.8 slice.12
  269.1 0.6 constant_dynamic-slice_fusion
  269.7 0.0 copy-start
  269.7 5.4 %slice.13 = f32[2,96,7040]{2,1,0:T(8,128)} slice(f32[2,96,7168]{2,1,0:T(8,128)} %bitcast.7), slice={[0:2], [0:96], [0:7040]} | slice | bytes 10813440 | tf_op jit(solution)/shard_map/slice | solution.py:1178
  275.1 0.0 copy-done
  275.1 0.0 copy-start.2
  275.2 0.0 copy-start.1
  275.2 1.8 slice.14
  276.9 0.0 copy-done.2
  276.9 0.7 copy.13
  277.7 0.0 copy-done.1
  277.7 0.7 copy.14
Async XLA Ops:
  269.7 5.4 %copy-start = (f32[2,4,4,32,768]{4,3,2,1,0:T(8,128)S(1)}, f32[2,4,4,32,768]{4,3,2,1,0:T(8,128)}, u32[]{:S(2)}) copy-start(f32[2,4,4,32,768]{4,3,2,1,0:T(8,128)} %get-tuple-element.39) | copy-start | bytes 9437188
  275.1 1.8 copy-start.2
  275.2 2.5 copy-start.1

commit v6 on v5

--- a/solution.py
+++ b/solution.py
@@ -186,7 +186,6 @@
             follow(("far_z", l, axis), 14, [(("pass_z", l, axis, by), 0) for by in BOTH], [])
         send(("send_scale", l), 15, ZERO, ("back_norm", l), [])
     send(("own_z",), 15, ZERO, ("back_keys", 0), [])
-    send(("late_z",), 14, ZERO, ("back_mlp", 0), [])
     return plan(tasks)
 
 
@@ -327,7 +326,7 @@
 
 
 def layers_kernel(order, sc_ref, wi_ref, wo_ref, x_ref, dy_ref, freq_ref,
-                  y_ref, gx_ref, hy_a, hy_b, hz_a, hz_b, mx_a, mx_b, yx_b, zy_b, zz_b, zy_a, zz_a, z_a, dy_a, sc_out, relay_m, relay_z,
+                  y_ref, gx_ref, hy_a, hy_b, hz_a, hz_b, mx_a, mx_b, yx_b, zy_b, zz_b, z_a, dy_a, sc_out, relay_m, relay_z,
                   wi, wo, z, om, h, hid, qr, kts, vsl, ksl, turned_q, turned_o, scores, dscores, pcat, dscat, cos_ref, sin_ref, turn_ref,
                   dot_heads, qt, dht, dkv, omt, ht, dyt, sc, gains, own_gain, gain_ref, load_sems, own_sems, send_sems, recv_sems,
                   share_send_sems, share_recv_sems):
@@ -483,35 +482,6 @@
             push_z(l, axis, o, spot(axis, o) != 0 if axis == "y" else None)
         if axis == "z":
             own_part(l, axis)
-
-    def late_z():
-        for axis, out in (("z", zz_a), ("y", zy_a)):
-            for o in AROUND:
-                def start():
-                    shared.send(("late", axis), z.at[0, :, columns(axis, o)], out.at[tokens(axis, 0, core)], device(axis, o, core),
-                                batch=("late", axis), whole=out.at[pl.ds(0, TRIO * seq)])
-
-                if axis == "y":
-                    pl.when(spot("y", o) != 0)(start)
-                else:
-                    start()
-
-    def settle_late():
-        shared.arrive(("late", "z"), zz_a.at[pl.ds(0, TRIO * seq)])
-        _, leaving = shared.sent.pop(("late", "y"))
-
-        def left(n):
-            part = zy_a.at[pl.ds(0, n * seq)]
-            pltpu.make_async_copy(part, part, share_send_sems.at[leaving]).wait()
-
-        @pl.when(y == 0)
-        def _():
-            left(TRIO)
-
-        @pl.when(y != 0)
-        def _():
-            left(PAIR)
-            shared.arrive(("late", "y"), zy_a.at[pl.ds(0, TRIO * seq)])
 
     def rest_z(l):
         for o in (PAIR, 1, -1):
@@ -787,7 +757,7 @@
     stages.update(
         norm=do_norm, project=do_project, attend=attend, mlp=do_mlp, put=do_put, back_out=back_out, back_mlp=back_mlp, back_heads=back_heads,
         back_quad=back_quad, back_keys=back_keys, back_in=back_in, back_norm=back_norm, send_h=send_h, pass_h=pass_h, send_m=send_m,
-        pass_m=pass_m, send_y=send_y, pass_y=pass_y, far_y=far_y, send_z=send_z, rest_z=rest_z, late_z=late_z, pass_z=pass_z, twin_z=twin_z, far_z=far_z,
+        pass_m=pass_m, send_y=send_y, pass_y=pass_y, far_y=far_y, send_z=send_z, rest_z=rest_z, pass_z=pass_z, twin_z=twin_z, far_z=far_z,
         send_scale=send_scale, own_z=lambda: keep(z.at[0], z_a), own_y=lambda: keep(middle, dy_a))
     for kind, *task in order:
         stages[kind](*task)
@@ -798,7 +768,6 @@
     arrive_y(1)
     for l, axis in z_out:
         arrive_z(l, axis)
-    settle_late()
     for copy in stored:
         copy.wait()
     shared.drain()
@@ -817,10 +786,10 @@
     return pl.pallas_call(
         functools.partial(layers_kernel, layers_order(*w_in.shape[1:], *w_out.shape[1:], seq, starts)),
         out_shape=(out(seq, dim), out(seq, dim), *[out(ROW, SIDE, dim // ROW, seq)] * SIDE, *[out(ROW, cat // ROW, seq)] * PAIR, out(line, dim),
-                   *[out(line, wide // ROW)] * SIDE, out(seq, wide), out(seq, dim), out(PAIR, ROW, ROW, dim, dtype=F32),
+                   *[out(line, wide // ROW)] * PAIR, out(seq, wide), out(seq, dim), out(PAIR, ROW, ROW, dim, dtype=F32),
                    out(PAIR, PAIR, PAIR, cat // 16, seq), out(PAIR, PAIR, PAIR, seq // PAIR, wide // ROW)),
         in_specs=[vmem, hbm, hbm] + [vmem] * TRIO,
-        out_specs=[vmem] * PAIR + [hbm] * 16,
+        out_specs=[vmem] * PAIR + [hbm] * 14,
         scratch_shapes=[
             buffer(PAIR, dim, proj), buffer(PAIR, cat, dim), buffer(PAIR, seq, wide), buffer(seq, cat), buffer(PAIR, seq, dim),
             buffer(PAIR, seq, dim), buffer(PAIR, seq, dim),
@@ -830,7 +799,7 @@
             buffer(dim, seq), buffer(dim, seq), buffer(dim, seq, dtype=F32), buffer(PAIR, seq, LANE, dtype=F32),
             buffer(PAIR, cat, seq), buffer(PAIR, SIDE, PAIR, dim // ROW, seq), buffer(dim, seq), buffer(PAIR, ROW, dim, dtype=F32),
             buffer(ROW, ROW, dim, dtype=F32), buffer(ROW, dim, dtype=F32), buffer(ROW, dim, dtype=F32),
-            sem((SIDE,)), sem((13,)), sem((15,)), sem((107,)), sem((15,)), sem((HEAD,)),
+            sem((SIDE,)), sem((13,)), sem((15,)), sem((107,)), sem((13,)), sem((HEAD,)),
         ],
         compiler_params=pltpu.CompilerParams(collective_id=PAIR, has_side_effects=True, vmem_limit_bytes=67043328),
         name="run_layers",
@@ -845,20 +814,20 @@
     rate = 11650.0
     tasks = []
     sizes = {"y": WIDE * 896 / (PAIR * rate), "z": WIDE * 896 / (PAIR * rate), "x": WIDE * 768 / (PAIR * rate)}
-    tasks.append((("swap", "x"), (0, 0), starts[PAIR], [], [], [(("x", by), sizes["x"] * n) for by, n in ((1, 1), (-1, 1), (1, PAIR))], SHORT))
-    tasks.append((("swap", "z"), (0, 0), starts[TRIO], [], [], [("chip", 1.6)] * SIDE, 0.4))
-    tasks.append((("swap", "y"), (0, 0), starts[TRIO], [], [], [(("y", by), sizes["y"] * n / PAIR) for by, n in ((1, 1), (-1, 1), (1, PAIR))] + [("chip", 1.6)] * SIDE, 0.4))
-    for axis in "yx":
-        for i, o in enumerate(AROUND):
-            tasks.append((("near", axis, o), (0, PAIR), ZERO, [(("swap", axis), i)], [], [("chip", 1.6)], QUICK))
+    for axis in "yzx":
+        size = sizes[axis]
+        tasks.append((("swap", axis), (0, 0), starts[PAIR] if axis == "x" else starts[TRIO], [], [],
+                      [((axis, by), size * n) for by, n in ((-1, 0.5), (1, 1), (-1, 1), (1, 1))], SHORT))
+        tasks.append((("relay", axis), (0, 0), ZERO, [(("swap", axis), 0)], [], [((axis, -1), size / PAIR)], SHORT))
+        for o, needs in ((1, [(("swap", axis), 1)]), (-1, [(("swap", axis), PAIR)]), (PAIR, [(("swap", axis), TRIO), (("relay", axis), 0)])):
+            tasks.append((("near", axis, o), (0, PAIR), ZERO, needs, [], [("chip", 1.6)], QUICK))
     tasks.append((("fetch", 0), (5, 0), ZERO, [], [("make", 1, len(PARTS) - 1)], [], QUICK))
     for l in (1, 0):
         late = 1 - l
         for c, (kind, first, then, last, at, width) in enumerate(PARTS):
             needs, cost = [], 1.6 * width / STRIP
             if l == 0:
-                needs = [(("swap", "z"), k) for k in range(SIDE)] if (kind, last) == ("i", "z") else [
-                    (("near", last if kind == "i" else "x", o), 0) for o in AROUND]
+                needs = [(("near", last if kind == "i" else "x", o), 0) for o in AROUND]
             tasks.append((("make", l, c), (9 * late, c), starts[late], needs, [] if l else [("fetch", 0)], [], cost))
             full = SIDE * SIDE * (rows if kind == "i" else rows_b) * width / rate
             sends = [[((first, by), full / ROW) for by in BOTH], [((first, by), full / SIDE) for by in BOTH],
@@ -875,11 +844,11 @@
 
 def reduce_kernel(order, *refs):
     hy, hz, mx = refs[0:PAIR], refs[PAIR:SIDE], refs[SIDE:6]
-    yx1, zy1, zz1, zy0, zz0, z0, y0, sc = refs[6:14]
-    oa, ob = refs[14:16]
+    yx1, zy1, zz1, z0, y0, sc = refs[6:12]
+    oa, ob = refs[12:14]
     n = len(PARTS)
-    total, half, full, small, front = (refs[16 + k * n:16 + (k + 1) * n] for k in range(5))
-    (hbuf, zbuf, mbuf, ybuf, scbuf, ssem, rsem, isem, osem, fsem) = refs[16 + 5 * n:]
+    total, half, full, small, front = (refs[14 + k * n:14 + (k + 1) * n] for k in range(5))
+    (hbuf, zbuf, mbuf, ybuf, scbuf, rz, ry, ssem, rsem, isem, osem) = refs[14 + 5 * n:]
     position = chip_position()
     x, y, zc, core = position
     place = {"x": x, "y": y, "z": zc}
@@ -935,66 +904,45 @@
     def target(axis):
         return ybuf.at[0] if axis == "x" else zbuf.at[0, "yz".index(axis)]
 
-    def seven(axis, n):
-        return dict(batch=("swap", axis), whole=target(axis).at[pl.ds(0, n * seq)])
-
-    batches = {axis: seven(axis, OTHERS if axis == "x" else SIDE) for axis in "xyz"}
-
-    def to_twin(axis, src, o):
-        near_core = device_at(x, y, zc, 1 - core)
-        links.send(("near", axis), src, target(axis).at[tokens(axis, -o, core)], near_core, **batches[axis])
+    def leaving(axis):
+        return dict(batch=("swap", axis), whole=target(axis).at[pl.ds(0, OTHERS * seq + seq // PAIR)])
+
+    def half_at(axis, o, k):
+        start = (PAIR * spot(axis, o) + core) * seq + k * (seq // PAIR)
+        return target(axis).at[pl.ds(pl.multiple_of(start, seq // PAIR), seq // PAIR)]
+
+    def relay_of(axis):
+        return ry if axis == "x" else rz.at["yz".index(axis)]
 
     def swap(axis):
-        def part(o):
-            return y0 if axis == "x" else z0.at[:, columns(axis, o)]
+        def part(o, rows=slice(None)):
+            return y0.at[rows] if axis == "x" else z0.at[rows, columns(axis, o)]
 
         mine = target(axis).at[tokens(axis, 0, core)]
-        if axis == "x":
-            for o in AROUND:
-                links.send(("swap", axis, o), y0, mine, peer(axis, o), **batches[axis])
-        elif axis == "y":
-            for o in AROUND:
-                @pl.when(spot("y", o) == 0)
-                def _():
-                    links.send(("swap", axis, o), part(o), mine, device_at(x, spot("y", o), zc, core), batch=("first",), whole=mine)
-        to_twin(axis, part(0), 0)
+        links.send(("relay", axis), part(PAIR, pl.ds(seq // PAIR, seq // PAIR)), relay_of(axis), peer(axis, -1), **leaving(axis))
+        for by in BOTH:
+            links.send(("swap", axis, by), part(by), mine, peer(axis, by), **leaving(axis))
+        links.send(("swap", axis, PAIR), part(PAIR, pl.ds(0, seq // PAIR)), half_at(axis, 0, 0), peer(axis, PAIR), **leaving(axis))
+        links.send(("near", axis), part(0), mine, twin, **leaving(axis))
         load(("own", axis), part(0), mine)
-        if axis == "z":
-            for o in AROUND:
-                landed = zz0.at[tokens(axis, -o, core)]
-                to_twin(axis, landed, o)
-                load(("far", axis, o), landed, target(axis).at[tokens(axis, -o, core)])
-        if axis == "y":
-            @pl.when(y != 0)
-            def _():
-                for k, o in enumerate(AROUND):
-                    landed = zy0.at[tokens(axis, -o, core)]
-                    to_twin(axis, landed, o)
-                    pltpu.make_async_copy(landed, target(axis).at[tokens(axis, -o, core)], fsem.at[k]).start()
+
+    def relay(axis):
+        links.arrive(("relay", axis), relay_of(axis))
+        links.send(("relayed", axis), relay_of(axis), half_at(axis, 1, 1), peer(axis, -1), **leaving(axis))
 
     def near(axis, o):
-        def go():
-            landed = target(axis).at[tokens(axis, -o, core)]
+        landed = target(axis).at[tokens(axis, -o, core)]
+        if o == PAIR:
+            links.arrive(("swap", axis, PAIR), half_at(axis, PAIR, 0))
+            links.arrive(("relayed", axis), half_at(axis, PAIR, 1))
+        else:
             links.arrive(("swap", axis, o), landed)
-            to_twin(axis, landed, o)
-
-        if axis == "x":
-            go()
-        else:
-            pl.when(y == 0)(go)
+        links.send(("near", axis), landed, landed, twin, **leaving(axis))
 
     def joined(axis):
         if axis not in done:
             done.add(axis)
             loaded(("own", axis))
-            if axis == "z":
-                loaded(*[("far", axis, o) for o in AROUND])
-            if axis == "y":
-                @pl.when(y != 0)
-                def _():
-                    for k, o in enumerate(AROUND):
-                        landed = target(axis).at[tokens(axis, -o, core)]
-                        pltpu.make_async_copy(landed, landed, fsem.at[k]).wait()
             links.arrive(("near", axis), target(axis).at[pl.ds(0, SIDE * seq)])
 
     def joined_lanes(ref, l, i):
@@ -1096,16 +1044,9 @@
         else:
             links.arrive((l, c, "a3"), area(l, c, PAIR, slice(None)))
 
-    stages = {"swap": swap, "near": near, "fetch": fetch, "make": make, "sum": add}
+    stages = {"swap": swap, "relay": relay, "near": near, "fetch": fetch, "make": make, "sum": add}
     for kind, *task in order:
         stages[kind](*task)
-    _, leaving = links.sent.pop(("first",))
-
-    @pl.when(y != 0)
-    def _():
-        mine = target("y").at[tokens("y", 0, core)]
-        pltpu.make_async_copy(mine, mine, ssem.at[leaving]).wait()
-
     links.drain()
 
 
@@ -1130,7 +1071,7 @@
     return spots, peers
 
 
-def reduce_gradients(operands, starts=(ZERO, ZERO, 8.0, ZERO)):
+def reduce_gradients(operands, starts=(ZERO, ZERO, 20.0, 3.0)):
     hbm = pl.BlockSpec(memory_space=pltpu.HBM)
     h_rows, m_rows, y_cols, z_cols, z_own, y_own, scale_parts = operands
     part, part_b = h_rows[0].shape[PAIR] // SIDE, (m_rows[0].shape[1] + BAND) // 16
@@ -1144,13 +1085,14 @@
     return pl.pallas_call(
         functools.partial(reduce_kernel, reduce_order(part, part_b, starts)),
         out_shape=(out(PAIR, SIDE, part, wide), out(PAIR, SIDE, SIDE, part_b, dim)),
-        in_specs=[hbm] * 14,
+        in_specs=[hbm] * 12,
         out_specs=[hbm] * PAIR,
         scratch_shapes=[
             *buffers(SIDE, SIDE), *buffers(PAIR, PAIR), *buffers(PAIR, SIDE), *buffers(TRIO), *buffers(),
             pltpu.VMEM((PAIR, PAIR, *h_rows[0].shape), BF), pltpu.VMEM((PAIR, PAIR, line, wide // ROW), BF), pltpu.VMEM((PAIR, *m_rows[0].shape), BF),
             pltpu.VMEM((PAIR, line, dim), BF), pltpu.VMEM(scale_parts.shape, F32),
-            sem((40,)), sem((96,)), sem((17,)), sem((PAIR, len(PARTS))), sem((TRIO,)),
+            pltpu.VMEM((PAIR, z_own.shape[0] // PAIR, wide // ROW), BF), pltpu.VMEM((y_own.shape[0] // PAIR, dim), BF),
+            sem((39,)), sem((102,)), sem((14,)), sem((PAIR, len(PARTS))),
         ],
         compiler_params=pltpu.CompilerParams(collective_id=1, has_side_effects=True, vmem_limit_bytes=67043328),
         name="reduce_gradients",
@@ -1174,7 +1116,7 @@
         freq = 10000.0 ** (-np.arange(half_dim, dtype=np.float32) * 2.0 / head_dim)
         freq = jnp.asarray(np.tile(freq.astype(np.float32), (ROW, LANE // half_dim)))
         hidden, grad_hidden, *rest = run_layers(x_in[0], grad_y[0], norm_scale, w_in, w_out, freq)
-        in_sums, out_sums = reduce_gradients((rest[0:SIDE], rest[SIDE:6], rest[6], rest[OTHERS:11], rest[11], rest[12], rest[13]))
+        in_sums, out_sums = reduce_gradients((rest[0:SIDE], rest[SIDE:6], rest[6], rest[OTHERS:9], rest[9], rest[10], rest[11]))
         in_grads = in_sums.reshape(n_layers, rows, -1)[:, :, :proj_dim]
         out_rows = out_sums.reshape(n_layers, -1, model_dim)
         scale_grads = lax.dynamic_slice(out_rows[:, rows_out], (0, lax.axis_index("fsdp") * rows), (n_layers, rows))

time: 279 us -> 244 us (0.87)
  Pallas kernels: 268 us -> 233 us
    pallas_call x1, Pallas kernels: 130 us -> 106 us  [reduce_gradients(): pl.pallas_call(functools.partial(reduce_kernel, reduce_order(part, part_b...]
    pallas_call x1, Pallas kernels: 137 us -> 127 us  [run_layers(): pl.pallas_call(functools.partial(layers_kernel, layers_order(*w_in.shape[...]
where the time goes in v6:
time: 244 us
  Pallas kernels  233 us (95%)
  local copies, waits for them, and re-layouts  10.2 us (4%)
    pallas_call x1, Pallas kernels, run_layers(): pl.pallas_call(functools.partial(layers_kernel, layers_order(*w_in.shape[...  127 us
    pallas_call x1, Pallas kernels, reduce_gradients(): pl.pallas_call(functools.partial(reduce_kernel, reduce_order(part, part_b...  106 us
    slice x1, local copies, waits for them, and re-layouts, device_step(): in_grads = in_sums.reshape(n_layers, rows, -1)[:, :, :proj_dim]  5.44 us

profile of v6, /device:TPU:0, one launch (start us, length us, event | category | flops | bytes accessed | tf_op | source)
XLA Modules:
  0.0 244.1 jit_solution(15862824117899018632)
XLA Ops:
  0.6 127.3 %run_layers.1 = (bf16[256,768]{1,0:T(8,128)(2,1)}, bf16[256,768]{1,0:T(8,128)(2,1)}, bf16[8,4,96,256]{3,2,1,0:T(8,128)(2,1)}, bf16[8,4,96,256]{3,2,1,0:T(8,128)(...) custom-call(bf16[2,96]{1,0:T(2,128)(2,1)} %sc_ref.1, ...), custom_call_target="tpu_custom_call" | custom-call | tf_op jit(solution)/shard_map/run_layers/pallas_call | solution.py:786
  128.0 106.0 %reduce_gradients.1 = (f32[2,4,24,7168]{3,2,1,0:T(8,128)}, f32[2,4,4,32,768]{4,3,2,1,0:T(8,128)}) custom-call(bf16[8,4,96,256]{3,2,1,0:T(8,128)(2,1)} %get-tuple-element.23.refs_0_, bf16[8,4,96,256]{3,2,1,0:T(8,128)(2,1)} %get-tuple-element.24.refs_1_, bf16[8,4,96,256]{3,2,1,0:T(8,128)(2,1)} %get-tuple-element.25.refs_2_, ...), custom_call_target="tpu_custom_call" | custom-call | tf_op jit(solution)/shard_map/reduce_gradients/pallas_call | solution.py:1085
  234.0 0.8 slice.12
  234.8 0.6 constant_dynamic-slice_fusion
  235.4 0.0 copy-start
  235.4 5.4 %slice.13 = f32[2,96,7040]{2,1,0:T(8,128)} slice(f32[2,96,7168]{2,1,0:T(8,128)} %bitcast.7), slice={[0:2], [0:96], [0:7040]} | slice | bytes 10813440 | tf_op jit(solution)/shard_map/slice | solution.py:1120
  240.8 0.0 copy-done
  240.9 0.0 copy-start.2
  240.9 0.0 copy-start.1
  240.9 1.8 slice.14
  242.6 0.0 copy-done.2
  242.6 0.7 copy.13
  243.4 0.0 copy-done.1
  243.4 0.7 copy.14
Async XLA Ops:
  235.4 5.4 %copy-start = (f32[2,4,4,32,768]{4,3,2,1,0:T(8,128)S(1)}, f32[2,4,4,32,768]{4,3,2,1,0:T(8,128)}, u32[]{:S(2)}) copy-start(f32[2,4,4,32,768]{4,3,2,1,0:T(8,128)} %get-tuple-element.35) | copy-start | bytes 9437188
  240.9 1.8 copy-start.2
  240.9 2.5 %copy-start.1 = (bf16[256,768]{1,0:T(8,128)(2,1)S(1)}, bf16[256,768]{1,0:T(8,128)(2,1)}, u32[]{:S(2)}) copy-start(bf16[256,768]{1,0:T(8,128)(2,1)} %get-tuple-element.22) | copy-start | bytes 1179652

commit v7 on v6

--- a/solution.py
+++ b/solution.py
@@ -99,6 +99,7 @@
         size = {"y": rows_i // SIDE * edge, "x": rows_i * (cols_i - PAIR * edge)} if is_in else {"y": rows_o // SIDE * cols_o // PAIR}
         size["z"] = size["y"]
         colors = "yzx" if is_in else "yz"
+        tasks.append((("lend", m), 5, 3.0 + SIDE * m, [], [], [("chip", (rows_i * cols_i if is_in else rows_o * cols_o) / 150000.0)], QUICK))
         for color in colors:
             cost = size[color] / rate
             both = [(("x", by), cost) for by in BOTH]
@@ -123,7 +124,7 @@
     before = []
 
     def work(name, cost, mats=()):
-        needs = [(("hand", m, off), 0) for m in mats for off in (-1, 1, PAIR)]
+        needs = [(("hand", m, off), 0) for m in mats for off in (-1, 1, PAIR)] + [(("lend", m), 0) for m in mats]
         tasks.append((name, 99, ZERO, needs, list(before), [], cost))
         before[:] = [name]
 
@@ -305,13 +306,15 @@
             copy = pltpu.make_async_copy(src, block(m, x, core), lsem.at[m])
             copy.start()
             owns.append(copy)
-            give(m, src, block(m, x, core))
+
+    def lend(m):
+        give(m, mats[m][0], block(m, x, core))
 
     def ready(m):
         owns[m].wait()
         links.arrive((m, "chip"), four(m))
 
-    return begin, ready, peer, {"reach": reach, "relay": relay, "far": far, "pass": pass_on, "close": close, "hand": hand}
+    return begin, ready, peer, {"reach": reach, "relay": relay, "far": far, "pass": pass_on, "close": close, "hand": hand, "lend": lend}
 
 
 BF, F32 = jnp.bfloat16, jnp.float32
@@ -690,11 +693,13 @@
         dq = product(kts[ALL], dscat[ALL]).astype(BF).T
         back = dq.astype(F32) * cos_ref[ALL] - product(dq, turn_ref[ALL]) * sin_ref[ALL]
         z[l, :, cols] = (back * 0.125).astype(BF)
-        for i in range(SIDE):
-            keys, pair = slice(i * seq, (i + 1) * seq), lanes(g * WIDE + i // PAIR * LANE, LANE)
-            even = i % PAIR == 0
-            dkv[0] += product(dscat[keys], qr[l, :, pair] if even else turned_q[:, pair])
-            dkv[1] += product(pcat[keys], turned_o[:, pair] if even else om[:, pair])
+        def pieces(left, even, odd):
+            for i in range(SIDE):
+                pair = lanes(g * WIDE + i // PAIR * LANE, LANE)
+                yield product(left[i * seq:(i + 1) * seq, :], odd(pair) if i % PAIR else even(pair))
+
+        dkv[0] += sum(pieces(dscat, lambda at: qr[l, :, at], lambda at: turned_q[:, at]))
+        dkv[1] += sum(pieces(pcat, lambda at: turned_o[:, at], lambda at: om[:, at]))
 
     def back_keys(l):
         dk = dkv[0].astype(BF)
@@ -1099,6 +1104,61 @@
     )(*h_rows, *m_rows, y_cols, *z_cols, z_own, y_own, scale_parts)
 
 
+def finish_kernel(count, in_ref, out_ref, y_ref, gx_ref, in_grad, out_grad, y_out, gx_out, scale_out, in_buf, out_buf, y_buf, gx_buf, came, left):
+    moves = [(out_ref.at[l, p], out_buf.at[l, pl.ds(SIDE * p, SIDE)]) for l in range(PAIR) for p in range(SIDE)]
+    moves += [(y_ref, y_buf), (gx_ref, gx_buf)]
+    size, width = in_buf.shape[PAIR:]
+    moves += [(in_ref.at[l, p, :, pl.ds(0, width)], in_buf.at[l, p]) for l in range(PAIR) for p in range(SIDE)]
+    loads = [pltpu.make_async_copy(src, dst, came.at[k]) for k, (src, dst) in enumerate(moves)]
+    for copy in loads:
+        copy.start()
+    stores = []
+
+    def store(src, dst):
+        copy = pltpu.make_async_copy(src, dst, left.at[len(stores)])
+        copy.start()
+        stores.append(copy)
+
+    for l in range(PAIR):
+        for p in range(SIDE):
+            loads[SIDE * l + p].wait()
+        store(out_buf.at[l, pl.ds(0, 15)], out_grad.at[l])
+    for k, (src, dst) in enumerate(((y_buf, y_out), (gx_buf, gx_out))):
+        loads[ROW + k].wait()
+        store(src, dst)
+    me = lax.axis_index("fsdp")
+    for l in range(PAIR):
+        for f in range(ROW):
+            @pl.when(me == f)
+            def _():
+                scale_out[l:l + 1] = out_buf[l, 15, 0:1, f * count:(f + 1) * count]
+    for l in range(PAIR):
+        for p in range(SIDE):
+            loads[10 + SIDE * l + p].wait()
+            store(in_buf.at[l, p], in_grad.at[l, pl.ds(p * size, size)])
+    for copy in stores:
+        copy.wait()
+
+
+def finish(in_sums, out_sums, y, gx, rows, proj):
+    hbm = pl.BlockSpec(memory_space=pltpu.HBM)
+    out = lambda *shape, dtype=F32: jax.ShapeDtypeStruct(shape, dtype)
+    size, (depth, dim) = in_sums.shape[PAIR], out_sums.shape[TRIO:]
+    in_grad, out_grad, y_out, gx_out, scale = pl.pallas_call(
+        functools.partial(finish_kernel, rows),
+        out_shape=(out(PAIR, rows, proj), out(PAIR, 15, depth, dim), out(*y.shape, dtype=BF), out(*gx.shape, dtype=BF), out(PAIR, rows)),
+        in_specs=[hbm] * SIDE,
+        out_specs=[hbm] * SIDE + [pl.BlockSpec(memory_space=pltpu.VMEM)],
+        scratch_shapes=[
+            pltpu.VMEM((PAIR, SIDE, size, proj), F32), pltpu.VMEM((PAIR, 16, depth, dim), F32), pltpu.VMEM(y.shape, BF), pltpu.VMEM(gx.shape, BF),
+            pltpu.SemaphoreType.DMA((18,)), pltpu.SemaphoreType.DMA((12,)),
+        ],
+        compiler_params=pltpu.CompilerParams(vmem_limit_bytes=67043328),
+        name="finish",
+    )(in_sums, out_sums, y, gx)
+    return y_out[None], gx_out[None], scale, in_grad, out_grad.reshape(PAIR, 15 * depth, dim)
+
+
 def solution(mesh):
     fsdp_size = mesh.shape["fsdp"]
     batch_spec = P(("dp", "fsdp"), None, None)
@@ -1117,11 +1177,7 @@
         freq = jnp.asarray(np.tile(freq.astype(np.float32), (ROW, LANE // half_dim)))
         hidden, grad_hidden, *rest = run_layers(x_in[0], grad_y[0], norm_scale, w_in, w_out, freq)
         in_sums, out_sums = reduce_gradients((rest[0:SIDE], rest[SIDE:6], rest[6], rest[OTHERS:9], rest[9], rest[10], rest[11]))
-        in_grads = in_sums.reshape(n_layers, rows, -1)[:, :, :proj_dim]
-        out_rows = out_sums.reshape(n_layers, -1, model_dim)
-        scale_grads = lax.dynamic_slice(out_rows[:, rows_out], (0, lax.axis_index("fsdp") * rows), (n_layers, rows))
-        out_grads = out_rows[:, :rows_out]
-        return hidden[None], grad_hidden[None], scale_grads, in_grads, out_grads
+        return finish(in_sums, out_sums, hidden, grad_hidden, rows, proj_dim)
 
     return jax.shard_map(
         device_step,

time: 244 us -> 242 us (level)
  local copies, waits for them, and re-layouts: 10.2 us -> 0 us
  Pallas kernels: 233 us -> 241 us
    slice x3 -> x0, local copies, waits for them, and re-layouts: 8.03 us -> none  [the longest x1 5.44 us: device_step(): in_grads = in_sums.reshape(n_layers, rows, -1)[:, :, :proj_dim]]
    pallas_call x0 -> x1, Pallas kernels: none -> 7.6 us  [finish(): pl.pallas_call(functools.partial(finish_kernel, rows), out_shape=(out(PAI...]
where the time goes in v7:
time: 242 us
  Pallas kernels  241 us (100%)
    pallas_call x1, Pallas kernels, run_layers(): pl.pallas_call(functools.partial(layers_kernel, layers_order(*w_in.shape[...  127 us
    pallas_call x1, Pallas kernels, reduce_gradients(): pl.pallas_call(functools.partial(reduce_kernel, reduce_order(part, part_b...  106 us
    pallas_call x1, Pallas kernels, finish(): pl.pallas_call(functools.partial(finish_kernel, rows), out_shape=(out(PAI...  7.6 us

profile of v7, /device:TPU:0, one launch (start us, length us, event | category | flops | bytes accessed | tf_op | source)
XLA Modules:
  0.0 241.9 jit_solution(2196978905457437564)
XLA Ops:
  0.6 127.1 %run_layers.1 = (bf16[256,768]{1,0:T(8,128)(2,1)}, bf16[256,768]{1,0:T(8,128)(2,1)}, bf16[8,4,96,256]{3,2,1,0:T(8,128)(2,1)}, bf16[8,4,96,256]{3,2,1,0:T(8,128)(...) custom-call(bf16[2,96]{1,0:T(2,128)(2,1)} %sc_ref.1, ...), custom_call_target="tpu_custom_call" | custom-call | tf_op jit(solution)/shard_map/run_layers/pallas_call | solution.py:791
  127.8 106.3 %reduce_gradients.1 = (f32[2,4,24,7168]{3,2,1,0:T(8,128)}, f32[2,4,4,32,768]{4,3,2,1,0:T(8,128)}) custom-call(bf16[8,4,96,256]{3,2,1,0:T(8,128)(2,1)} %get-tuple-element.26.refs_0_, bf16[8,4,96,256]{3,2,1,0:T(8,128)(2,1)} %get-tuple-element.27.refs_1_, bf16[8,4,96,256]{3,2,1,0:T(8,128)(2,1)} %get-tuple-element.28.refs_2_, ...), custom_call_target="tpu_custom_call" | custom-call | tf_op jit(solution)/shard_map/reduce_gradients/pallas_call | solution.py:1090
  234.1 7.6 %finish.1 = (f32[2,96,7040]{2,1,0:T(8,128)}, f32[2,15,32,768]{3,2,1,0:T(8,128)}, bf16[256,768]{1,0:T(8,128)(2,1)}, bf16[256,768]{1,0:T(8,128)(2,1)}, f32[2,96]{1,0:T(2,128)}) custom-call(f32[2,4,24,7168]{3,2,1,0:T(8,128)} %get-tuple-element.38.in_ref, f32[2,4,4,32,768]{4,3,2,1,0:T(8,128)} %get-tuple-element.39.out_ref, ...), custom_call_target="tpu_custom_call" | custom-call | tf_op jit(solution)/shard_map/finish/pallas_call | solution.py:1147

commit v8 on v7

--- a/solution.py
+++ b/solution.py
@@ -155,16 +155,8 @@
     model, margin = rows_i * ROW, 2.0
     for l in (1, 0):
         for axis in "yz":
-            name = ("send_h", l, axis)
-            send(name, 20 - l, 58.0, ("norm", l), both(axis, seq * model))
-            for i, by in enumerate(BOTH):
-                for index in range(PAIR):
-                    follow(("pass_h", l, axis, by, index), 10, [(name, i)], [((axis, by), seq * model / SIDE / rate, margin)])
-        name = ("send_m", l)
-        send(name, 22 - l, ZERO, ("mlp", l), both("x", seq * rows_o) + both("x", PAIR * seq * rows_o))
-        for i, by in enumerate(BOTH):
-            for index in range(PAIR):
-                follow(("pass_m", l, by, index), 11, [(name, i)], [(("x", by), seq * rows_o / PAIR / rate, margin)])
+            send(("send_h", l, axis), 20 - l, 58.0, ("norm", l), both(axis, seq * model) + both(axis, seq * model))
+        send(("send_m", l), 22 - l, ZERO, ("mlp", l), both("x", PAIR * seq * rows_o) + both("x", PAIR * seq * rows_o))
         if l == 0:
             send(("own_y",), 15, ZERO, ("back_norm", 1), [])
             send(("send_scale", l), 15, ZERO, ("back_norm", l), [])
@@ -329,7 +321,7 @@
 
 
 def layers_kernel(order, sc_ref, wi_ref, wo_ref, x_ref, dy_ref, freq_ref,
-                  y_ref, gx_ref, hy_a, hy_b, hz_a, hz_b, mx_a, mx_b, yx_b, zy_b, zz_b, z_a, dy_a, sc_out, relay_m, relay_z,
+                  y_ref, gx_ref, hy_a, hy_b, hz_a, hz_b, mx_a, mx_b, yx_b, zy_b, zz_b, z_a, dy_a, sc_out, relay_z,
                   wi, wo, z, om, h, hid, qr, kts, vsl, ksl, turned_q, turned_o, scores, dscores, pcat, dscat, cos_ref, sin_ref, turn_ref,
                   dot_heads, qt, dht, dkv, omt, ht, dyt, sc, gains, own_gain, gain_ref, load_sems, own_sems, send_sems, recv_sems,
                   share_send_sems, share_recv_sems):
@@ -385,51 +377,28 @@
         return dict(batch=batch, whole=whole)
 
     def send_h(l, axis):
-        out = h_out[axis][l].at[place(axis, 0, core)]
-        for by in BOTH:
+        out, batch = h_out[axis][l].at[place(axis, 0, core)], several(("h", l, axis), h_out[axis][l], OTHERS)
+        for o in AROUND:
             for index in range(PAIR):
-                shared.send(("h", l, axis, by), ht.at[l, :, index], out, device(axis, by, index), lane=core, **several(("h", l, axis), h_out[axis][l], OTHERS))
-        shared.send(("h", l, axis), ht.at[l, :, 1 - core], out, twin, **several(("h", l, axis), h_out[axis][l], OTHERS))
+                shared.send(("h", l, axis), ht.at[l, :, index], out, device(axis, o, index), **batch)
+        shared.send(("h", l, axis), ht.at[l, :, 1 - core], out, twin, **batch)
         keep(ht.at[l, :, core], out)
-
-    def pass_h(l, axis, by, index):
-        out = h_out[axis][l]
-        shared.arrive(("h", l, axis, by), out.at[place(axis, -by, index)], index)
-        part = out.at[place(axis, -by, index), pl.ds(1 - by, PAIR)]
-        shared.send(("h", l, axis), part, part, device(axis, by, core), **several(("h", l, axis), out, OTHERS))
 
     def arrive_h(l):
         for axis in "yz":
-            shared.arrive(("h", l, axis), h_out[axis][l].at[pl.ds(0, TRIO)])
-
-    def row_block(l, o, index, part=None):
+            shared.arrive(("h", l, axis), h_out[axis][l].at[pl.ds(0, OTHERS)])
+
+    def row_block(l, o, index):
         size = omt.shape[1] // ROW
-        start = (PAIR * spot("x", o) + index) * size
-        if part is not None:
-            size = size // PAIR
-            start = start + part * size
-        return omt.at[l, pl.ds(pl.multiple_of(start, 16), size)]
-
-    def row_half(k):
-        size = m_out[0].shape[1] // PAIR
-        return pl.ds(k * size, size)
+        return omt.at[l, pl.ds(pl.multiple_of((PAIR * spot("x", o) + index) * size, BAND), size)]
 
     def send_m(l):
-        out = m_out[l].at[place("x", 0, core)]
-        for k, by in enumerate(BOTH):
+        out, batch = m_out[l].at[place("x", 0, core)], several(("m", l), m_out[l], OTHERS)
+        for o in AROUND:
             for index in range(PAIR):
-                shared.send(("mr", l, by), row_block(l, PAIR, index, k), relay_m.at[l, k, core], device("x", by, index), lane=core, **several(("m", l), m_out[l], OTHERS))
-        for by in BOTH:
-            for index in range(PAIR):
-                shared.send(("m", l), row_block(l, by, index), out, device("x", by, index), **several(("m", l), m_out[l], OTHERS))
-        shared.send(("m", l), row_block(l, 0, 1 - core), out, twin, **several(("m", l), m_out[l], OTHERS))
+                shared.send(("m", l), row_block(l, o, index), out, device("x", o, index), **batch)
+        shared.send(("m", l), row_block(l, 0, 1 - core), out, twin, **batch)
         keep(row_block(l, 0, core), out)
-
-    def pass_m(l, by, index):
-        k = (1 - by) // PAIR
-        shared.arrive(("mr", l, by), relay_m.at[l, k, index], index)
-        shared.send(("m", l), relay_m.at[l, k, index], m_out[l].at[place("x", -by, index), row_half(k)], device("x", by, core),
-                    **several(("m2", l), m_out[l], PAIR))
 
     def arrive_m(l):
         shared.arrive(("m", l), m_out[l].at[pl.ds(0, OTHERS)])
@@ -761,8 +730,7 @@
 
     stages.update(
         norm=do_norm, project=do_project, attend=attend, mlp=do_mlp, put=do_put, back_out=back_out, back_mlp=back_mlp, back_heads=back_heads,
-        back_quad=back_quad, back_keys=back_keys, back_in=back_in, back_norm=back_norm, send_h=send_h, pass_h=pass_h, send_m=send_m,
-        pass_m=pass_m, send_y=send_y, pass_y=pass_y, far_y=far_y, send_z=send_z, rest_z=rest_z, pass_z=pass_z, twin_z=twin_z, far_z=far_z,
+        back_quad=back_quad, back_keys=back_keys, back_in=back_in, back_norm=back_norm, send_h=send_h, send_m=send_m, send_y=send_y, pass_y=pass_y, far_y=far_y, send_z=send_z, rest_z=rest_z, pass_z=pass_z, twin_z=twin_z, far_z=far_z,
         send_scale=send_scale, own_z=lambda: keep(z.at[0], z_a), own_y=lambda: keep(middle, dy_a))
     for kind, *task in order:
         stages[kind](*task)
@@ -792,9 +760,9 @@
         functools.partial(layers_kernel, layers_order(*w_in.shape[1:], *w_out.shape[1:], seq, starts)),
         out_shape=(out(seq, dim), out(seq, dim), *[out(ROW, SIDE, dim // ROW, seq)] * SIDE, *[out(ROW, cat // ROW, seq)] * PAIR, out(line, dim),
                    *[out(line, wide // ROW)] * PAIR, out(seq, wide), out(seq, dim), out(PAIR, ROW, ROW, dim, dtype=F32),
-                   out(PAIR, PAIR, PAIR, cat // 16, seq), out(PAIR, PAIR, PAIR, seq // PAIR, wide // ROW)),
+                   out(PAIR, PAIR, PAIR, seq // PAIR, wide // ROW)),
         in_specs=[vmem, hbm, hbm] + [vmem] * TRIO,
-        out_specs=[vmem] * PAIR + [hbm] * 14,
+        out_specs=[vmem] * PAIR + [hbm] * 13,
         scratch_shapes=[
             buffer(PAIR, dim, proj), buffer(PAIR, cat, dim), buffer(PAIR, seq, wide), buffer(seq, cat), buffer(PAIR, seq, dim),
             buffer(PAIR, seq, dim), buffer(PAIR, seq, dim),
@@ -804,7 +772,7 @@
             buffer(dim, seq), buffer(dim, seq), buffer(dim, seq, dtype=F32), buffer(PAIR, seq, LANE, dtype=F32),
             buffer(PAIR, cat, seq), buffer(PAIR, SIDE, PAIR, dim // ROW, seq), buffer(dim, seq), buffer(PAIR, ROW, dim, dtype=F32),
             buffer(ROW, ROW, dim, dtype=F32), buffer(ROW, dim, dtype=F32), buffer(ROW, dim, dtype=F32),
-            sem((SIDE,)), sem((13,)), sem((15,)), sem((107,)), sem((13,)), sem((HEAD,)),
+            sem((SIDE,)), sem((13,)), sem((15,)), sem((107,)), sem((11,)), sem((24,)),
         ],
         compiler_params=pltpu.CompilerParams(collective_id=PAIR, has_side_effects=True, vmem_limit_bytes=67043328),
         name="run_layers",
@@ -838,9 +806,9 @@
             sends = [[((first, by), full / ROW) for by in BOTH], [((first, by), full / SIDE) for by in BOTH],
                      [((then, o), full / 16) for o in (1, -1, 1)], []]
             piece = full / 16
-            sends += [[((then, by), piece) for by in BOTH], [((then, 1 - PAIR * (c % PAIR)), piece)], [((last, by), SIDE * piece) for by in BOTH],
+            sends += [[((then, o), piece) for o in (1, -1, 1)], [((last, by), SIDE * piece) for by in BOTH],
                       [((last, by), PAIR * piece) for by in BOTH], []]
-            for s in range(9):
+            for s in range(ROW):
                 task = ("sum", l, c, s)
                 needs = [(("sum", l, c, s - 1), k) for k in range(len(sends[s - 1]))] if s else []
                 tasks.append((task, (late, -s), ZERO, needs, [("make", l, c)] if s == 0 else [("sum", l, c, s - 1)], sends[s], SHORT))
@@ -999,10 +967,9 @@
     def add(l, c, s):
         kind, first, then, last, at, width = PARTS[c]
         t = total[c].at[l]
-        way = 1 - PAIR * (c % PAIR)
         sums = dict(batch=(l, c, 0), whole=t)
-        wide_ones = dict(batch=(l, c, 1), whole=t.at[pl.ds(0, TRIO)])
-        narrow = dict(batch=(l, c, PAIR), whole=t.at[0, pl.ds(0, PAIR)])
+        lines = dict(batch=(l, c, 1), whole=t.at[pl.ds(0, PAIR)])
+        singles = dict(batch=(l, c, PAIR), whole=t.at[pl.ds(0, PAIR), pl.ds(0, TRIO)])
         if s == 0:
             far = t.at[spot(first, PAIR)]
             for k, by in enumerate(BOTH):
@@ -1019,29 +986,25 @@
             for k in range(PAIR):
                 add_into(mine, full[c].at[l, k])
             for k, o in enumerate(AROUND):
-                links.send((l, c, "small"), mine.at[spot(then, o)], small[c].at[l, k], peer(then, o), **wide_ones)
+                links.send((l, c, "small"), mine.at[spot(then, o)], small[c].at[l, k], peer(then, o), **singles)
         elif s == TRIO:
             links.arrive((l, c, "small"), small[c].at[l])
             mine = t.at[spot(first, 0), spot(then, 0)]
             front[c][l] = (mine[ALL] + small[c][l, 0]) + (small[c][l, 1] + small[c][l, PAIR])
         elif s == SIDE:
             src, dst = front[c].at[l], area(l, c, 0, 0)
-            for by in BOTH:
-                links.send((l, c, "a1"), src, dst, peer(then, by), **narrow)
+            for o in AROUND:
+                links.send((l, c, "a1"), src, dst, peer(then, o), **singles)
             copy = pltpu.make_async_copy(src, dst, osem.at[l, c])
             copy.start()
             loads["front", l, c] = copy
         elif s == 5:
-            links.arrive((l, c, "a1"), t.at[0, pl.ds(0, PAIR)])
-            landed = area(l, c, 0, -way)
-            links.send((l, c, "b1"), landed, landed, peer(then, way), **wide_ones)
-        elif s == 6:
             loaded(("front", l, c))
-            links.arrive((l, c, "b1"), area(l, c, 0, PAIR))
+            links.arrive((l, c, "a1"), t.at[0, pl.ds(0, TRIO)])
             line = area(l, c, 0, slice(None))
             for by in BOTH:
-                links.send((l, c, "a2"), line, line, peer(last, by), **wide_ones)
-        elif s == OTHERS:
+                links.send((l, c, "a2"), line, line, peer(last, by), **lines)
+        elif s == 6:
             links.arrive((l, c, "a2"), t.at[pl.ds(0, PAIR)])
             for k, by in enumerate(BOTH):
                 part = area(l, c, -by, pl.ds(PAIR * k, PAIR))
@@ -1097,7 +1060,7 @@
             pltpu.VMEM((PAIR, PAIR, *h_rows[0].shape), BF), pltpu.VMEM((PAIR, PAIR, line, wide // ROW), BF), pltpu.VMEM((PAIR, *m_rows[0].shape), BF),
             pltpu.VMEM((PAIR, line, dim), BF), pltpu.VMEM(scale_parts.shape, F32),
             pltpu.VMEM((PAIR, z_own.shape[0] // PAIR, wide // ROW), BF), pltpu.VMEM((y_own.shape[0] // PAIR, dim), BF),
-            sem((39,)), sem((102,)), sem((14,)), sem((PAIR, len(PARTS))),
+            sem((39,)), sem((90,)), sem((14,)), sem((PAIR, len(PARTS))),
         ],
         compiler_params=pltpu.CompilerParams(collective_id=1, has_side_effects=True, vmem_limit_bytes=67043328),
         name="reduce_gradients",

time: 242 us -> 242 us (level)
  no operation moved by 1% of the time
where the time goes in v8:
time: 242 us
  Pallas kernels  242 us (100%)
    pallas_call x1, Pallas kernels, run_layers(): pl.pallas_call(functools.partial(layers_kernel, layers_order(*w_in.shape[...  127 us
    pallas_call x1, Pallas kernels, reduce_gradients(): pl.pallas_call(functools.partial(reduce_kernel, reduce_order(part, part_b...  107 us
    pallas_call x1, Pallas kernels, finish(): pl.pallas_call(functools.partial(finish_kernel, rows), out_shape=(out(PAI...  7.6 us

profile of v8, /device:TPU:0, one launch (start us, length us, event | category | flops | bytes accessed | tf_op | source)
XLA Modules:
  0.0 242.4 jit_solution(10720883696141162025)
XLA Ops:
  0.6 127.0 %run_layers.1 = (bf16[256,768]{1,0:T(8,128)(2,1)}, bf16[256,768]{1,0:T(8,128)(2,1)}, bf16[8,4,96,256]{3,2,1,0:T(8,128)(2,1)}, bf16[8,4,96,256]{3,2,1,0:T(8,128)(...) custom-call(bf16[2,96]{1,0:T(2,128)(2,1)} %sc_ref.1, ...), custom_call_target="tpu_custom_call" | custom-call | tf_op jit(solution)/shard_map/run_layers/pallas_call | solution.py:759
  127.6 107.0 %reduce_gradients.1 = (f32[2,4,24,7168]{3,2,1,0:T(8,128)}, f32[2,4,4,32,768]{4,3,2,1,0:T(8,128)}) custom-call(bf16[8,4,96,256]{3,2,1,0:T(8,128)(2,1)} %get-tuple-element.26.refs_0_, bf16[8,4,96,256]{3,2,1,0:T(8,128)(2,1)} %get-tuple-element.27.refs_1_, bf16[8,4,96,256]{3,2,1,0:T(8,128)(2,1)} %get-tuple-element.28.refs_2_, ...), custom_call_target="tpu_custom_call" | custom-call | tf_op jit(solution)/shard_map/reduce_gradients/pallas_call | solution.py:1053
  234.6 7.6 %finish.1 = (f32[2,96,7040]{2,1,0:T(8,128)}, f32[2,15,32,768]{3,2,1,0:T(8,128)}, bf16[256,768]{1,0:T(8,128)(2,1)}, bf16[256,768]{1,0:T(8,128)(2,1)}, f32[2,96]{1,0:T(2,128)}) custom-call(f32[2,4,24,7168]{3,2,1,0:T(8,128)} %get-tuple-element.38.in_ref, f32[2,4,4,32,768]{4,3,2,1,0:T(8,128)} %get-tuple-element.39.out_ref, ...), custom_call_target="tpu_custom_call" | custom-call | tf_op jit(solution)/shard_map/finish/pallas_call | solution.py:1110

commit v9 on v8

--- a/solution.py
+++ b/solution.py
@@ -155,7 +155,7 @@
     model, margin = rows_i * ROW, 2.0
     for l in (1, 0):
         for axis in "yz":
-            send(("send_h", l, axis), 20 - l, 58.0, ("norm", l), both(axis, seq * model) + both(axis, seq * model))
+            send(("send_h", l, axis), 20 - l, 58.0, ("back_keys" if l else "norm", l), both(axis, seq * model) + both(axis, seq * model))
         send(("send_m", l), 22 - l, ZERO, ("mlp", l), both("x", PAIR * seq * rows_o) + both("x", PAIR * seq * rows_o))
         if l == 0:
             send(("own_y",), 15, ZERO, ("back_norm", 1), [])

time: 242 us -> 245 us (1.012)
    pallas_call x1, Pallas kernels: 127 us -> 131 us  [run_layers(): pl.pallas_call(functools.partial(layers_kernel, layers_order(*w_in.shape[...]
where the time goes in v9:
time: 245 us
  Pallas kernels  244 us (100%)
    pallas_call x1, Pallas kernels, run_layers(): pl.pallas_call(functools.partial(layers_kernel, layers_order(*w_in.shape[...  131 us
    pallas_call x1, Pallas kernels, reduce_gradients(): pl.pallas_call(functools.partial(reduce_kernel, reduce_order(part, part_b...  105 us
    pallas_call x1, Pallas kernels, finish(): pl.pallas_call(functools.partial(finish_kernel, rows), out_shape=(out(PAI...  7.6 us

profile of v9, /device:TPU:0, one launch (start us, length us, event | category | flops | bytes accessed | tf_op | source)
XLA Modules:
  0.0 244.8 jit_solution(9414402182515601409)
XLA Ops:
  0.6 130.9 %run_layers.1 = (bf16[256,768]{1,0:T(8,128)(2,1)}, bf16[256,768]{1,0:T(8,128)(2,1)}, bf16[8,4,96,256]{3,2,1,0:T(8,128)(2,1)}, bf16[8,4,96,256]{3,2,1,0:T(8,128)(...) custom-call(bf16[2,96]{1,0:T(2,128)(2,1)} %sc_ref.1, ...), custom_call_target="tpu_custom_call" | custom-call | tf_op jit(solution)/shard_map/run_layers/pallas_call | solution.py:759
  131.5 105.5 %reduce_gradients.1 = (f32[2,4,24,7168]{3,2,1,0:T(8,128)}, f32[2,4,4,32,768]{4,3,2,1,0:T(8,128)}) custom-call(bf16[8,4,96,256]{3,2,1,0:T(8,128)(2,1)} %get-tuple-element.26.refs_0_, bf16[8,4,96,256]{3,2,1,0:T(8,128)(2,1)} %get-tuple-element.27.refs_1_, bf16[8,4,96,256]{3,2,1,0:T(8,128)(2,1)} %get-tuple-element.28.refs_2_, ...), custom_call_target="tpu_custom_call" | custom-call | tf_op jit(solution)/shard_map/reduce_gradients/pallas_call | solution.py:1053
  237.0 7.6 %finish.1 = (f32[2,96,7040]{2,1,0:T(8,128)}, f32[2,15,32,768]{3,2,1,0:T(8,128)}, bf16[256,768]{1,0:T(8,128)(2,1)}, bf16[256,768]{1,0:T(8,128)(2,1)}, f32[2,96]{1,0:T(2,128)}) custom-call(f32[2,4,24,7168]{3,2,1,0:T(8,128)} %get-tuple-element.38.in_ref, f32[2,4,4,32,768]{4,3,2,1,0:T(8,128)} %get-tuple-element.39.out_ref, ...), custom_call_target="tpu_custom_call" | custom-call | tf_op jit(solution)/shard_map/finish/pallas_call | solution.py:1110

commit v10 on v9

--- a/solution.py
+++ b/solution.py
@@ -152,10 +152,14 @@
     def both(axis, size):
         return [((axis, by), size / rate, margin) for by in BOTH]
 
-    model, margin = rows_i * ROW, 2.0
+    model, margin = rows_i * ROW, 0.5
     for l in (1, 0):
         for axis in "yz":
-            send(("send_h", l, axis), 20 - l, 58.0, ("back_keys" if l else "norm", l), both(axis, seq * model) + both(axis, seq * model))
+            name = ("send_h", l, axis)
+            send(name, 20 - l, 58.0, ("norm", l), both(axis, seq * model))
+            for i, by in enumerate(BOTH):
+                for index in range(PAIR):
+                    follow(("pass_h", l, axis, by, index), 10, [(name, i)], [((axis, by), seq * model / SIDE / rate, margin)])
         send(("send_m", l), 22 - l, ZERO, ("mlp", l), both("x", PAIR * seq * rows_o) + both("x", PAIR * seq * rows_o))
         if l == 0:
             send(("own_y",), 15, ZERO, ("back_norm", 1), [])
@@ -377,16 +381,22 @@
         return dict(batch=batch, whole=whole)
 
     def send_h(l, axis):
-        out, batch = h_out[axis][l].at[place(axis, 0, core)], several(("h", l, axis), h_out[axis][l], OTHERS)
-        for o in AROUND:
+        out = h_out[axis][l].at[place(axis, 0, core)]
+        for by in BOTH:
             for index in range(PAIR):
-                shared.send(("h", l, axis), ht.at[l, :, index], out, device(axis, o, index), **batch)
-        shared.send(("h", l, axis), ht.at[l, :, 1 - core], out, twin, **batch)
+                shared.send(("h", l, axis, by), ht.at[l, :, index], out, device(axis, by, index), lane=core, **several(("h", l, axis), h_out[axis][l], OTHERS))
+        shared.send(("h", l, axis), ht.at[l, :, 1 - core], out, twin, **several(("h", l, axis), h_out[axis][l], OTHERS))
         keep(ht.at[l, :, core], out)
+
+    def pass_h(l, axis, by, index):
+        out = h_out[axis][l]
+        shared.arrive(("h", l, axis, by), out.at[place(axis, -by, index)], index)
+        part = out.at[place(axis, -by, index), pl.ds(1 - by, PAIR)]
+        shared.send(("h", l, axis), part, part, device(axis, by, core), **several(("h", l, axis), out, OTHERS))
 
     def arrive_h(l):
         for axis in "yz":
-            shared.arrive(("h", l, axis), h_out[axis][l].at[pl.ds(0, OTHERS)])
+            shared.arrive(("h", l, axis), h_out[axis][l].at[pl.ds(0, TRIO)])
 
     def row_block(l, o, index):
         size = omt.shape[1] // ROW
@@ -730,7 +740,7 @@
 
     stages.update(
         norm=do_norm, project=do_project, attend=attend, mlp=do_mlp, put=do_put, back_out=back_out, back_mlp=back_mlp, back_heads=back_heads,
-        back_quad=back_quad, back_keys=back_keys, back_in=back_in, back_norm=back_norm, send_h=send_h, send_m=send_m, send_y=send_y, pass_y=pass_y, far_y=far_y, send_z=send_z, rest_z=rest_z, pass_z=pass_z, twin_z=twin_z, far_z=far_z,
+        back_quad=back_quad, back_keys=back_keys, back_in=back_in, back_norm=back_norm, send_h=send_h, pass_h=pass_h, send_m=send_m, send_y=send_y, pass_y=pass_y, far_y=far_y, send_z=send_z, rest_z=rest_z, pass_z=pass_z, twin_z=twin_z, far_z=far_z,
         send_scale=send_scale, own_z=lambda: keep(z.at[0], z_a), own_y=lambda: keep(middle, dy_a))
     for kind, *task in order:
         stages[kind](*task)
@@ -772,7 +782,7 @@
             buffer(dim, seq), buffer(dim, seq), buffer(dim, seq, dtype=F32), buffer(PAIR, seq, LANE, dtype=F32),
             buffer(PAIR, cat, seq), buffer(PAIR, SIDE, PAIR, dim // ROW, seq), buffer(dim, seq), buffer(PAIR, ROW, dim, dtype=F32),
             buffer(ROW, ROW, dim, dtype=F32), buffer(ROW, dim, dtype=F32), buffer(ROW, dim, dtype=F32),
-            sem((SIDE,)), sem((13,)), sem((15,)), sem((107,)), sem((11,)), sem((24,)),
+            sem((SIDE,)), sem((13,)), sem((15,)), sem((107,)), sem((11,)), sem((40,)),
         ],
         compiler_params=pltpu.CompilerParams(collective_id=PAIR, has_side_effects=True, vmem_limit_bytes=67043328),
         name="run_layers",

time: 245 us -> 242 us (0.988)
  Pallas kernels: 244 us -> 241 us
    pallas_call x1, Pallas kernels: 131 us -> 128 us  [run_layers(): pl.pallas_call(functools.partial(layers_kernel, layers_order(*w_in.shape[...]
where the time goes in v10:
time: 242 us
  Pallas kernels  241 us (100%)
    pallas_call x1, Pallas kernels, run_layers(): pl.pallas_call(functools.partial(layers_kernel, layers_order(*w_in.shape[...  128 us
    pallas_call x1, Pallas kernels, reduce_gradients(): pl.pallas_call(functools.partial(reduce_kernel, reduce_order(part, part_b...  105 us
    pallas_call x1, Pallas kernels, finish(): pl.pallas_call(functools.partial(finish_kernel, rows), out_shape=(out(PAI...  7.6 us

profile of v10, /device:TPU:0, one launch (start us, length us, event | category | flops | bytes accessed | tf_op | source)
XLA Modules:
  0.0 241.8 jit_solution(17132983164990378333)
XLA Ops:
  0.6 128.0 %run_layers.1 = (bf16[256,768]{1,0:T(8,128)(2,1)}, bf16[256,768]{1,0:T(8,128)(2,1)}, bf16[8,4,96,256]{3,2,1,0:T(8,128)(2,1)}, bf16[8,4,96,256]{3,2,1,0:T(8,128)(...) custom-call(bf16[2,96]{1,0:T(2,128)(2,1)} %sc_ref.1, ...), custom_call_target="tpu_custom_call" | custom-call | tf_op jit(solution)/shard_map/run_layers/pallas_call | solution.py:769
  128.6 105.4 %reduce_gradients.1 = (f32[2,4,24,7168]{3,2,1,0:T(8,128)}, f32[2,4,4,32,768]{4,3,2,1,0:T(8,128)}) custom-call(bf16[8,4,96,256]{3,2,1,0:T(8,128)(2,1)} %get-tuple-element.26.refs_0_, bf16[8,4,96,256]{3,2,1,0:T(8,128)(2,1)} %get-tuple-element.27.refs_1_, bf16[8,4,96,256]{3,2,1,0:T(8,128)(2,1)} %get-tuple-element.28.refs_2_, ...), custom_call_target="tpu_custom_call" | custom-call | tf_op jit(solution)/shard_map/reduce_gradients/pallas_call | solution.py:1063
  234.0 7.6 %finish.1 = (f32[2,96,7040]{2,1,0:T(8,128)}, f32[2,15,32,768]{3,2,1,0:T(8,128)}, bf16[256,768]{1,0:T(8,128)(2,1)}, bf16[256,768]{1,0:T(8,128)(2,1)}, f32[2,96]{1,0:T(2,128)}) custom-call(f32[2,4,24,7168]{3,2,1,0:T(8,128)} %get-tuple-element.38.in_ref, f32[2,4,4,32,768]{4,3,2,1,0:T(8,128)} %get-tuple-element.39.out_ref, ...), custom_call_target="tpu_custom_call" | custom-call | tf_op jit(solution)/shard_map/finish/pallas_call | solution.py:1120

commit v11 on v10

--- a/solution.py
+++ b/solution.py
@@ -99,7 +99,7 @@
         size = {"y": rows_i // SIDE * edge, "x": rows_i * (cols_i - PAIR * edge)} if is_in else {"y": rows_o // SIDE * cols_o // PAIR}
         size["z"] = size["y"]
         colors = "yzx" if is_in else "yz"
-        tasks.append((("lend", m), 5, 3.0 + SIDE * m, [], [], [("chip", (rows_i * cols_i if is_in else rows_o * cols_o) / 150000.0)], QUICK))
+        tasks.append((("lend", m), 5, 3.0 + SIDE * m, [], [], [("chip", (rows_i * cols_i if is_in else rows_o * cols_o) / 200000.0)], QUICK))
         for color in colors:
             cost = size[color] / rate
             both = [(("x", by), cost) for by in BOTH]
@@ -120,7 +120,7 @@
             last = [("close", m, color, off) for color in "yz"]
             if is_in:
                 last.append(("far", m, "x") if off == PAIR else ("relay", m, "x", -off))
-            tasks.append((("hand", m, off), m, ZERO, [], last, [("chip", (rows_i * cols_i if is_in else rows_o * cols_o) / 150000.0)], QUICK))
+            tasks.append((("hand", m, off), m, ZERO, [], last, [("chip", (rows_i * cols_i if is_in else rows_o * cols_o) / 200000.0)], QUICK))
     before = []
 
     def work(name, cost, mats=()):
@@ -855,10 +855,9 @@
         loads[key] = copy
 
     def fetch(l):
-        if l:
-            load(("z", 1, "y"), zy1, zbuf.at[1, 0])
-        load(("h", l, "y"), hy[l], hbuf.at[l, 0])
-        if l:
+        if not l:
+            load(("h", 0, "y"), hy[0], hbuf.at[0, 0])
+        else:
             load(("z", 1, "z"), zz1, zbuf.at[1, 1])
         load(("h", l, "z"), hz[l], hbuf.at[l, 1])
         load(("m", l), mx[l], mbuf.at[l])
@@ -866,7 +865,8 @@
             load(("y", 1), yx1, ybuf.at[1])
         load(("s", l), sc.at[l], scbuf.at[l])
 
-    fetch(1)
+    load(("z", 1, "y"), zy1, zbuf.at[1, 0])
+    load(("h", 1, "y"), hy[1], hbuf.at[1, 0])
     done = set()
 
     def loaded(*keys):
@@ -876,6 +876,7 @@
                 done.add(key)
 
     announce([peer(axis, o) for axis in "xyz" for o in AROUND] + [twin])
+    fetch(1)
     links = Links(ssem, rsem)
 
     def columns(axis, o):

time: 242 us -> 245 us (1.012)
  Pallas kernels: 241 us -> 244 us
    pallas_call x1, Pallas kernels: 128 us -> 131 us  [run_layers(): pl.pallas_call(functools.partial(layers_kernel, layers_order(*w_in.shape[...]
where the time goes in v11:
time: 245 us
  Pallas kernels  244 us (100%)
    pallas_call x1, Pallas kernels, run_layers(): pl.pallas_call(functools.partial(layers_kernel, layers_order(*w_in.shape[...  131 us
    pallas_call x1, Pallas kernels, reduce_gradients(): pl.pallas_call(functools.partial(reduce_kernel, reduce_order(part, part_b...  106 us
    pallas_call x1, Pallas kernels, finish(): pl.pallas_call(functools.partial(finish_kernel, rows), out_shape=(out(PAI...  7.6 us

profile of v11, /device:TPU:0, one launch (start us, length us, event | category | flops | bytes accessed | tf_op | source)
XLA Modules:
  0.0 245.2 jit_solution(16612937390506118462)
XLA Ops:
  0.6 130.9 %run_layers.1 = (bf16[256,768]{1,0:T(8,128)(2,1)}, bf16[256,768]{1,0:T(8,128)(2,1)}, bf16[8,4,96,256]{3,2,1,0:T(8,128)(2,1)}, bf16[8,4,96,256]{3,2,1,0:T(8,128)(...) custom-call(bf16[2,96]{1,0:T(2,128)(2,1)} %sc_ref.1, ...), custom_call_target="tpu_custom_call" | custom-call | tf_op jit(solution)/shard_map/run_layers/pallas_call | solution.py:769
  131.6 105.8 %reduce_gradients.1 = (f32[2,4,24,7168]{3,2,1,0:T(8,128)}, f32[2,4,4,32,768]{4,3,2,1,0:T(8,128)}) custom-call(bf16[8,4,96,256]{3,2,1,0:T(8,128)(2,1)} %get-tuple-element.26.refs_0_, bf16[8,4,96,256]{3,2,1,0:T(8,128)(2,1)} %get-tuple-element.27.refs_1_, bf16[8,4,96,256]{3,2,1,0:T(8,128)(2,1)} %get-tuple-element.28.refs_2_, ...), custom_call_target="tpu_custom_call" | custom-call | tf_op jit(solution)/shard_map/reduce_gradients/pallas_call | solution.py:1064
  237.4 7.6 %finish.1 = (f32[2,96,7040]{2,1,0:T(8,128)}, f32[2,15,32,768]{3,2,1,0:T(8,128)}, bf16[256,768]{1,0:T(8,128)(2,1)}, bf16[256,768]{1,0:T(8,128)(2,1)}, f32[2,96]{1,0:T(2,128)}) custom-call(f32[2,4,24,7168]{3,2,1,0:T(8,128)} %get-tuple-element.38.in_ref, f32[2,4,4,32,768]{4,3,2,1,0:T(8,128)} %get-tuple-element.39.out_ref, ...), custom_call_target="tpu_custom_call" | custom-call | tf_op jit(solution)/shard_map/finish/pallas_call | solution.py:1121

commit v12 on v11

--- a/solution.py
+++ b/solution.py
@@ -99,7 +99,7 @@
         size = {"y": rows_i // SIDE * edge, "x": rows_i * (cols_i - PAIR * edge)} if is_in else {"y": rows_o // SIDE * cols_o // PAIR}
         size["z"] = size["y"]
         colors = "yzx" if is_in else "yz"
-        tasks.append((("lend", m), 5, 3.0 + SIDE * m, [], [], [("chip", (rows_i * cols_i if is_in else rows_o * cols_o) / 200000.0)], QUICK))
+        tasks.append((("lend", m), 5, 3.0 + SIDE * m, [], [], [("chip", (rows_i * cols_i if is_in else rows_o * cols_o) / 120000.0)], QUICK))
         for color in colors:
             cost = size[color] / rate
             both = [(("x", by), cost) for by in BOTH]
@@ -120,7 +120,7 @@
             last = [("close", m, color, off) for color in "yz"]
             if is_in:
                 last.append(("far", m, "x") if off == PAIR else ("relay", m, "x", -off))
-            tasks.append((("hand", m, off), m, ZERO, [], last, [("chip", (rows_i * cols_i if is_in else rows_o * cols_o) / 200000.0)], QUICK))
+            tasks.append((("hand", m, off), m, ZERO, [], last, [("chip", (rows_i * cols_i if is_in else rows_o * cols_o) / 120000.0)], QUICK))
     before = []
 
     def work(name, cost, mats=()):

time: 245 us -> 248 us (1.012)
  Pallas kernels: 244 us -> 247 us
where the time goes in v12:
time: 248 us
  Pallas kernels  247 us (100%)
    pallas_call x1, Pallas kernels, run_layers(): pl.pallas_call(functools.partial(layers_kernel, layers_order(*w_in.shape[...  133 us
    pallas_call x1, Pallas kernels, reduce_gradients(): pl.pallas_call(functools.partial(reduce_kernel, reduce_order(part, part_b...  106 us
    pallas_call x1, Pallas kernels, finish(): pl.pallas_call(functools.partial(finish_kernel, rows), out_shape=(out(PAI...  7.6 us

profile of v12, /device:TPU:0, one launch (start us, length us, event | category | flops | bytes accessed | tf_op | source)
XLA Modules:
  0.0 247.8 jit_solution(4187371228722778160)
XLA Ops:
  0.6 133.1 %run_layers.1 = (bf16[256,768]{1,0:T(8,128)(2,1)}, bf16[256,768]{1,0:T(8,128)(2,1)}, bf16[8,4,96,256]{3,2,1,0:T(8,128)(2,1)}, bf16[8,4,96,256]{3,2,1,0:T(8,128)(...) custom-call(bf16[2,96]{1,0:T(2,128)(2,1)} %sc_ref.1, ...), custom_call_target="tpu_custom_call" | custom-call | tf_op jit(solution)/shard_map/run_layers/pallas_call | solution.py:769
  133.7 106.3 %reduce_gradients.1 = (f32[2,4,24,7168]{3,2,1,0:T(8,128)}, f32[2,4,4,32,768]{4,3,2,1,0:T(8,128)}) custom-call(bf16[8,4,96,256]{3,2,1,0:T(8,128)(2,1)} %get-tuple-element.26.refs_0_, bf16[8,4,96,256]{3,2,1,0:T(8,128)(2,1)} %get-tuple-element.27.refs_1_, bf16[8,4,96,256]{3,2,1,0:T(8,128)(2,1)} %get-tuple-element.28.refs_2_, ...), custom_call_target="tpu_custom_call" | custom-call | tf_op jit(solution)/shard_map/reduce_gradients/pallas_call | solution.py:1064
  240.0 7.6 %finish.1 = (f32[2,96,7040]{2,1,0:T(8,128)}, f32[2,15,32,768]{3,2,1,0:T(8,128)}, bf16[256,768]{1,0:T(8,128)(2,1)}, bf16[256,768]{1,0:T(8,128)(2,1)}, f32[2,96]{1,0:T(2,128)}) custom-call(f32[2,4,24,7168]{3,2,1,0:T(8,128)} %get-tuple-element.38.in_ref, f32[2,4,4,32,768]{4,3,2,1,0:T(8,128)} %get-tuple-element.39.out_ref, ...), custom_call_target="tpu_custom_call" | custom-call | tf_op jit(solution)/shard_map/finish/pallas_call | solution.py:1121

commit v13 on v7

--- a/solution.py
+++ b/solution.py
@@ -838,9 +838,9 @@
             sends = [[((first, by), full / ROW) for by in BOTH], [((first, by), full / SIDE) for by in BOTH],
                      [((then, o), full / 16) for o in (1, -1, 1)], []]
             piece = full / 16
-            sends += [[((then, by), piece) for by in BOTH], [((then, 1 - PAIR * (c % PAIR)), piece)], [((last, by), SIDE * piece) for by in BOTH],
+            sends += [[((then, o), piece) for o in (1, -1, 1)], [((last, by), SIDE * piece) for by in BOTH],
                       [((last, by), PAIR * piece) for by in BOTH], []]
-            for s in range(9):
+            for s in range(ROW):
                 task = ("sum", l, c, s)
                 needs = [(("sum", l, c, s - 1), k) for k in range(len(sends[s - 1]))] if s else []
                 tasks.append((task, (late, -s), ZERO, needs, [("make", l, c)] if s == 0 else [("sum", l, c, s - 1)], sends[s], SHORT))
@@ -877,10 +877,9 @@
         loads[key] = copy
 
     def fetch(l):
-        if l:
-            load(("z", 1, "y"), zy1, zbuf.at[1, 0])
-        load(("h", l, "y"), hy[l], hbuf.at[l, 0])
-        if l:
+        if not l:
+            load(("h", 0, "y"), hy[0], hbuf.at[0, 0])
+        else:
             load(("z", 1, "z"), zz1, zbuf.at[1, 1])
         load(("h", l, "z"), hz[l], hbuf.at[l, 1])
         load(("m", l), mx[l], mbuf.at[l])
@@ -888,7 +887,8 @@
             load(("y", 1), yx1, ybuf.at[1])
         load(("s", l), sc.at[l], scbuf.at[l])
 
-    fetch(1)
+    load(("z", 1, "y"), zy1, zbuf.at[1, 0])
+    load(("h", 1, "y"), hy[1], hbuf.at[1, 0])
     done = set()
 
     def loaded(*keys):
@@ -898,6 +898,7 @@
                 done.add(key)
 
     announce([peer(axis, o) for axis in "xyz" for o in AROUND] + [twin])
+    fetch(1)
     links = Links(ssem, rsem)
 
     def columns(axis, o):
@@ -999,10 +1000,9 @@
     def add(l, c, s):
         kind, first, then, last, at, width = PARTS[c]
         t = total[c].at[l]
-        way = 1 - PAIR * (c % PAIR)
         sums = dict(batch=(l, c, 0), whole=t)
-        wide_ones = dict(batch=(l, c, 1), whole=t.at[pl.ds(0, TRIO)])
-        narrow = dict(batch=(l, c, PAIR), whole=t.at[0, pl.ds(0, PAIR)])
+        lines = dict(batch=(l, c, 1), whole=t.at[pl.ds(0, PAIR)])
+        singles = dict(batch=(l, c, PAIR), whole=t.at[pl.ds(0, PAIR), pl.ds(0, TRIO)])
         if s == 0:
             far = t.at[spot(first, PAIR)]
             for k, by in enumerate(BOTH):
@@ -1019,29 +1019,25 @@
             for k in range(PAIR):
                 add_into(mine, full[c].at[l, k])
             for k, o in enumerate(AROUND):
-                links.send((l, c, "small"), mine.at[spot(then, o)], small[c].at[l, k], peer(then, o), **wide_ones)
+                links.send((l, c, "small"), mine.at[spot(then, o)], small[c].at[l, k], peer(then, o), **singles)
         elif s == TRIO:
             links.arrive((l, c, "small"), small[c].at[l])
             mine = t.at[spot(first, 0), spot(then, 0)]
             front[c][l] = (mine[ALL] + small[c][l, 0]) + (small[c][l, 1] + small[c][l, PAIR])
         elif s == SIDE:
             src, dst = front[c].at[l], area(l, c, 0, 0)
-            for by in BOTH:
-                links.send((l, c, "a1"), src, dst, peer(then, by), **narrow)
+            for o in AROUND:
+                links.send((l, c, "a1"), src, dst, peer(then, o), **singles)
             copy = pltpu.make_async_copy(src, dst, osem.at[l, c])
             copy.start()
             loads["front", l, c] = copy
         elif s == 5:
-            links.arrive((l, c, "a1"), t.at[0, pl.ds(0, PAIR)])
-            landed = area(l, c, 0, -way)
-            links.send((l, c, "b1"), landed, landed, peer(then, way), **wide_ones)
-        elif s == 6:
             loaded(("front", l, c))
-            links.arrive((l, c, "b1"), area(l, c, 0, PAIR))
+            links.arrive((l, c, "a1"), t.at[0, pl.ds(0, TRIO)])
             line = area(l, c, 0, slice(None))
             for by in BOTH:
-                links.send((l, c, "a2"), line, line, peer(last, by), **wide_ones)
-        elif s == OTHERS:
+                links.send((l, c, "a2"), line, line, peer(last, by), **lines)
+        elif s == 6:
             links.arrive((l, c, "a2"), t.at[pl.ds(0, PAIR)])
             for k, by in enumerate(BOTH):
                 part = area(l, c, -by, pl.ds(PAIR * k, PAIR))
@@ -1097,7 +1093,7 @@
             pltpu.VMEM((PAIR, PAIR, *h_rows[0].shape), BF), pltpu.VMEM((PAIR, PAIR, line, wide // ROW), BF), pltpu.VMEM((PAIR, *m_rows[0].shape), BF),
             pltpu.VMEM((PAIR, line, dim), BF), pltpu.VMEM(scale_parts.shape, F32),
             pltpu.VMEM((PAIR, z_own.shape[0] // PAIR, wide // ROW), BF), pltpu.VMEM((y_own.shape[0] // PAIR, dim), BF),
-            sem((39,)), sem((102,)), sem((14,)), sem((PAIR, len(PARTS))),
+            sem((39,)), sem((90,)), sem((14,)), sem((PAIR, len(PARTS))),
         ],
         compiler_params=pltpu.CompilerParams(collective_id=1, has_side_effects=True, vmem_limit_bytes=67043328),
         name="reduce_gradients",

time: 242 us -> 241 us (level)
  no operation moved by 1% of the time
where the time goes in v13:
time: 241 us
  Pallas kernels  240 us (100%)
    pallas_call x1, Pallas kernels, run_layers(): pl.pallas_call(functools.partial(layers_kernel, layers_order(*w_in.shape[...  127 us
    pallas_call x1, Pallas kernels, reduce_gradients(): pl.pallas_call(functools.partial(reduce_kernel, reduce_order(part, part_b...  105 us
    pallas_call x1, Pallas kernels, finish(): pl.pallas_call(functools.partial(finish_kernel, rows), out_shape=(out(PAI...  7.6 us

profile of v13, /device:TPU:0, one launch (start us, length us, event | category | flops | bytes accessed | tf_op | source)
XLA Modules:
  0.0 240.8 jit_solution(15448992765674023003)
XLA Ops:
  0.6 127.1 %run_layers.1 = (bf16[256,768]{1,0:T(8,128)(2,1)}, bf16[256,768]{1,0:T(8,128)(2,1)}, bf16[8,4,96,256]{3,2,1,0:T(8,128)(2,1)}, bf16[8,4,96,256]{3,2,1,0:T(8,128)(...) custom-call(bf16[2,96]{1,0:T(2,128)(2,1)} %sc_ref.1, ...), custom_call_target="tpu_custom_call" | custom-call | tf_op jit(solution)/shard_map/run_layers/pallas_call | solution.py:791
  127.8 105.3 %reduce_gradients.1 = (f32[2,4,24,7168]{3,2,1,0:T(8,128)}, f32[2,4,4,32,768]{4,3,2,1,0:T(8,128)}) custom-call(bf16[8,4,96,256]{3,2,1,0:T(8,128)(2,1)} %get-tuple-element.26.refs_0_, bf16[8,4,96,256]{3,2,1,0:T(8,128)(2,1)} %get-tuple-element.27.refs_1_, bf16[8,4,96,256]{3,2,1,0:T(8,128)(2,1)} %get-tuple-element.28.refs_2_, ...), custom_call_target="tpu_custom_call" | custom-call | tf_op jit(solution)/shard_map/reduce_gradients/pallas_call | solution.py:1086
  233.1 7.6 %finish.1 = (f32[2,96,7040]{2,1,0:T(8,128)}, f32[2,15,32,768]{3,2,1,0:T(8,128)}, bf16[256,768]{1,0:T(8,128)(2,1)}, bf16[256,768]{1,0:T(8,128)(2,1)}, f32[2,96]{1,0:T(2,128)}) custom-call(f32[2,4,24,7168]{3,2,1,0:T(8,128)} %get-tuple-element.38.in_ref, f32[2,4,4,32,768]{4,3,2,1,0:T(8,128)} %get-tuple-element.39.out_ref, ...), custom_call_target="tpu_custom_call" | custom-call | tf_op jit(solution)/shard_map/finish/pallas_call | solution.py:1143

commit v14 on v13

--- a/solution.py
+++ b/solution.py
@@ -1072,7 +1072,7 @@
     return spots, peers
 
 
-def reduce_gradients(operands, starts=(ZERO, ZERO, 20.0, 3.0)):
+def reduce_gradients(operands, starts=(ZERO, ZERO, 26.0, 1.0)):
     hbm = pl.BlockSpec(memory_space=pltpu.HBM)
     h_rows, m_rows, y_cols, z_cols, z_own, y_own, scale_parts = operands
     part, part_b = h_rows[0].shape[PAIR] // SIDE, (m_rows[0].shape[1] + BAND) // 16

time: 241 us -> 240 us (level)
  no operation moved by 1% of the time
where the time goes in v14:
time: 240 us; the launch traced here: 239 us
  Pallas kernels  239 us (100%)
    pallas_call x1, Pallas kernels, run_layers(): pl.pallas_call(functools.partial(layers_kernel, layers_order(*w_in.shape[...  127 us
    pallas_call x1, Pallas kernels, reduce_gradients(): pl.pallas_call(functools.partial(reduce_kernel, reduce_order(part, part_b...  104 us
    pallas_call x1, Pallas kernels, finish(): pl.pallas_call(functools.partial(finish_kernel, rows), out_shape=(out(PAI...  7.6 us

profile of v14, /device:TPU:0, one launch (start us, length us, event | category | flops | bytes accessed | tf_op | source)
XLA Modules:
  0.0 239.4 jit_solution(3594808068740251863)
XLA Ops:
  0.6 127.1 %run_layers.1 = (bf16[256,768]{1,0:T(8,128)(2,1)}, bf16[256,768]{1,0:T(8,128)(2,1)}, bf16[8,4,96,256]{3,2,1,0:T(8,128)(2,1)}, bf16[8,4,96,256]{3,2,1,0:T(8,128)(...) custom-call(bf16[2,96]{1,0:T(2,128)(2,1)} %sc_ref.1, ...), custom_call_target="tpu_custom_call" | custom-call | tf_op jit(solution)/shard_map/run_layers/pallas_call | solution.py:791
  127.8 103.9 %reduce_gradients.1 = (f32[2,4,24,7168]{3,2,1,0:T(8,128)}, f32[2,4,4,32,768]{4,3,2,1,0:T(8,128)}) custom-call(bf16[8,4,96,256]{3,2,1,0:T(8,128)(2,1)} %get-tuple-element.26.refs_0_, bf16[8,4,96,256]{3,2,1,0:T(8,128)(2,1)} %get-tuple-element.27.refs_1_, bf16[8,4,96,256]{3,2,1,0:T(8,128)(2,1)} %get-tuple-element.28.refs_2_, ...), custom_call_target="tpu_custom_call" | custom-call | tf_op jit(solution)/shard_map/reduce_gradients/pallas_call | solution.py:1086
  231.6 7.6 %finish.1 = (f32[2,96,7040]{2,1,0:T(8,128)}, f32[2,15,32,768]{3,2,1,0:T(8,128)}, bf16[256,768]{1,0:T(8,128)(2,1)}, bf16[256,768]{1,0:T(8,128)(2,1)}, f32[2,96]{1,0:T(2,128)}) custom-call(f32[2,4,24,7168]{3,2,1,0:T(8,128)} %get-tuple-element.38.in_ref, f32[2,4,4,32,768]{4,3,2,1,0:T(8,128)} %get-tuple-element.39.out_ref, ...), custom_call_target="tpu_custom_call" | custom-call | tf_op jit(solution)/shard_map/finish/pallas_call | solution.py:1143
